TPU v7x, 32 devices: a whole 2x2x4 slice. The times are simulated.
32 devices in a mesh: ctx: 16 (over z, y, core), wsh: 2 (over x).
Axes of the slice: x: 2, y: 2, z: 4, core: 2. Of those that a mesh axis runs over, the one named last changes fastest.
Arguments:
- tokens: bfloat16 [4, 2048, 1152], P('wsh', 'ctx'), may hold values from -6 to 6
- block_order: int32 [16], replicated, may hold values from 0 to 15, each once
- gain_attn_pre: bfloat16 [1152], P('wsh'), may hold values from 0.25 to 1.75
- gain_query: bfloat16 [256], P('wsh'), may hold values from 0.25 to 1.75
- gain_key: bfloat16 [256], P('wsh'), may hold values from 0.25 to 1.75
- gain_attn_post: bfloat16 [1152], P('wsh'), may hold values from 0.25 to 1.75
- gain_ff_pre: bfloat16 [1152], P('wsh'), may hold values from 0.25 to 1.75
- gain_ff_post: bfloat16 [1152], P('wsh'), may hold values from 0.25 to 1.75
- weight_query: bfloat16 [1152, 1024], P(None, 'wsh'), may hold values from -0.1875 to 0.1875
- weight_key: bfloat16 [1152, 256], P(None, 'wsh'), may hold values from -0.1875 to 0.1875
- weight_value: bfloat16 [1152, 256], P(None, 'wsh'), may hold values from -0.1875 to 0.1875
- weight_out: bfloat16 [1024, 1152], P(None, 'wsh'), may hold values from -0.1875 to 0.1875
- weight_gate: bfloat16 [1152, 6912], P(None, 'wsh'), may hold values from -0.1875 to 0.1875
- weight_up: bfloat16 [1152, 6912], P(None, 'wsh'), may hold values from -0.1875 to 0.1875
- weight_down: bfloat16 [1152, 6912], P(None, 'wsh'), may hold values from -0.078125 to 0.078125
- cotangent: bfloat16 [4, 2048, 1152], P('wsh', 'ctx'), may hold values from -6 to 6
Outputs:
- output: bfloat16 [4, 2048, 1152], P('wsh', 'ctx')
- grad_tokens: float32 [4, 2048, 1152], P('wsh', 'ctx')
- grad_gain_attn_pre: float32 [1152], P(('ctx', 'wsh'))
- grad_gain_query: float32 [256], P(('ctx', 'wsh'))
- grad_gain_key: float32 [256], P(('ctx', 'wsh'))
- grad_gain_attn_post: float32 [1152], P(('ctx', 'wsh'))
- grad_gain_ff_pre: float32 [1152], P(('ctx', 'wsh'))
- grad_gain_ff_post: float32 [1152], P(('ctx', 'wsh'))
- grad_weight_query: float32 [1152, 1024], P('ctx', 'wsh')
- grad_weight_key: float32 [1152, 256], P('ctx', 'wsh')
- grad_weight_value: float32 [1152, 256], P('ctx', 'wsh')
- grad_weight_out: float32 [1024, 1152], P('ctx', 'wsh')
- grad_weight_gate: float32 [1152, 6912], P('ctx', 'wsh')
- grad_weight_up: float32 [1152, 6912], P('ctx', 'wsh')
- grad_weight_down: float32 [1152, 6912], P('ctx', 'wsh')
Inputs may be any that keep to these rules, and one draw needn't show every extreme that they name: block_order is a permutation of 0 to 15.
All inputs are finite; a program needn't handle non-finite values.
Results may differ from a plain program's by a relative error of at most 0.025.
Values may be sent and summed in bfloat16 or wider, within the bound.
A program may use at most 384 MiB of HBM per device.

v0:
```python
import math

import jax
import jax.numpy as jnp
from jax import lax
from jax.sharding import PartitionSpec as P

EPS = 1e-06
ROPE_BASE = 1000000.0
SCORE_SCALE = 0.0625


def norm_gain(vector, gain):
    return vector * lax.rsqrt(jnp.mean(vector * vector, -1, keepdims=True) + EPS) * gain


def rotate(vector, cosine, sine):
    middle = vector.shape[-1] // 2
    first = vector[..., :middle]
    second = vector[..., middle:]
    return jnp.concatenate([first * cosine - second * sine, second * cosine + first * sine], -1)


def angle_tables(positions, head_size):
    middle = head_size // 2
    inverse = jnp.exp(
        jnp.arange(middle, dtype=jnp.float32) * (-2.0 * math.log(ROPE_BASE) / head_size)
    )
    theta = positions.astype(jnp.float32)[:, None] * inverse[None, :]
    return (jnp.cos(theta), jnp.sin(theta))


def block_positions(pairs, first, count, block):
    chosen = lax.dynamic_slice_in_dim(pairs, first, count)
    return (chosen[:, None] * block + jnp.arange(block, dtype=jnp.int32)[None, :]).reshape(-1)


def group_size():
    return 8


def attend_forward(queries, keys, values, allowed):
    weights = jnp.exp(
        jnp.einsum("sgrhd,sgkd->sghrk", queries, keys, preferred_element_type=jnp.float32)
        * SCORE_SCALE
    )
    if allowed is not None:
        weights = jnp.where(allowed, weights, 0.0)
    weights_low = weights.astype(jnp.bfloat16)
    summed = jnp.einsum(
        "sghrk,sgkd->sghrd", weights_low, values, preferred_element_type=jnp.float32
    )
    return (summed, jnp.sum(weights_low.astype(jnp.float32), -1))


def attend_backward(queries, keys, values, scaled, correction, allowed):
    weights = jnp.exp(
        jnp.einsum("sgrhd,sgkd->sghrk", queries, keys, preferred_element_type=jnp.float32)
        * SCORE_SCALE
    )
    if allowed is not None:
        weights = jnp.where(allowed, weights, 0.0)
    weights_low = weights.astype(jnp.bfloat16)
    grad_weights = jnp.einsum(
        "sghrd,sgkd->sghrk", scaled, values, preferred_element_type=jnp.float32
    )
    grad_scores = (weights * (grad_weights - correction[..., None])).astype(jnp.bfloat16)
    grad_query = SCORE_SCALE * jnp.einsum(
        "sghrk,sgkd->sgrhd", grad_scores, keys, preferred_element_type=jnp.float32
    )
    grad_keys = SCORE_SCALE * jnp.einsum(
        "sghrk,sgrhd->sgkd", grad_scores, queries, preferred_element_type=jnp.float32
    )
    grad_values = jnp.einsum(
        "sghrk,sghrd->sgkd", weights_low, scaled, preferred_element_type=jnp.float32
    )
    return (grad_query, grad_keys, grad_values)


def gate_up(gate, upward):
    return jax.nn.gelu(gate, approximate=True) * upward


def body(
    tokens,
    block_order,
    gain_attn_pre,
    gain_query,
    gain_key,
    gain_attn_post,
    gain_ff_pre,
    gain_ff_post,
    weight_query,
    weight_key,
    weight_value,
    weight_out,
    weight_gate,
    weight_up,
    weight_down,
    cotangent,
):
    sequences, rows, width = tokens.shape
    block = rows // 2
    span_devices = lax.axis_size("ctx")
    my_index = lax.axis_index("ctx")
    pairs = jnp.stack([block_order, 2 * span_devices - 1 - block_order], 1).reshape(-1)
    own_pos = block_positions(pairs, 2 * my_index, 2, block)
    first_block = lax.dynamic_slice_in_dim(block_order, my_index, 1)[0]
    (
        gain_attn_pre,
        gain_query,
        gain_key,
        gain_attn_post,
        gain_ff_pre,
        gain_ff_post,
        weight_query,
        weight_key,
        weight_value,
        weight_out,
    ) = (
        lax.all_gather(gain_attn_pre, "wsh", axis=0, tiled=True),
        lax.all_gather(gain_query, "wsh", axis=0, tiled=True),
        lax.all_gather(gain_key, "wsh", axis=0, tiled=True),
        lax.all_gather(gain_attn_post, "wsh", axis=0, tiled=True),
        lax.all_gather(gain_ff_pre, "wsh", axis=0, tiled=True),
        lax.all_gather(gain_ff_post, "wsh", axis=0, tiled=True),
        lax.all_gather(weight_query, "wsh", axis=1, tiled=True),
        lax.all_gather(weight_key, "wsh", axis=1, tiled=True),
        lax.all_gather(weight_value, "wsh", axis=1, tiled=True),
        lax.all_gather(weight_out, "wsh", axis=1, tiled=True),
    )
    attn_pre = gain_attn_pre.astype(jnp.float32)
    query_gain = gain_query.astype(jnp.float32)
    key_gain = gain_key.astype(jnp.float32)
    attn_post = gain_attn_post.astype(jnp.float32)
    ff_pre = gain_ff_pre.astype(jnp.float32)
    ff_post = gain_ff_post.astype(jnp.float32)
    head_size = query_gain.shape[0]
    heads = weight_query.shape[1] // head_size
    inputs = tokens.astype(jnp.float32)
    normed, pre_back = jax.vjp(norm_gain, inputs, attn_pre)
    normed_low = normed.astype(jnp.bfloat16)
    query_raw = jnp.einsum(
        "srd,de->sre", normed_low, weight_query, preferred_element_type=jnp.float32
    ).reshape(sequences, rows, heads, head_size)
    pair_weight = jnp.concatenate([weight_key, weight_value], 1)
    key_value = jnp.einsum(
        "srd,de->sre", normed_low, pair_weight, preferred_element_type=jnp.float32
    )
    key_raw = key_value[..., :head_size]
    value_low = key_value[..., head_size:].astype(jnp.bfloat16)
    cosine, sine = angle_tables(own_pos, head_size)

    def query_key(query_in, key_in, query_scale, key_scale):
        return (
            rotate(
                norm_gain(query_in, query_scale), cosine[None, :, None, :], sine[None, :, None, :]
            ),
            rotate(norm_gain(key_in, key_scale), cosine[None], sine[None]),
        )

    (query_rot, key_rot), rope_back = jax.vjp(query_key, query_raw, key_raw, query_gain, key_gain)
    query_low = query_rot.astype(jnp.bfloat16)
    key_low = key_rot.astype(jnp.bfloat16)
    local_pair = jnp.concatenate([key_low, value_low], -1).reshape(
        sequences, 2, block, 2 * head_size
    )
    query_early = query_low[:, None, :block]
    query_late = query_low[:, None, block:]
    early_mask = own_pos[:block, None] >= own_pos[None, :block]
    late_mask = own_pos[block:, None] >= own_pos[None, block:]
    own_early = attend_forward(
        query_early, key_low[:, None, :block], value_low[:, None, :block], early_mask
    )
    own_late = attend_forward(
        query_late, key_low[:, None, block:], value_low[:, None, block:], late_mask
    )
    initial = (own_early[0][:, 0], own_early[1][:, 0], own_late[0][:, 0], own_late[1][:, 0])
    piece = lax.all_gather(local_pair, "ctx", axis=1, tiled=True)
    shard_count = piece.shape[1] // 2
    fold_group = group_size()
    shards = piece.reshape(sequences, shard_count, 2, block, 2 * head_size)

    def inner(index, state):
        early_sum, early_tot, late_sum, late_tot = state
        portion = lax.dynamic_slice_in_dim(shards, index * fold_group, fold_group, 1)
        orders = lax.dynamic_slice_in_dim(block_order, index * fold_group, fold_group)
        take_early = orders < first_block
        early_keys = portion[:, :, 0]
        late_keys = portion[:, :, 1]
        flat = early_keys.reshape(sequences, 1, fold_group * block, 2 * head_size)
        dense_sum, dense_tot = attend_forward(
            query_late, flat[..., :head_size], flat[..., head_size:], None
        )
        late_sum = late_sum + dense_sum[:, 0]
        late_tot = late_tot + dense_tot[:, 0]
        chosen_query = jnp.where(take_early[None, :, None, None, None], query_early, query_late)
        chosen_keys = jnp.where(take_early[None, :, None, None], early_keys, late_keys)
        part_sum, part_tot = attend_forward(
            chosen_query, chosen_keys[..., :head_size], chosen_keys[..., head_size:], None
        )
        early_flag = take_early.astype(jnp.float32)
        late_flag = (orders > first_block).astype(jnp.float32)
        early_sum = early_sum + jnp.sum(part_sum * early_flag[None, :, None, None, None], 1)
        early_tot = early_tot + jnp.sum(part_tot * early_flag[None, :, None, None], 1)
        late_sum = late_sum + jnp.sum(part_sum * late_flag[None, :, None, None, None], 1)
        late_tot = late_tot + jnp.sum(part_tot * late_flag[None, :, None, None], 1)
        return (early_sum, early_tot, late_sum, late_tot)

    early_sum, early_tot, late_sum, late_tot = lax.fori_loop(
        0, shard_count // fold_group, inner, initial
    )
    summed = jnp.concatenate([early_sum, late_sum], 2)
    totals = jnp.concatenate([early_tot, late_tot], 2)
    mixed = summed / totals[..., None]
    mixed_low = mixed.astype(jnp.bfloat16)
    out_weight = weight_out.reshape(heads, head_size, width)
    attended = jnp.einsum(
        "shrd,hde->sre", mixed_low, out_weight, preferred_element_type=jnp.float32
    )
    post_attn, post_attn_back = jax.vjp(norm_gain, attended, attn_post)
    hidden_state = inputs + post_attn
    ff_input, ff_pre_back = jax.vjp(norm_gain, hidden_state, ff_pre)
    ff_low = ff_input.astype(jnp.bfloat16)
    gate_matrix, up_matrix, down_matrix = (
        lax.all_gather(weight_gate, "wsh", axis=1, tiled=True),
        lax.all_gather(weight_up, "wsh", axis=1, tiled=True),
        lax.all_gather(weight_down, "wsh", axis=1, tiled=True),
    )
    gate = jnp.einsum("srd,df->srf", ff_low, gate_matrix, preferred_element_type=jnp.float32)
    upward = jnp.einsum("srd,df->srf", ff_low, up_matrix, preferred_element_type=jnp.float32)
    activated, gelu_back = jax.vjp(gate_up, gate, upward)
    activated_low = activated.astype(jnp.bfloat16)
    lowered = jnp.einsum(
        "srf,ef->sre", activated_low, down_matrix, preferred_element_type=jnp.float32
    )
    post_ff, post_ff_back = jax.vjp(norm_gain, lowered, ff_post)
    output = (hidden_state + post_ff).astype(jnp.bfloat16)
    grad_output = cotangent.astype(jnp.float32)
    grad_lowered, grad_ff_post = post_ff_back(grad_output)
    lowered_grad_low = grad_lowered.astype(jnp.bfloat16)
    grad_activated = jnp.einsum(
        "sre,ef->srf", lowered_grad_low, down_matrix, preferred_element_type=jnp.float32
    )
    grad_down_w = jnp.einsum(
        "sre,srf->ef", lowered_grad_low, activated_low, preferred_element_type=jnp.float32
    )
    grad_gate, grad_up = gelu_back(grad_activated)
    gate_grad_low = grad_gate.astype(jnp.bfloat16)
    up_grad_low = grad_up.astype(jnp.bfloat16)
    grad_gate_w = jnp.einsum(
        "srd,srf->df", ff_low, gate_grad_low, preferred_element_type=jnp.float32
    )
    grad_up_w = jnp.einsum("srd,srf->df", ff_low, up_grad_low, preferred_element_type=jnp.float32)
    grad_ff_input = jnp.einsum(
        "srf,df->srd", gate_grad_low, gate_matrix, preferred_element_type=jnp.float32
    ) + jnp.einsum("srf,df->srd", up_grad_low, up_matrix, preferred_element_type=jnp.float32)
    grad_gate_w, grad_up_w, grad_down_w = (
        lax.psum_scatter(
            grad_gate_w.astype(jnp.bfloat16), "wsh", scatter_dimension=1, tiled=True
        ).astype(jnp.float32),
        lax.psum_scatter(
            grad_up_w.astype(jnp.bfloat16), "wsh", scatter_dimension=1, tiled=True
        ).astype(jnp.float32),
        lax.psum_scatter(
            grad_down_w.astype(jnp.bfloat16), "wsh", scatter_dimension=1, tiled=True
        ).astype(jnp.float32),
    )
    grad_gate_w, grad_up_w, grad_down_w = (
        lax.psum_scatter(grad_gate_w, "ctx", scatter_dimension=0, tiled=True),
        lax.psum_scatter(grad_up_w, "ctx", scatter_dimension=0, tiled=True),
        lax.psum_scatter(grad_down_w, "ctx", scatter_dimension=0, tiled=True),
    )
    grad_hidden, grad_ff_pre = ff_pre_back(grad_ff_input)
    grad_hidden = grad_hidden + grad_output
    grad_attended, grad_attn_post = post_attn_back(grad_hidden)
    attended_grad_low = grad_attended.astype(jnp.bfloat16)
    grad_out_w = jnp.einsum(
        "shrd,sre->hde", mixed_low, attended_grad_low, preferred_element_type=jnp.float32
    ).reshape(heads * head_size, width)
    grad_mixed_low = jnp.einsum(
        "sre,hde->shrd", attended_grad_low, out_weight, preferred_element_type=jnp.float32
    ).astype(jnp.bfloat16)
    grad_mixed_wide = grad_mixed_low.astype(jnp.float32)
    delta = jnp.sum(grad_mixed_wide * mixed, -1)
    scaled_low = (grad_mixed_wide / totals[..., None]).astype(jnp.bfloat16)
    correction = delta / totals
    scaled_early = scaled_low[:, None, :, :block]
    scaled_late = scaled_low[:, None, :, block:]
    correction_early = correction[:, None, :, :block]
    correction_late = correction[:, None, :, block:]
    gathered = lax.all_gather(local_pair, "ctx", axis=1, tiled=True)
    shard_total = gathered.shape[1] // 2
    group = group_size()
    all_shards = gathered.reshape(sequences, shard_total, 2, block, 2 * head_size)

    def back_step(carry, index):
        query_grad_early, query_grad_late = carry
        portion = lax.dynamic_slice_in_dim(all_shards, index * group, group, 1)
        orders = lax.dynamic_slice_in_dim(block_order, index * group, group)
        take_early = orders < first_block
        early_keys = portion[:, :, 0]
        late_keys = portion[:, :, 1]
        flat = early_keys.reshape(sequences, 1, group * block, 2 * head_size)
        dense_query, dense_keys, dense_values = attend_backward(
            query_late,
            flat[..., :head_size],
            flat[..., head_size:],
            scaled_late,
            correction_late,
            None,
        )
        query_grad_late = query_grad_late + dense_query[:, 0]
        dense_keys = dense_keys.reshape(sequences, group, block, head_size)
        dense_values = dense_values.reshape(sequences, group, block, head_size)
        chosen_query = jnp.where(take_early[None, :, None, None, None], query_early, query_late)
        chosen_keys = jnp.where(take_early[None, :, None, None], early_keys, late_keys)
        chosen_scaled = jnp.where(take_early[None, :, None, None, None], scaled_early, scaled_late)
        chosen_correction = jnp.where(
            take_early[None, :, None, None], correction_early, correction_late
        )
        part_query, part_keys, part_values = attend_backward(
            chosen_query,
            chosen_keys[..., :head_size],
            chosen_keys[..., head_size:],
            chosen_scaled,
            chosen_correction,
            None,
        )
        early_flag = take_early.astype(jnp.float32)
        late_flag = (orders > first_block).astype(jnp.float32)
        query_grad_early = query_grad_early + jnp.sum(
            part_query * early_flag[None, :, None, None, None], 1
        )
        query_grad_late = query_grad_late + jnp.sum(
            part_query * late_flag[None, :, None, None, None], 1
        )
        early_slot = jnp.concatenate(
            [
                dense_keys + part_keys * early_flag[None, :, None, None],
                dense_values + part_values * early_flag[None, :, None, None],
            ],
            -1,
        )
        late_slot = jnp.concatenate(
            [
                part_keys * late_flag[None, :, None, None],
                part_values * late_flag[None, :, None, None],
            ],
            -1,
        )
        both = jnp.transpose(jnp.stack([early_slot, late_slot], 2), (1, 2, 0, 3, 4))
        return ((query_grad_early, query_grad_late), both)

    diag_early = attend_backward(
        query_early,
        key_low[:, None, :block],
        value_low[:, None, :block],
        scaled_early,
        correction_early,
        early_mask,
    )
    diag_late = attend_backward(
        query_late,
        key_low[:, None, block:],
        value_low[:, None, block:],
        scaled_late,
        correction_late,
        late_mask,
    )
    (query_grad_early, query_grad_late), grad_pairs = lax.scan(
        back_step,
        (diag_early[0][:, 0], diag_late[0][:, 0]),
        jnp.arange(shard_total // group, dtype=jnp.int32),
    )
    grad_pairs = grad_pairs.reshape(2 * shard_total, sequences, block, 2 * head_size)
    own_block = jnp.stack(
        [
            jnp.concatenate([diag_early[1], diag_early[2]], -1)[:, 0],
            jnp.concatenate([diag_late[1], diag_late[2]], -1)[:, 0],
        ],
        0,
    )
    own_slots = lax.dynamic_slice_in_dim(grad_pairs, 2 * my_index, 2, 0) + own_block
    grad_pairs = lax.dynamic_update_slice_in_dim(grad_pairs, own_slots, 2 * my_index, 0)
    grad_query = jnp.concatenate([query_grad_early, query_grad_late], 1)
    own_grads = lax.psum_scatter(grad_pairs, "ctx", scatter_dimension=0, tiled=True)
    own_grads = jnp.transpose(own_grads, (1, 0, 2, 3)).reshape(sequences, rows, 2 * head_size)
    grad_key_rot = own_grads[..., :head_size]
    value_grad_low = own_grads[..., head_size:].astype(jnp.bfloat16)
    grad_query_raw, grad_key_raw, grad_query_gain, grad_key_gain = rope_back(
        (grad_query, grad_key_rot)
    )
    query_grad_low = grad_query_raw.reshape(sequences, rows, heads * head_size).astype(jnp.bfloat16)
    pair_grad_low = jnp.concatenate([grad_key_raw.astype(jnp.bfloat16), value_grad_low], -1)
    grad_query_w = jnp.einsum(
        "srd,sre->de", normed_low, query_grad_low, preferred_element_type=jnp.float32
    )
    grad_pair_w = jnp.einsum(
        "srd,sre->de", normed_low, pair_grad_low, preferred_element_type=jnp.float32
    )
    grad_normed = jnp.einsum(
        "sre,de->srd", query_grad_low, weight_query, preferred_element_type=jnp.float32
    ) + jnp.einsum("sre,de->srd", pair_grad_low, pair_weight, preferred_element_type=jnp.float32)
    grad_inputs, grad_attn_pre = pre_back(grad_normed)
    grad_tokens = grad_inputs + grad_hidden
    reduced = (
        lax.psum_scatter(grad_query_w, "ctx", scatter_dimension=0, tiled=True),
        lax.psum_scatter(grad_pair_w[:, :head_size], "ctx", scatter_dimension=0, tiled=True),
        lax.psum_scatter(grad_pair_w[:, head_size:], "ctx", scatter_dimension=0, tiled=True),
        lax.psum_scatter(grad_out_w, "ctx", scatter_dimension=0, tiled=True),
        lax.psum_scatter(grad_attn_pre, "ctx", scatter_dimension=0, tiled=True),
        lax.psum_scatter(grad_query_gain, "ctx", scatter_dimension=0, tiled=True),
        lax.psum_scatter(grad_key_gain, "ctx", scatter_dimension=0, tiled=True),
        lax.psum_scatter(grad_attn_post, "ctx", scatter_dimension=0, tiled=True),
        lax.psum_scatter(grad_ff_pre, "ctx", scatter_dimension=0, tiled=True),
        lax.psum_scatter(grad_ff_post, "ctx", scatter_dimension=0, tiled=True),
    )
    (
        grad_query_w,
        grad_key_w,
        grad_value_w,
        grad_out_w,
        grad_attn_pre,
        grad_query_gain,
        grad_key_gain,
        grad_attn_post,
        grad_ff_pre,
        grad_ff_post,
    ) = (
        lax.psum_scatter(
            reduced[0].astype(jnp.bfloat16), "wsh", scatter_dimension=1, tiled=True
        ).astype(jnp.float32),
        lax.psum_scatter(
            reduced[1].astype(jnp.bfloat16), "wsh", scatter_dimension=1, tiled=True
        ).astype(jnp.float32),
        lax.psum_scatter(
            reduced[2].astype(jnp.bfloat16), "wsh", scatter_dimension=1, tiled=True
        ).astype(jnp.float32),
        lax.psum_scatter(
            reduced[3].astype(jnp.bfloat16), "wsh", scatter_dimension=1, tiled=True
        ).astype(jnp.float32),
        lax.psum_scatter(
            reduced[4].astype(jnp.bfloat16), "wsh", scatter_dimension=0, tiled=True
        ).astype(jnp.float32),
        lax.psum_scatter(
            reduced[5].astype(jnp.bfloat16), "wsh", scatter_dimension=0, tiled=True
        ).astype(jnp.float32),
        lax.psum_scatter(
            reduced[6].astype(jnp.bfloat16), "wsh", scatter_dimension=0, tiled=True
        ).astype(jnp.float32),
        lax.psum_scatter(
            reduced[7].astype(jnp.bfloat16), "wsh", scatter_dimension=0, tiled=True
        ).astype(jnp.float32),
        lax.psum_scatter(
            reduced[8].astype(jnp.bfloat16), "wsh", scatter_dimension=0, tiled=True
        ).astype(jnp.float32),
        lax.psum_scatter(
            reduced[9].astype(jnp.bfloat16), "wsh", scatter_dimension=0, tiled=True
        ).astype(jnp.float32),
    )
    return (
        output,
        grad_tokens,
        grad_attn_pre,
        grad_query_gain,
        grad_key_gain,
        grad_attn_post,
        grad_ff_pre,
        grad_ff_post,
        grad_query_w,
        grad_key_w,
        grad_value_w,
        grad_out_w,
        grad_gate_w,
        grad_up_w,
        grad_down_w,
    )


def solution(mesh):
    in_specs = (
        P("wsh", "ctx", None),
        P(),
        P("wsh"),
        P("wsh"),
        P("wsh"),
        P("wsh"),
        P("wsh"),
        P("wsh"),
        P(None, "wsh"),
        P(None, "wsh"),
        P(None, "wsh"),
        P(None, "wsh"),
        P(None, "wsh"),
        P(None, "wsh"),
        P(None, "wsh"),
        P("wsh", "ctx", None),
    )
    out_specs = (
        P("wsh", "ctx", None),
        P("wsh", "ctx", None),
        P(("ctx", "wsh")),
        P(("ctx", "wsh")),
        P(("ctx", "wsh")),
        P(("ctx", "wsh")),
        P(("ctx", "wsh")),
        P(("ctx", "wsh")),
        P("ctx", "wsh"),
        P("ctx", "wsh"),
        P("ctx", "wsh"),
        P("ctx", "wsh"),
        P("ctx", "wsh"),
        P("ctx", "wsh"),
        P("ctx", "wsh"),
    )
    return jax.shard_map(body, mesh=mesh, in_specs=in_specs, out_specs=out_specs, check_vma=False)
```

profile of v0, /device:TPU:0, one launch (start us, length us, event | category | flops | bytes accessed | tf_op | source)
XLA Modules:
  0.0 2353.7 jit_solution(4288942187021070026)
XLA Ops:
  25.4 15.7 all_gather.45
  41.1 15.2 all_gather.44
  71.2 27.5 %all-gather.13.cloned.1.call-done = bf16[1024,1152]{0,1:T(8,128)(2,1)} async-done(((bf16[1024,576]{0,1:T(8,128)(2,1)}), bf16[1024,1152]{0,1:T(8,128)(2,1)}) %all-gather.13.cloned.1.call-update) | async-done | bytes 2359312 | tf_op jit(solution)/shard_map/all_gather | solution.py:130
  105.1 46.8 %all-gather.11.cloned.1.call-done = bf16[2,32,64,512]{3,2,1,0:T(8,128)(2,1)} async-done(((bf16[2,2,64,512]{3,2,1,0:T(8,128)(2,1)}), bf16[2,32,64,512]{3,2,1,0:T(8,128)(2,1)}) %all-gather.11.cloned.1.call-update) | async-done | bytes 4194320 | tf_op jit(solution)/shard_map/all_gather | solution.py:179
  156.6 15.6 while.33
  177.4 163.7 %all-gather.15.cloned.1.call-done = bf16[1152,6912]{1,0:T(8,128)(2,1)} async-done(((bf16[1152,3456]{1,0:T(8,128)(2,1)}), bf16[1152,6912]{1,0:T(8,128)(2,1)}) %all-gather.15.cloned.1.call-update) | async-done | bytes 15925264 | tf_op jit(solution)/shard_map/all_gather | solution.py:226
  341.1 13.0 fusion.77
  354.1 177.7 %all-gather.17.cloned.1.call-done = bf16[1152,6912]{1,0:T(8,128)(2,1)} async-done(((bf16[1152,3456]{1,0:T(8,128)(2,1)}), bf16[1152,6912]{1,0:T(8,128)(2,1)}) %all-gather.17.cloned.1.call-update) | async-done | bytes 15925264 | tf_op jit(solution)/shard_map/all_gather | solution.py:227
  531.8 16.4 multiply_convert_fusion.1
  548.2 174.3 %all-gather.19.cloned.1.call-done = bf16[1152,6912]{1,0:T(8,128)(2,1)} async-done(((bf16[1152,3456]{1,0:T(8,128)(2,1)}), bf16[1152,6912]{1,0:T(8,128)(2,1)}) %all-gather.19.cloned.1.call-update) | async-done | bytes 15925264 | tf_op jit(solution)/shard_map/all_gather | solution.py:228
  722.5 12.4 multiply_reduce_fusion.10
  739.9 18.8 fusion.85
  758.7 12.4 fusion.71
  771.0 13.6 multiply_reduce_fusion.6
  795.9 43.5 %while.34 = (s32[]{:T(128)}, f32[2,64,4,256]{3,1,2,0:T(8,128)S(1)}, f32[2,64,4,256]{3,1,2,0:T(8,128)S(1)}, f32[2,8,2,2,64,512]{5,4,3,2,1,0:T(8,128)}, s32[2]{0:T...) while((s32[]{:T(128)}, f32[2,64,4,256]{3,1,2,0:T(8,128)S(1)}, ...), condition=%wide.region_23.24_spmd, body=%wide.region_20.23_spmd.sunk | while | flops 1358172160 | bytes 111734232 | solution.py:371
  852.7 93.2 %reduce-scatter.34.cloned.1.call-done = f32[2,2,64,512]{3,2,1,0:T(8,128)} async-done(((f32[32,2,64,512]{3,2,1,0:T(8,128)}), f32[2,2,64,512]{3,2,1,0:T(8,128)}) %reduce-scatter.34.cloned.1.call-update) | async-done | bytes 524304 | tf_op jit(solution)/shard_map/reduce_scatter | solution.py:387
  960.8 21.7 copy.283
  992.5 21.7 copy.285
  1025.2 22.0 copy.287
  1049.3 54.3 %reduce-scatter.36.cloned.1.call-done = f32[72,1024]{1,0:T(8,128)} async-done(((f32[1152,1024]{1,0:T(8,128)}), f32[72,1024]{1,0:T(8,128)}) %reduce-scatter.36.cloned.1.call-update) | async-done | bytes 294928 | tf_op jit(solution)/shard_map/reduce_scatter | solution.py:408
  1105.4 59.1 %reduce-scatter.40.cloned.1.call-done = f32[72,256]{1,0:T(8,128)} async-done(((f32[1152,256]{1,0:T(8,128)}), f32[72,256]{1,0:T(8,128)}) %reduce-scatter.40.cloned.1.call-update) | async-done | bytes 73744 | tf_op jit(solution)/shard_map/reduce_scatter | solution.py:409
  1166.2 59.3 %reduce-scatter.42.cloned.1.call-done = f32[72,256]{1,0:T(8,128)} async-done(((f32[1152,256]{1,0:T(8,128)}), f32[72,256]{1,0:T(8,128)}) %reduce-scatter.42.cloned.1.call-update) | async-done | bytes 73744 | tf_op jit(solution)/shard_map/reduce_scatter | solution.py:410
  1227.1 179.5 %reduce-scatter.52.cloned.1.call-done = bf16[3456,1152]{1,0:T(8,128)(2,1)} async-done(((bf16[6912,1152]{1,0:T(8,128)(2,1)}), bf16[3456,1152]{1,0:T(8,128)(2,1)}) %reduce-scatter.52.cloned.1.call-update) | async-done | bytes 7962640
  1406.6 11.8 copy.284
  1428.3 160.7 %reduce-scatter.54.cloned.1.call-done = bf16[3456,1152]{1,0:T(8,128)(2,1)} async-done(((bf16[6912,1152]{1,0:T(8,128)(2,1)}), bf16[3456,1152]{1,0:T(8,128)(2,1)}) %reduce-scatter.54.cloned.1.call-update) | async-done | bytes 7962640
  1589.0 11.8 copy.286
  1610.8 160.5 %reduce-scatter.56.cloned.1.call-done = bf16[3456,1152]{1,0:T(8,128)(2,1)} async-done(((bf16[6912,1152]{1,0:T(8,128)(2,1)}), bf16[3456,1152]{1,0:T(8,128)(2,1)}) %reduce-scatter.56.cloned.1.call-update) | async-done | bytes 7962640
  1771.3 11.8 copy.288
  1803.8 61.0 %all-reduce.23 = (bf16[1152]{0:T(1024)(128)(2,1)S(1)}, bf16[256]{0:T(256)(128)(2,1)S(1)}, bf16[256]{0:T(256)(128)(2,1)S(1)}, bf16[1152]{0:T(1024)(128)(2,1)S(1)}...) all-reduce(f32[1152]{0:T(1024)S(1)} %get-tuple-element.452, ...), channel_id=3, replica_groups=mesh['ctx'=16,'wsh'=2] {'ctx'}, use_global_device_ids=true, to_apply=%region_29.30.clone | all-reduce | flops 5120 | bytes 30720
  1878.0 120.1 %reduce-scatter.58.cloned.1.call-done = f32[72,3456]{1,0:T(8,128)} async-done(((f32[1152,3456]{1,0:T(8,128)}), f32[72,3456]{1,0:T(8,128)}) %reduce-scatter.58.cloned.1.call-update) | async-done | bytes 995344
  1998.1 174.1 %reduce-scatter.60.cloned.1.call-done = f32[72,3456]{1,0:T(8,128)} async-done(((f32[1152,3456]{1,0:T(8,128)}), f32[72,3456]{1,0:T(8,128)}) %reduce-scatter.60.cloned.1.call-update) | async-done | bytes 995344
  2172.3 174.3 %reduce-scatter.62.cloned.1.call-done = f32[72,3456]{1,0:T(8,128)} async-done(((f32[1152,3456]{1,0:T(8,128)}), f32[72,3456]{1,0:T(8,128)}) %reduce-scatter.62.cloned.1.call-update) | async-done | bytes 995344
  (445 shorter events, 228.1 us)
Async XLA Ops:
  7.3 49.1 %copy-start = (bf16[2,128,1152]{2,1,0:T(8,128)(2,1)S(1)}, bf16[2,128,1152]{2,1,0:T(8,128)(2,1)}, u32[]{:S(2)}) copy-start(bf16[2,128,1152]{2,1,0:T(8,128)(2,1)} %param.20) | copy-start | bytes 1769476
  7.3 60.2 %all-gather.9.cloned.1.call-start = ((), (), s32[]{:S(2)}) async-start(), calls=%async_computation.15 | async-start | bytes 3538944 | tf_op jit(solution)/shard_map/all_gather | solution.py:127
  8.0 90.7 %all-gather.13.cloned.1.call-start = ((), (), s32[]{:S(2)}) async-start(), calls=%async_computation.17 | async-start | bytes 3538944 | tf_op jit(solution)/shard_map/all_gather | solution.py:130
  8.8 143.1 %all-gather.11.cloned.1.call-start = ((), (), s32[]{:S(2)}) async-start(), calls=%async_computation.16 | async-start | bytes 4456448 | tf_op jit(solution)/shard_map/all_gather | solution.py:179
  58.9 282.2 %all-gather.15.cloned.1.call-start = ((), (), s32[]{:S(2)}) async-start(), calls=%async_computation.18 | async-start | bytes 23887872 | tf_op jit(solution)/shard_map/all_gather | solution.py:226
  59.5 472.3 %all-gather.17.cloned.1.call-start = ((), (), s32[]{:S(2)}) async-start(), calls=%async_computation.19 | async-start | bytes 23887872 | tf_op jit(solution)/shard_map/all_gather | solution.py:227
  60.1 662.4 %all-gather.19.cloned.1.call-start = ((), (), s32[]{:S(2)}) async-start(), calls=%async_computation.20 | async-start | bytes 23887872 | tf_op jit(solution)/shard_map/all_gather | solution.py:228
  60.6 885.3 %reduce-scatter.34.cloned.1.call-start = ((), (), s32[]{:S(2)}) async-start(), calls=%async_computation.21 | async-start | bytes 8912896 | tf_op jit(solution)/shard_map/reduce_scatter | solution.py:387
  104.2 52.3 %copy-start.21 = (f32[2,1,4,64,64]{3,4,2,0,1:T(8,128)}, f32[2,1,4,64,64]{3,4,2,0,1:T(8,128)S(1)}, u32[]{:S(2)}) copy-start(f32[2,1,4,64,64]{3,4,2,0,1:T(8,128)S(1)} %get-tuple-element.576) | copy-start | bytes 393220
  104.5 52.0 %copy-start.14 = (f32[2,1,4,64,64]{3,4,2,0,1:T(8,128)}, f32[2,1,4,64,64]{3,4,2,0,1:T(8,128)S(1)}, u32[]{:S(2)}) copy-start(f32[2,1,4,64,64]{3,4,2,0,1:T(8,128)S(1)} %get-tuple-element.578) | copy-start | bytes 393220
  172.3 619.8 %copy-start.54 = (f32[2,4,128]{2,1,0:T(4,128)}, f32[2,4,128]{2,1,0:T(4,128)S(1)}, u32[]{:S(2)}) copy-start(f32[2,4,128]{2,1,0:T(4,128)S(1)} %pad_maximum_fusion.6) | copy-start | bytes 12292
  177.4 354.4 %copy-start.11 = (bf16[2,128,1152]{2,1,0:T(8,128)(2,1)}, bf16[2,128,1152]{2,1,0:T(8,128)(2,1)S(1)}, u32[]{:S(2)}) copy-start(bf16[2,128,1152]{2,1,0:T(8,128)(2,1)S(1)} %multiply_convert_fusion.2) | copy-start | bytes 1769476
  842.3 205.0 %reduce-scatter.44.cloned.1.call-start = ((), (), s32[]{:S(2)}) async-start(), calls=%async_computation.26 | async-start | bytes 5013504 | tf_op jit(solution)/shard_map/reduce_scatter | solution.py:411
  846.6 257.0 %reduce-scatter.36.cloned.1.call-start = ((), (), s32[]{:S(2)}) async-start(), calls=%async_computation.22 | async-start | bytes 5013504 | tf_op jit(solution)/shard_map/reduce_scatter | solution.py:408
  852.7 94.4 %copy-start.64 = (f32[2,1,128]{2,1,0:T(1,128)S(1)}, f32[2,1,128]{2,1,0:T(1,128)}, u32[]{:S(2)}) copy-start(f32[2,1,128]{2,1,0:T(1,128)} %copy-done.63) | copy-start | bytes 3076
  852.7 94.4 %copy-start.66 = (f32[2,128]{1,0:T(2,128)S(1)}, f32[2,128]{1,0:T(2,128)}, u32[]{:S(2)}) copy-start(f32[2,128]{1,0:T(2,128)} %copy-done.65) | copy-start | bytes 3076
  852.7 94.4 %copy-start.24 = (f32[2,128,512]{2,1,0:T(8,128)S(1)}, f32[2,128,512]{2,1,0:T(8,128)}, u32[]{:S(2)}) copy-start(f32[2,128,512]{2,1,0:T(8,128)} %copy-done.23) | copy-start | bytes 1572868
  852.7 94.6 %copy-start.72 = (f32[2,128]{1,0:T(2,128)S(1)}, f32[2,128]{1,0:T(2,128)}, u32[]{:S(2)}) copy-start(f32[2,128]{1,0:T(2,128)} %copy-done.71) | copy-start | bytes 3076
  852.7 311.8 %reduce-scatter.40.cloned.1.call-start = ((), (), s32[]{:S(2)}) async-start(), calls=%async_computation.24 | async-start | bytes 1253376 | tf_op jit(solution)/shard_map/reduce_scatter | solution.py:409
  949.6 275.8 %reduce-scatter.42.cloned.1.call-start = ((), (), s32[]{:S(2)}) async-start(), calls=%async_computation.25 | async-start | bytes 1253376 | tf_op jit(solution)/shard_map/reduce_scatter | solution.py:410
  950.3 456.3 %reduce-scatter.52.cloned.1.call-start = ((), (), s32[]{:S(2)}) async-start(), calls=%async_computation.30 | async-start | bytes 23887872
  982.4 606.6 %reduce-scatter.54.cloned.1.call-start = ((), (), s32[]{:S(2)}) async-start(), calls=%async_computation.31 | async-start | bytes 23887872
  1014.2 757.0 %reduce-scatter.56.cloned.1.call-start = ((), (), s32[]{:S(2)}) async-start(), calls=%async_computation.32 | async-start | bytes 23887872
  1047.3 749.6 %reduce-scatter.50.cloned.1.call-start = ((), (), s32[]{:S(2)}) async-start(), calls=%async_computation.29 | async-start | bytes 442368
  1049.3 749.4 %reduce-scatter.38.cloned.1.call-start = ((), (), s32[]{:S(2)}) async-start(), calls=%async_computation.23 | async-start | bytes 221184 | tf_op jit(solution)/shard_map/reduce_scatter | solution.py:431
  1105.3 769.7 %reduce-scatter.46.cloned.1.call-start = ((), (), s32[]{:S(2)}) async-start(), calls=%async_computation.27 | async-start | bytes 98304
  1166.1 710.4 %reduce-scatter.48.cloned.1.call-start = ((), (), s32[]{:S(2)}) async-start(), calls=%async_computation.28 | async-start | bytes 98304
  1227.1 771.1 %reduce-scatter.58.cloned.1.call-start = ((), (), s32[]{:S(2)}) async-start(), calls=%async_computation.33 | async-start | bytes 16920576
  1428.3 744.0 %reduce-scatter.60.cloned.1.call-start = ((), (), s32[]{:S(2)}) async-start(), calls=%async_computation.34 | async-start | bytes 16920576
  1610.7 735.9 %reduce-scatter.62.cloned.1.call-start = ((), (), s32[]{:S(2)}) async-start(), calls=%async_computation.35 | async-start | bytes 16920576
  1800.8 72.9 %copy-start.70 = (f32[2,128]{1,0:T(2,128)S(1)}, f32[2,128]{1,0:T(2,128)}, u32[]{:S(2)}) copy-start(f32[2,128]{1,0:T(2,128)} %copy-done.69) | copy-start | bytes 3076
  1800.9 72.9 %copy-start.7 = (f32[2,128,1152]{2,1,0:T(8,128)S(1)}, f32[2,128,1152]{2,1,0:T(8,128)}, u32[]{:S(2)}) copy-start(f32[2,128,1152]{2,1,0:T(8,128)} %copy-done.6) | copy-start | bytes 3538948
  (86 other events, 691.3 us)
Sparse Core Ops, SparseCore 0:
  9.6 51.4 all-gather.8
  62.6 36.0 all-gather.12
  101.5 50.3 all-gather.10
  153.3 187.7 all-gather.14
  342.5 189.2 all-gather.16
  533.2 189.2 all-gather.18
  842.5 103.4 reduce-scatter.33
  949.8 75.2 reduce-scatter.43
  1028.9 74.7 reduce-scatter.35
  1107.1 57.2 reduce-scatter.39
  1168.1 57.2 reduce-scatter.41
  1227.6 178.9 reduce-scatter.51
  1408.9 180.0 reduce-scatter.53
  1591.2 180.0 reduce-scatter.55
  1773.4 12.1 reduce-scatter.49
  1788.2 10.5 reduce-scatter.37
  1800.8 10.0 reduce-scatter.45
  1812.9 10.0 reduce-scatter.47
  1827.6 170.4 reduce-scatter.57
  2002.7 169.5 reduce-scatter.59
  2177.0 169.5 reduce-scatter.61
where the time goes:
time: 2360 us; the launch traced here: 2350 us
  waiting for transfers between devices  1830 us (78%)
  matrix products  159 us (7%)
  local copies, waits for them, and re-layouts  148 us (6%)
  blocking collectives  115 us (5%)
  other arithmetic  80 us (3%)
    unnamed x30, waiting for transfers between devices  973 us
    all_gather x1, waiting for transfers between devices, body(): lax.all_gather(weight_up, 'wsh', axis=1, tiled=True)  178 us
    all_gather x1, waiting for transfers between devices, body(): lax.all_gather(weight_down, 'wsh', axis=1, tiled=True)  174 us
    all_gather x1, waiting for transfers between devices, body(): lax.all_gather(weight_gate, 'wsh', axis=1, tiled=True)  164 us
    unnamed x183, local copies, waits for them, and re-layouts  117 us
    reduce_scatter x1, waiting for transfers between devices, body(): lax.psum_scatter(grad_pairs, 'ctx', scatter_dimension=0, tiled=True)  93.2 us
    unnamed x3, blocking collectives  75.5 us
    reduce_scatter x1, waiting for transfers between devices, body(): lax.psum_scatter(grad_pair_w[:, head_size:], 'ctx', scatter_dimension=0,...  59.3 us
  transfers between devices with their start and end apart: 21, of which 16 were waited for; matrix products, arithmetic and copies ran while one was open for 11% of the time, Pallas kernels for 0%

commit v1 on v0

v1 whole, which is shorter than its diff:
```python
import functools
import math

import jax
import jax.numpy as jnp
from jax import lax
from jax.experimental import pallas as pl
from jax.experimental.pallas import tpu as pltpu
from jax.sharding import PartitionSpec as P

EPS = 1e-06
ROPE_BASE = 1000000.0
SCORE_SCALE = 0.0625
F32 = jnp.float32
BF16 = jnp.bfloat16


def norm_gain(vector, gain):
    return vector * lax.rsqrt(jnp.mean(vector * vector, -1, keepdims=True) + EPS) * gain


def rotate(vector, cosine, sine):
    middle = vector.shape[-1] // 2
    first = vector[..., :middle]
    second = vector[..., middle:]
    return jnp.concatenate([first * cosine - second * sine, second * cosine + first * sine], -1)


def angle_tables(positions, head_size):
    middle = head_size // 2
    inverse = jnp.exp(
        jnp.arange(middle, dtype=F32) * (-2.0 * math.log(ROPE_BASE) / head_size)
    )
    theta = positions.astype(F32)[:, None] * inverse[None, :]
    return (jnp.cos(theta), jnp.sin(theta))


def gate_up(gate, upward):
    return jax.nn.gelu(gate, approximate=True) * upward


def swap(value):
    return lax.ppermute(value, "wsh", [(0, 1), (1, 0)])


def join_halves(mine, local, other):
    return jnp.where(
        mine == 0,
        jnp.concatenate([local, other], -1),
        jnp.concatenate([other, local], -1),
    )


def half_of(value, which):
    middle = value.shape[-1] // 2
    return jnp.where(which == 0, value[..., :middle], value[..., middle:])


def dot(left, right, dims):
    return lax.dot_general(left, right, (dims, ((), ())), preferred_element_type=F32)


def stack_heads(ref, half, block, heads, size):
    rows = slice(half * block, (half + 1) * block)
    return jnp.concatenate([ref[0, rows, h * size : (h + 1) * size] for h in range(heads)], 0)


def attend_forward_kernel(heads, chunk, q_ref, kv_ref, qpos_ref, kpos_ref, o_ref, mix_ref, tot_ref):
    shards, _, rows, pair = kv_ref.shape
    block, size = rows // 2, pair // 2
    queries = [stack_heads(q_ref, half, block, heads, size) for half in range(2)]
    stacked = heads * block
    sums = [jnp.zeros((stacked, size), F32) for _ in range(2)]
    totals = [jnp.zeros((stacked, 1), F32) for _ in range(2)]
    for first in range(0, shards, chunk):
        span = slice(first * block, (first + chunk) * block)
        for key_half in range(2):
            part = kv_ref[first : first + chunk, 0, key_half * block : (key_half + 1) * block, :]
            part = part.reshape(chunk * block, pair)
            keys, values = part[:, :size], part[:, size:]
            for half in range(key_half, 2):
                weights = jnp.exp(dot(queries[half], keys, ((1,), (1,))) * SCORE_SCALE)
                if half == key_half:
                    allowed = (
                        kpos_ref[key_half : key_half + 1, span]
                        <= qpos_ref[half * stacked : (half + 1) * stacked, :]
                    )
                    weights = jnp.where(allowed, weights, 0.0)
                low = weights.astype(BF16)
                totals[half] += jnp.sum(low.astype(F32), -1, keepdims=True)
                sums[half] += dot(low, values, ((1,), (0,)))
    for half in range(2):
        mixed = sums[half] / totals[half]
        mix_ref[0, half * stacked : (half + 1) * stacked, :] = mixed
        tot_ref[0, half * stacked : (half + 1) * stacked, :] = jnp.broadcast_to(
            totals[half], (stacked, tot_ref.shape[2])
        )
        for h in range(heads):
            o_ref[0, half * block : (half + 1) * block, h * size : (h + 1) * size] = mixed[
                h * block : (h + 1) * block
            ].astype(BF16)


def attend_backward_kernel(
    heads, chunk, q_ref, kv_ref, g_ref, mix_ref, tot_ref, qpos_ref, kpos_ref, dq_ref, dkv_ref
):
    shards, _, rows, pair = kv_ref.shape
    block, size = rows // 2, pair // 2
    stacked = heads * block
    queries, scaled, correction = [], [], []
    for half in range(2):
        queries.append(stack_heads(q_ref, half, block, heads, size))
        grad = stack_heads(g_ref, half, block, heads, size).astype(F32)
        span = slice(half * stacked, (half + 1) * stacked)
        total = tot_ref[0, span, :1]
        delta = jnp.sum(grad * mix_ref[0, span, :], -1, keepdims=True)
        scaled.append((grad / total).astype(BF16))
        correction.append(delta / total)
    grad_query = [jnp.zeros((stacked, size), F32) for _ in range(2)]
    for first in range(0, shards, chunk):
        span = slice(first * block, (first + chunk) * block)
        for key_half in range(2):
            part = kv_ref[first : first + chunk, 0, key_half * block : (key_half + 1) * block, :]
            part = part.reshape(chunk * block, pair)
            keys, values = part[:, :size], part[:, size:]
            grad_keys = jnp.zeros((chunk * block, size), F32)
            grad_values = jnp.zeros((chunk * block, size), F32)
            for half in range(key_half, 2):
                weights = jnp.exp(dot(queries[half], keys, ((1,), (1,))) * SCORE_SCALE)
                if half == key_half:
                    allowed = (
                        kpos_ref[key_half : key_half + 1, span]
                        <= qpos_ref[half * stacked : (half + 1) * stacked, :]
                    )
                    weights = jnp.where(allowed, weights, 0.0)
                low = weights.astype(BF16)
                grad_weights = dot(scaled[half], values, ((1,), (1,)))
                grad_scores = (weights * (grad_weights - correction[half])).astype(BF16)
                grad_query[half] += dot(grad_scores, keys, ((1,), (0,)))
                grad_keys += dot(grad_scores, queries[half], ((0,), (0,)))
                grad_values += dot(low, scaled[half], ((0,), (0,)))
            both = jnp.concatenate([grad_keys * SCORE_SCALE, grad_values], -1).astype(BF16)
            dkv_ref[first : first + chunk, 0, key_half * block : (key_half + 1) * block, :] = (
                both.reshape(chunk, block, pair)
            )
    for half in range(2):
        for h in range(heads):
            dq_ref[0, half * block : (half + 1) * block, h * size : (h + 1) * size] = (
                grad_query[half][h * block : (h + 1) * block] * SCORE_SCALE
            )


def whole(shape):
    return pl.BlockSpec(shape, lambda s: (0,) * len(shape))


def attend_forward(query_low, pairs, query_pos, key_pos, heads):
    sequences, rows, width = query_low.shape
    shards, _, _, pair = pairs.shape
    stacked = query_pos.shape[0]
    row = pl.BlockSpec((1, rows, width), lambda s: (s, 0, 0))
    stack = lambda last: pl.BlockSpec((1, stacked, last), lambda s: (s, 0, 0))
    return pl.pallas_call(
        functools.partial(attend_forward_kernel, heads, min(shards, 16)),
        grid=(sequences,),
        in_specs=[
            row,
            pl.BlockSpec((shards, 1, rows, pair), lambda s: (0, s, 0, 0)),
            whole(query_pos.shape),
            whole(key_pos.shape),
        ],
        out_specs=[row, stack(pair // 2), stack(128)],
        out_shape=[
            jax.ShapeDtypeStruct((sequences, rows, width), BF16),
            jax.ShapeDtypeStruct((sequences, stacked, pair // 2), F32),
            jax.ShapeDtypeStruct((sequences, stacked, 128), F32),
        ],
        name="attend_forward",
    )(query_low, pairs, query_pos, key_pos)


def attend_backward(query_low, pairs, grad_mixed, mixed, totals, query_pos, key_pos, heads):
    sequences, rows, width = query_low.shape
    shards, _, _, pair = pairs.shape
    stacked = query_pos.shape[0]
    row = pl.BlockSpec((1, rows, width), lambda s: (s, 0, 0))
    stack = lambda last: pl.BlockSpec((1, stacked, last), lambda s: (s, 0, 0))
    pairs_spec = pl.BlockSpec((shards, 1, rows, pair), lambda s: (0, s, 0, 0))
    return pl.pallas_call(
        functools.partial(attend_backward_kernel, heads, min(shards, 16)),
        grid=(sequences,),
        in_specs=[
            row,
            pairs_spec,
            row,
            stack(pair // 2),
            stack(128),
            whole(query_pos.shape),
            whole(key_pos.shape),
        ],
        out_specs=[row, pairs_spec],
        out_shape=[
            jax.ShapeDtypeStruct((sequences, rows, width), F32),
            jax.ShapeDtypeStruct(pairs.shape, BF16),
        ],
        name="attend_backward",
    )(query_low, pairs, grad_mixed, mixed, totals, query_pos, key_pos)


def body(
    tokens,
    block_order,
    gain_attn_pre,
    gain_query,
    gain_key,
    gain_attn_post,
    gain_ff_pre,
    gain_ff_post,
    weight_query,
    weight_key,
    weight_value,
    weight_out,
    weight_gate,
    weight_up,
    weight_down,
    cotangent,
):
    sequences, rows, width = tokens.shape
    count = sequences * rows
    block = rows // 2
    devices = lax.axis_size("ctx")
    me = lax.axis_index("ctx")
    mine = lax.axis_index("wsh")

    key_value_other = swap(jnp.concatenate([weight_key, weight_value], 1))
    local_size = weight_key.shape[1]
    gains = [gain_attn_pre, gain_query, gain_key, gain_attn_post, gain_ff_pre, gain_ff_post]
    gain_sizes = [g.shape[0] for g in gains]
    gains_other = swap(jnp.concatenate(gains))
    starts = [sum(gain_sizes[:i]) for i in range(len(gains))]
    attn_pre, query_gain, key_gain, attn_post, ff_pre, ff_post = [
        join_halves(mine, g, gains_other[s : s + n]).astype(F32)
        for g, s, n in zip(gains, starts, gain_sizes)
    ]
    pair_weight = jnp.concatenate(
        [
            join_halves(mine, weight_key, key_value_other[:, :local_size]),
            join_halves(mine, weight_value, key_value_other[:, local_size:]),
        ],
        1,
    )
    weight_query = join_halves(mine, weight_query, swap(weight_query))
    weight_out = join_halves(mine, weight_out, swap(weight_out))

    head_size = query_gain.shape[0]
    heads = weight_query.shape[1] // head_size

    lane = jnp.arange(block, dtype=jnp.int32)
    late_order = 2 * devices - 1 - block_order
    early_pos = (block_order[:, None] * block + lane[None]).reshape(-1)
    late_pos = (late_order[:, None] * block + lane[None]).reshape(-1)
    key_pos = jnp.stack([early_pos, late_pos], 0)
    own_first = lax.dynamic_slice_in_dim(block_order, me, 1)[0]
    own_early = own_first * block + lane
    own_late = (2 * devices - 1 - own_first) * block + lane
    own_pos = jnp.concatenate([own_early, own_late])
    query_pos = jnp.concatenate([jnp.tile(own_early, heads), jnp.tile(own_late, heads)])[:, None]

    inputs = tokens.astype(F32)
    normed, pre_back = jax.vjp(norm_gain, inputs, attn_pre)
    normed_low = normed.astype(BF16)
    key_value = jnp.einsum("srd,de->sre", normed_low, pair_weight, preferred_element_type=F32)
    key_raw = key_value[..., :head_size]
    value_low = key_value[..., head_size:].astype(BF16)
    cosine, sine = angle_tables(own_pos, head_size)

    def key_path(key_in, key_scale):
        return rotate(norm_gain(key_in, key_scale), cosine[None], sine[None])

    def query_path(query_in, query_scale):
        return rotate(
            norm_gain(query_in, query_scale), cosine[None, :, None, :], sine[None, :, None, :]
        )

    key_rot, key_back = jax.vjp(key_path, key_raw, key_gain)
    local_pair = jnp.concatenate([key_rot.astype(BF16), value_low], -1)
    pairs = lax.all_gather(local_pair, "ctx", axis=0, tiled=False)
    query_raw = jnp.einsum(
        "srd,de->sre", normed_low, weight_query, preferred_element_type=F32
    ).reshape(sequences, rows, heads, head_size)
    query_rot, query_back = jax.vjp(query_path, query_raw, query_gain)
    query_low = query_rot.astype(BF16).reshape(sequences, rows, heads * head_size)

    mixed_low, mixed, totals = attend_forward(query_low, pairs, query_pos, key_pos, heads)
    attended = jnp.einsum("sre,ed->srd", mixed_low, weight_out, preferred_element_type=F32)
    post_attn, post_attn_back = jax.vjp(norm_gain, attended, attn_post)
    hidden_state = inputs + post_attn
    ff_input, ff_pre_back = jax.vjp(norm_gain, hidden_state, ff_pre)
    ff_own = ff_input.astype(BF16).reshape(count, width)
    ff_other = swap(ff_own)

    def ff_forward(rows_in):
        gate = dot(rows_in, weight_gate, ((1,), (0,)))
        upward = dot(rows_in, weight_up, ((1,), (0,)))
        activated, gelu_back = jax.vjp(gate_up, gate, upward)
        activated_low = activated.astype(BF16)
        return activated_low, gelu_back, dot(activated_low, weight_down, ((1,), (1,)))

    act_own, gelu_own, lowered_own = ff_forward(ff_own)
    act_other, gelu_other, lowered_other = ff_forward(ff_other)
    lowered = lowered_own + swap(lowered_other.astype(BF16)).astype(F32)
    lowered = lowered.reshape(sequences, rows, width)
    post_ff, post_ff_back = jax.vjp(norm_gain, lowered, ff_post)
    output = (hidden_state + post_ff).astype(BF16)

    grad_output = cotangent.astype(F32)
    grad_lowered, grad_ff_post = post_ff_back(grad_output)
    low_own = grad_lowered.astype(BF16).reshape(count, width)
    low_other = swap(low_own)

    def ff_backward(rows_in, gelu_back):
        grad_gate, grad_up = gelu_back(dot(rows_in, weight_down, ((1,), (0,))))
        grad_gate, grad_up = grad_gate.astype(BF16), grad_up.astype(BF16)
        back = dot(grad_gate, weight_gate, ((1,), (1,))) + dot(grad_up, weight_up, ((1,), (1,)))
        return grad_gate, grad_up, back

    gate_own, up_own, back_own = ff_backward(low_own, gelu_own)
    gate_other, up_other, back_other = ff_backward(low_other, gelu_other)
    grad_ff_input = back_own + swap(back_other.astype(BF16)).astype(F32)
    grad_ff_input = grad_ff_input.reshape(sequences, rows, width)

    def both(own, other):
        return jnp.concatenate([own, other], 0)

    def weight_grad(left, right):
        return dot(left, right, ((0,), (0,))).astype(BF16)

    ff_rows = both(ff_own, ff_other)
    part_down = weight_grad(both(low_own, low_other), both(act_own, act_other))
    part_gate = weight_grad(ff_rows, both(gate_own, gate_other))
    part_up = weight_grad(ff_rows, both(up_own, up_other))

    grad_hidden, grad_ff_pre = ff_pre_back(grad_ff_input)
    grad_hidden = grad_hidden + grad_output
    grad_attended, grad_attn_post = post_attn_back(grad_hidden)
    attended_low = grad_attended.astype(BF16)
    grad_mixed = jnp.einsum(
        "srd,ed->sre", attended_low, weight_out, preferred_element_type=F32
    ).astype(BF16)
    attended_low = attended_low.reshape(count, width)
    mixed_rows = mixed_low.reshape(count, heads * head_size)
    part_out = weight_grad(
        both(mixed_rows, swap(mixed_rows)),
        both(half_of(attended_low, mine), swap(half_of(attended_low, 1 - mine))),
    )
    grad_query, grad_pairs = attend_backward(
        query_low, pairs, grad_mixed, mixed, totals, query_pos, key_pos, heads
    )
    own_grads = lax.psum_scatter(grad_pairs, "ctx", scatter_dimension=0, tiled=False).astype(F32)
    grad_key_raw, grad_key_gain = key_back(own_grads[..., :head_size])
    value_grad_low = own_grads[..., head_size:].astype(BF16)
    grad_query_raw, grad_query_gain = query_back(
        grad_query.reshape(sequences, rows, heads, head_size)
    )
    query_grad_low = grad_query_raw.reshape(count, heads * head_size).astype(BF16)
    key_grad_low = grad_key_raw.astype(BF16).reshape(count, head_size)
    value_grad_low = value_grad_low.reshape(count, head_size)
    grad_normed = (
        dot(query_grad_low, weight_query, ((1,), (1,)))
        + dot(jnp.concatenate([key_grad_low, value_grad_low], -1), pair_weight, ((1,), (1,)))
    ).reshape(sequences, rows, width)
    grad_inputs, grad_attn_pre = pre_back(grad_normed)
    grad_tokens = grad_inputs + grad_hidden

    def columns(which):
        return jnp.concatenate(
            [half_of(v, which) for v in (query_grad_low, key_grad_low, value_grad_low)], -1
        )

    normed_rows = normed_low.reshape(count, width)
    part_qkv = weight_grad(
        both(normed_rows, swap(normed_rows)), both(columns(mine), swap(columns(1 - mine)))
    )

    def reduce_rows(part):
        return lax.psum_scatter(part, "ctx", scatter_dimension=0, tiled=True).astype(F32)

    grad_down_w = reduce_rows(part_down)
    grad_gate_w = reduce_rows(part_gate)
    grad_up_w = reduce_rows(part_up)
    grad_out_w = reduce_rows(part_out)
    grad_qkv = reduce_rows(part_qkv)
    query_cols = query_grad_low.shape[1] // 2
    grad_query_w = grad_qkv[:, :query_cols]
    grad_key_w = grad_qkv[:, query_cols : query_cols + local_size]
    grad_value_w = grad_qkv[:, query_cols + local_size :]

    gain_grads = [
        grad_attn_pre,
        grad_query_gain,
        grad_key_gain,
        grad_attn_post,
        grad_ff_pre,
        grad_ff_post,
    ]
    packed = jnp.concatenate([g.reshape(devices, 2, -1) for g in gain_grads], -1)
    keep = jnp.where(mine == 0, packed[:, 0], packed[:, 1])
    send = jnp.where(mine == 0, packed[:, 1], packed[:, 0])
    packed = lax.psum_scatter(keep + swap(send), "ctx", scatter_dimension=0, tiled=False)
    outs, first = [], 0
    for g in gain_grads:
        size = g.shape[0] // (2 * devices)
        outs.append(packed[first : first + size])
        first += size
    return (
        output,
        grad_tokens,
        *outs,
        grad_query_w,
        grad_key_w,
        grad_value_w,
        grad_out_w,
        grad_gate_w,
        grad_up_w,
        grad_down_w,
    )


def solution(mesh):
    rows, vector, matrix = P("wsh", "ctx", None), P("wsh"), P(None, "wsh")
    in_specs = (rows, P()) + (vector,) * 6 + (matrix,) * 7 + (rows,)
    out_specs = (rows, rows) + (P(("ctx", "wsh")),) * 6 + (P("ctx", "wsh"),) * 7
    return jax.shard_map(body, mesh=mesh, in_specs=in_specs, out_specs=out_specs, check_vma=False)
```

time: 2360 us -> 725 us (0.31)
  waiting for transfers between devices: 1830 us -> 437 us
  local copies, waits for them, and re-layouts: 148 us -> 26.3 us
  blocking collectives: 115 us -> 57.7 us
  other arithmetic: 80 us -> 33.5 us
  matrix products: 159 us -> 114 us
    unnamed x30 -> x10, waiting for transfers between devices: 973 us -> 291 us
    all_gather x6 -> x1, waiting for transfers between devices: 590 us -> 15 us  [body(): pairs = lax.all_gather(local_pair, 'ctx', axis=0, tiled=False)]
    reduce_scatter x6 -> x3, waiting for transfers between devices: 266 us -> 51.9 us  [the longest x1 37.3 us: body(): lax.psum_scatter(grad_pairs, 'ctx', scatter_dimension=0, tiled=False)]
    unnamed x183 -> x125, local copies, waits for them, and re-layouts: 117 us -> 5.29 us
    ppermute x0 -> x13, waiting for transfers between devices: none -> 79 us  [swap(): return lax.ppermute(value, 'wsh', [(0, 1), (1, 0)])]
    dot_general x56 -> x21, matrix products: 156 us -> 110 us  [the longest x19 102 us: dot(): lax.dot_general(left, right, (dims, ((), ())), preferred_element_type=F32)]
    all_gather x4 -> x0, blocking collectives: 39.4 us -> none  [the longest x1 15.7 us: body(): lax.all_gather(weight_value, 'wsh', axis=1, tiled=True)]
    convert_element_type x33 -> x18, other arithmetic: 51 us -> 13 us  [the longest x4 7.7 us: reduce_rows(): lax.psum_scatter(part, 'ctx', scatter_dimension=0, tiled=True).astype(F32)]
  transfers between devices with their start and end apart: 21 -> 20, of which waited for: 16 -> 16; matrix products, arithmetic and copies ran while one was open for 11% -> 15% of each run, Pallas kernels for 0% -> 1%
where the time goes in v1:
time: 725 us; the launch traced here: 719 us
  waiting for transfers between devices  437 us (60%)
  matrix products  114 us (16%)
  blocking collectives  57.7 us (8%)
  other arithmetic  33.5 us (5%)
  local copies, waits for them, and re-layouts  26.3 us (4%)
  starting transfers between devices  18.7 us (3%)
  between operations  16.9 us (2%)
  Pallas kernels  15 us (2%)
    unnamed x10, waiting for transfers between devices  291 us
    dot_general x19, matrix products, dot(): lax.dot_general(left, right, (dims, ((), ())), preferred_element_type=F32)  102 us
    ppermute x13, waiting for transfers between devices, swap(): return lax.ppermute(value, 'wsh', [(0, 1), (1, 0)])  79 us
    unnamed x1, blocking collectives  57.7 us
    reduce_scatter x1, waiting for transfers between devices, body(): lax.psum_scatter(grad_pairs, 'ctx', scatter_dimension=0, tiled=False)  37.3 us
    ppermute x13, starting transfers between devices, swap(): return lax.ppermute(value, 'wsh', [(0, 1), (1, 0)])  17.9 us
    all_gather x1, waiting for transfers between devices, body(): pairs = lax.all_gather(local_pair, 'ctx', axis=0, tiled=False)  15 us
    reduce_scatter x2, waiting for transfers between devices, reduce_rows(): lax.psum_scatter(part, 'ctx', scatter_dimension=0, tiled=True).astype(F32)  14.6 us
  transfers between devices with their start and end apart: 20, of which 16 were waited for; matrix products, arithmetic and copies ran while one was open for 15% of the time, Pallas kernels for 1%

profile of v1, /device:TPU:0, one launch (start us, length us, event | category | flops | bytes accessed | tf_op | source)
XLA Modules:
  0.0 718.8 jit_solution(8114512666734239157)
XLA Ops:
  7.3 4.2 concatenate.176
  19.8 10.6 %collective-permute-done.2 = bf16[1152,256]{1,0:T(8,128)(2,1)S(1)} collective-permute-done((bf16[1152,256]{1,0:T(8,128)(2,1)S(1)}, bf16[1152,256]{1,0:T(8,128)(2,1)S(1)}, u32[]{:S(2)}, u32[]{:S(2)}) %collective-permute-start.2) | collective-permute-done | bytes 589856 | tf_op jit(solution)/shard_map/ppermute | solution.py:43
  37.6 25.0 %collective-permute-done.1 = bf16[1152,512]{1,0:T(8,128)(2,1)} collective-permute-done((bf16[1152,512]{1,0:T(8,128)(2,1)}, bf16[1152,512]{1,0:T(8,128)(2,1)}, u32[]{:S(2)}, u32[]{:S(2)}) %collective-permute-start.1) | collective-permute-done | bytes 1179680 | tf_op jit(solution)/shard_map/ppermute | solution.py:43
  69.1 15.0 %all-gather.3.cloned.1.call-done = bf16[32,128,512]{2,1,0:T(8,128)(2,1)} async-done(((bf16[2,128,512]{2,1,0:T(8,128)(2,1)}), bf16[32,128,512]{2,1,0:T(8,128)(2,1)}) %all-gather.3.cloned.1.call-update) | async-done | bytes 4194320 | tf_op jit(solution)/shard_map/all_gather | solution.py:287
  84.2 6.1 attend_forward.1
  90.2 3.6 multiply_reduce_fusion.6
  96.0 8.3 %fusion.105 = f32[256,3456]{1,0:T(8,128)} fusion(bf16[256,1152]{1,0:T(8,128)(2,1)S(1)} %bitcast.110, bf16[1152,3456]{1,0:T(8,128)(2,1)} %param.28), kind=kOutput, calls=%fused_computation.224 | convolution fusion | flops 2038431744 | bytes 12091392 | tf_op jit(solution)/shard_map/dot_general | solution.py:60
  104.3 5.7 collective-permute-done.4
  112.6 7.8 %multiply_convert_fusion.2 = (bf16[256,3456]{1,0:T(8,128)(2,1)S(1)}, f32[256,3456]{1,0:T(8,128)}) fusion(f32[256,3456]{1,0:T(8,128)S(1)} %fusion.106, bf16[256,1152]{1,0:T(8,128)(2,1)S(1)} %collective-permute-done.4, bf16[1152,3456]{1,0:T(8,128)(2,1)} %param.29), kind=kOutput, calls=%fused_computation.32 | convolution fusion | flops 2047279104 | bytes 17399808 | tf_op jit(solution)/shard_map/dot_general | solution.py:60
  124.5 8.9 %multiply_convert_fusion.3 = (bf16[256,3456]{1,0:T(8,128)(2,1)S(1)}, f32[256,3456]{1,0:T(8,128)}) fusion(f32[256,3456]{1,0:T(8,128)} %fusion.105, bf16[256,1152]{1,0:T(8,128)(2,1)S(1)} %bitcast.111, bf16[1152,3456]{1,0:T(8,128)(2,1)} %param.29), kind=kOutput, calls=%fused_computation.33 | convolution fusion | flops 2047279104 | bytes 17399808 | tf_op jit(solution)/shard_map/dot_general | solution.py:60
  133.4 4.2 collective-permute-done.5
  144.2 7.7 %multiply_convert_fusion.1 = (bf16[256,3456]{1,0:T(8,128)(2,1)S(1)}, bf16[256,3456]{1,0:T(8,128)(2,1)}) fusion(f32[256,3456]{1,0:T(8,128)} %fusion.105, f32[256,3456]{1,0:T(8,128)} %get-tuple-element.89, bf16[256,1152]{1,0:T(8,128)(2,1)S(1)} %bitcast.107, bf16[1152,3456]{1,0:T(8,128)(2,1)S(1)} %bitcast.124), kind=kOutput, calls=%fused_computation.31 | convolution fusion | flops 2059665408 | bytes 19169280 | tf_op jit(solution)/shard_map/dot_general | solution.py:60
  151.8 4.6 collective-permute-done.6
  156.4 6.0 multiply_convert_fusion
  162.5 4.2 fusion.108
  166.7 6.0 fusion.23
  176.8 8.8 %collective-permute-done.7 = bf16[256,1152]{1,0:T(8,128)(2,1)S(1)} collective-permute-done((bf16[256,1152]{1,0:T(8,128)(2,1)S(1)}, bf16[256,1152]{1,0:T(8,128)(2,1)S(1)}, u32[]{:S(2)}, u32[]{:S(2)}) %collective-permute-start.7) | collective-permute-done | bytes 589856 | tf_op jit(solution)/shard_map/ppermute | solution.py:43
  185.6 5.8 convert_add_fusion.2
  193.8 4.3 fusion.35.g_ref
  198.1 8.9 %attend_backward.1 = (f32[2,128,1024]{2,1,0:T(8,128)}, bf16[16,2,128,512]{3,2,1,0:T(8,128)(2,1)}) custom-call(bf16[2,128,1024]{2,1,0:T(8,128)(2,1)} %convert_element_type.161.q_ref, bf16[16,2,128,512]{3,2,1,0:T(8,128)(2,1)} %bitcast.98, bf16[2,128,1024]{2,1,0:T(8,128)(2,1)} %fusion.35.g_ref, f32[2,512,256]{2,1,0:T(8,128)} %get-tuple-element.21.mix_ref, ...), custom_call_target="tpu_custom_call" | custom-call | tf_op jit(solution)/shard_map/attend_backward/pallas_call | solution.py:189
  226.6 7.9 %collective-permute-done.11 = bf16[256,1024]{1,0:T(8,128)(2,1)} collective-permute-done((bf16[256,1024]{1,0:T(8,128)(2,1)}, bf16[256,1024]{1,0:T(8,128)(2,1)}, u32[]{:S(2)}, u32[]{:S(2)}) %collective-permute-start.11) | collective-permute-done | bytes 524320 | tf_op jit(solution)/shard_map/ppermute | solution.py:43
  241.3 37.3 %reduce-scatter.13.cloned.1.call-done = bf16[1,2,128,512]{3,2,1,0:T(8,128)(2,1)} async-done(((bf16[16,2,128,512]{3,2,1,0:T(8,128)(2,1)}), bf16[1,2,128,512]{3,2,1,0:T(8,128)(2,1)}) %reduce-scatter.13.cloned.1.call-update) | async-done | bytes 262160 | tf_op jit(solution)/shard_map/reduce_scatter | solution.py:359
  284.2 7.8 %collective-permute-done.10 = bf16[256,768]{1,0:T(8,128)(2,1)S(1)} collective-permute-done((bf16[256,768]{1,0:T(8,128)(2,1)S(1)}, bf16[256,768]{1,0:T(8,128)(2,1)S(1)}, u32[]{:S(2)}, u32[]{:S(2)}) %collective-permute-start.10) | collective-permute-done | bytes 393248 | tf_op jit(solution)/shard_map/ppermute | solution.py:43
  292.0 3.5 convolution_convert_fusion.3
  296.8 8.6 %convolution_convert_fusion.2 = bf16[1152,3456]{1,0:T(8,128)(2,1)} fusion(bf16[256,3456]{1,0:T(8,128)(2,1)} %get-tuple-element.42, bf16[256,3456]{1,0:T(8,128)(2,1)} %get-tuple-element.44, bf16[256,1152]{1,0:T(8,128)(2,1)S(1)} %copy-done.46, bf16[256,1152]{1,0:T(8,128)(2,1)S(1)} %bitcast.112), kind=kOutput, calls=%fused_computation.2 | convolution fusion | flops 4090281984 | bytes 12681216 | tf_op jit(solution)/shard_map/dot_general | solution.py:60
  305.4 8.4 %convolution_convert_fusion.1 = bf16[1152,3456]{1,0:T(8,128)(2,1)} fusion(bf16[256,3456]{1,0:T(8,128)(2,1)} %get-tuple-element.41, bf16[256,3456]{1,0:T(8,128)(2,1)} %copy-done.54, bf16[256,1152]{1,0:T(8,128)(2,1)S(1)} %copy-done.46, bf16[256,1152]{1,0:T(8,128)(2,1)S(1)} %bitcast.113), kind=kOutput, calls=%fused_computation.1 | convolution fusion | flops 4090281984 | bytes 12681216 | tf_op jit(solution)/shard_map/dot_general | solution.py:60
  315.1 8.4 %convolution_convert_fusion = bf16[1152,3456]{1,0:T(8,128)(2,1)} fusion(bf16[256,3456]{1,0:T(8,128)(2,1)} %copy-done.52, bf16[256,3456]{1,0:T(8,128)(2,1)} %copy-done.53, bf16[256,1152]{1,0:T(8,128)(2,1)S(1)} %copy-done.48, bf16[256,1152]{1,0:T(8,128)(2,1)S(1)} %bitcast.108), kind=kOutput, calls=%fused_computation | convolution fusion | flops 4090281984 | bytes 12681216 | tf_op jit(solution)/shard_map/dot_general | solution.py:60
  325.2 14.6 %reduce-scatter.17.cloned.1.call-done = bf16[64,576]{1,0:T(8,128)(2,1)} async-done(((bf16[1024,576]{1,0:T(8,128)(2,1)}), bf16[64,576]{1,0:T(8,128)(2,1)}) %reduce-scatter.17.cloned.1.call-update) | async-done | bytes 73744 | tf_op jit(solution)/shard_map/reduce_scatter | solution.py:386
  351.1 57.7 %all-reduce.4 = f32[16,160]{1,0:T(8,128)S(1)} all-reduce(f32[16,160]{1,0:T(8,128)S(1)} %fusion.77), channel_id=4, replica_groups=mesh['ctx'=16,'wsh'=2] {'ctx'}, use_global_device_ids=true, to_apply=%region_19.20.clone | all-reduce | flops 2560 | bytes 20480
  414.3 89.7 %reduce-scatter.19.cloned.1.call-done = bf16[72,3456]{1,0:T(8,128)(2,1)} async-done(((bf16[1152,3456]{1,0:T(8,128)(2,1)}), bf16[72,3456]{1,0:T(8,128)(2,1)}) %reduce-scatter.19.cloned.1.call-update) | async-done | bytes 497680
  506.0 100.6 %reduce-scatter.21.cloned.1.call-done = bf16[72,3456]{1,0:T(8,128)(2,1)} async-done(((bf16[1152,3456]{1,0:T(8,128)(2,1)}), bf16[72,3456]{1,0:T(8,128)(2,1)}) %reduce-scatter.21.cloned.1.call-update) | async-done | bytes 497680
  608.7 100.8 %reduce-scatter.23.cloned.1.call-done = bf16[72,3456]{1,0:T(8,128)(2,1)} async-done(((bf16[1152,3456]{1,0:T(8,128)(2,1)}), bf16[72,3456]{1,0:T(8,128)(2,1)}) %reduce-scatter.23.cloned.1.call-update) | async-done | bytes 497680
  (266 shorter events, 101.0 us)
Async XLA Ops:
  7.2 76.9 %all-gather.3.cloned.1.call-start = ((), (), s32[]{:S(2)}) async-start(), calls=%async_computation.9 | async-start | bytes 4456448 | tf_op jit(solution)/shard_map/all_gather | solution.py:287
  11.5 7.9 %collective-permute-start = (bf16[2560]{0:T(1024)(128)(2,1)S(1)}, bf16[2560]{0:T(1024)(128)(2,1)S(1)}, u32[]{:S(2)}, u32[]{:S(2)}) collective-permute-start(bf16[2560]{0:T(1024)(128)(2,1)S(1)} %concatenate.176), channel_id=1, source_target_pairs={{0,1},{1,0},{2,3},{3,2},{4,5},{5,4},{6,7},{7,6},{8,9},{9,8},{10,11... | collective-permute-start | bytes 15368 | tf_op jit(solution)/shard_map/ppermute | solution.py:43
  15.6 14.9 %collective-permute-start.2 = (bf16[1152,256]{1,0:T(8,128)(2,1)S(1)}, bf16[1152,256]{1,0:T(8,128)(2,1)S(1)}, u32[]{:S(2)}, u32[]{:S(2)}) collective-permute-start(bf16[1152,256]{1,0:T(8,128)(2,1)S(1)} %pad_maximum_fusion.7), channel_id=1, source_target_pairs={{0,1},{1,0},{2,3},{3,2},{4,5},{5,4},{6,7},{7,6},{8,9},{9,8},{10,11... | collective-permute-start | bytes 1769480 | tf_op jit(solution)/shard_map/ppermute | solution.py:43
  19.3 48.1 %copy-start.6 = (f32[128,128]{1,0:T(8,128)}, f32[128,128]{1,0:T(8,128)S(1)}, u32[]{:S(2)}) copy-start(f32[128,128]{1,0:T(8,128)S(1)} %get-tuple-element.83) | copy-start | bytes 196612
  19.8 42.8 %copy-start.18 = (bf16[2,128,1152]{2,1,0:T(8,128)(2,1)}, bf16[2,128,1152]{2,1,0:T(8,128)(2,1)S(1)}, u32[]{:S(2)}) copy-start(bf16[2,128,1152]{2,1,0:T(8,128)(2,1)S(1)} %fusion.38) | copy-start | bytes 1769476
  32.3 33.6 %copy-start.29 = (f32[2,128]{1,0:T(2,128)}, f32[2,128]{1,0:T(2,128)S(1)}, u32[]{:S(2)}) copy-start(f32[2,128]{1,0:T(2,128)S(1)} %fusion.84) | copy-start | bytes 3076
  33.3 245.3 %reduce-scatter.13.cloned.1.call-start = ((), (), s32[]{:S(2)}) async-start(), calls=%async_computation.6 | async-start | bytes 4456448 | tf_op jit(solution)/shard_map/reduce_scatter | solution.py:359
  33.4 29.2 %collective-permute-start.1 = (bf16[1152,512]{1,0:T(8,128)(2,1)}, bf16[1152,512]{1,0:T(8,128)(2,1)}, u32[]{:S(2)}, u32[]{:S(2)}) collective-permute-start(bf16[1152,512]{1,0:T(8,128)(2,1)} %param.24), channel_id=1, source_target_pairs={{0,1},{1,0},{2,3},{3,2},{4,5},{5,4},{6,7},{7,6},{8,9},{9,8},{10,11... | collective-permute-start | bytes 3538952 | tf_op jit(solution)/shard_map/ppermute | solution.py:43
  33.7 56.5 %collective-permute-start.3 = (bf16[1024,576]{0,1:T(8,128)(2,1)}, bf16[1024,576]{0,1:T(8,128)(2,1)}, u32[]{:S(2)}, u32[]{:S(2)}) collective-permute-start(bf16[1024,576]{0,1:T(8,128)(2,1)} %param.27), channel_id=1, source_target_pairs={{0,1},{1,0},{2,3},{3,2},{4,5},{5,4},{6,7},{7,6},{8,9},{9,8},{10,11... | collective-permute-start | bytes 3538952 | tf_op jit(solution)/shard_map/ppermute | solution.py:43
  37.4 29.7 %copy-start.31 = (f32[256]{0:T(256)}, f32[256]{0:T(256)S(1)}, u32[]{:S(2)}) copy-start(f32[256]{0:T(256)S(1)} %fusion.87) | copy-start | bytes 3076
  94.4 30.0 %copy-start.16 = (bf16[2,128,1152]{2,1,0:T(8,128)(2,1)}, bf16[2,128,1152]{2,1,0:T(8,128)(2,1)S(1)}, u32[]{:S(2)}) copy-start(bf16[2,128,1152]{2,1,0:T(8,128)(2,1)S(1)} %multiply_convert_fusion.4) | copy-start | bytes 1769476
  94.5 15.5 %collective-permute-start.4 = (bf16[256,1152]{1,0:T(8,128)(2,1)S(1)}, bf16[256,1152]{1,0:T(8,128)(2,1)S(1)}, u32[]{:S(2)}, u32[]{:S(2)}) collective-permute-start(bf16[256,1152]{1,0:T(8,128)(2,1)S(1)} %bitcast.109), channel_id=1, source_target_pairs={{0,1},{1,0},{2,3},{3,2},{4,5},{5,4},{6,7},{7,6},{8,9},{9,8},{10,11... | collective-permute-start | bytes 1769480 | tf_op jit(solution)/shard_map/ppermute | solution.py:43
  122.9 14.7 %collective-permute-start.5 = (bf16[256,1152]{1,0:T(8,128)(2,1)S(1)}, bf16[256,1152]{1,0:T(8,128)(2,1)S(1)}, u32[]{:S(2)}, u32[]{:S(2)}) collective-permute-start(bf16[256,1152]{1,0:T(8,128)(2,1)S(1)} %convolution_convert_fusion.4), channel_id=1, source_target_pairs={{0,1},{1,0},{2,3},{3,2},{4,5},{5,4},{6,7},{7,6},{8,9},{9,8},{10,11... | collective-permute-start | bytes 1769480 | tf_op jit(solution)/shard_map/ppermute | solution.py:43
  142.7 13.7 %collective-permute-start.6 = (bf16[256,1152]{1,0:T(8,128)(2,1)S(1)}, bf16[256,1152]{1,0:T(8,128)(2,1)S(1)}, u32[]{:S(2)}, u32[]{:S(2)}) collective-permute-start(bf16[256,1152]{1,0:T(8,128)(2,1)S(1)} %bitcast.106), channel_id=1, source_target_pairs={{0,1},{1,0},{2,3},{3,2},{4,5},{5,4},{6,7},{7,6},{8,9},{9,8},{10,11... | collective-permute-start | bytes 1769480 | tf_op jit(solution)/shard_map/ppermute | solution.py:43
  151.8 33.8 %copy-start.54 = (bf16[256,3456]{1,0:T(8,128)(2,1)}, bf16[256,3456]{1,0:T(8,128)(2,1)S(1)}, u32[]{:S(2)}) copy-start(bf16[256,3456]{1,0:T(8,128)(2,1)S(1)} %get-tuple-element.43) | copy-start | bytes 5308420
  172.6 13.0 %collective-permute-start.7 = (bf16[256,1152]{1,0:T(8,128)(2,1)S(1)}, bf16[256,1152]{1,0:T(8,128)(2,1)S(1)}, u32[]{:S(2)}, u32[]{:S(2)}) collective-permute-start(bf16[256,1152]{1,0:T(8,128)(2,1)S(1)} %fusion.23), channel_id=1, source_target_pairs={{0,1},{1,0},{2,3},{3,2},{4,5},{5,4},{6,7},{7,6},{8,9},{9,8},{10,11... | collective-permute-start | bytes 1769480 | tf_op jit(solution)/shard_map/ppermute | solution.py:43
  207.0 132.8 %reduce-scatter.17.cloned.1.call-start = ((), (), s32[]{:S(2)}) async-start(), calls=%async_computation.8 | async-start | bytes 1392640 | tf_op jit(solution)/shard_map/reduce_scatter | solution.py:386
  207.4 76.8 %collective-permute-start.9 = (bf16[256,1152]{1,0:T(8,128)(2,1)}, bf16[256,1152]{1,0:T(8,128)(2,1)}, u32[]{:S(2)}, u32[]{:S(2)}) collective-permute-start(bf16[256,1152]{1,0:T(8,128)(2,1)} %bitcast.115), channel_id=1, source_target_pairs={{0,1},{1,0},{2,3},{3,2},{4,5},{5,4},{6,7},{7,6},{8,9},{9,8},{10,11... | collective-permute-start | bytes 1769480 | tf_op jit(solution)/shard_map/ppermute | solution.py:43
  208.9 25.6 %collective-permute-start.11 = (bf16[256,1024]{1,0:T(8,128)(2,1)}, bf16[256,1024]{1,0:T(8,128)(2,1)}, u32[]{:S(2)}, u32[]{:S(2)}) collective-permute-start(bf16[256,1024]{1,0:T(8,128)(2,1)} %bitcast.25), channel_id=1, source_target_pairs={{0,1},{1,0},{2,3},{3,2},{4,5},{5,4},{6,7},{7,6},{8,9},{9,8},{10,11... | collective-permute-start | bytes 1572872 | tf_op jit(solution)/shard_map/ppermute | solution.py:43
  222.4 15.5 %collective-permute-start.12 = (bf16[256,576]{1,0:T(8,128)(2,1)}, bf16[256,576]{1,0:T(8,128)(2,1)S(1)}, u32[]{:S(2)}, u32[]{:S(2)}) collective-permute-start(bf16[256,576]{1,0:T(8,128)(2,1)} %get-tuple-element.54), channel_id=1, source_target_pairs={{0,1},{1,0},{2,3},{3,2},{4,5},{5,4},{6,7},{7,6},{8,9},{9,8},{10,11... | collective-permute-start | bytes 884744 | tf_op jit(solution)/shard_map/ppermute | solution.py:43
  241.2 39.4 %copy-start.7 = (f32[128,128]{1,0:T(8,128)S(1)}, f32[128,128]{1,0:T(8,128)}, u32[]{:S(2)}) copy-start(f32[128,128]{1,0:T(8,128)} %copy-done.6) | copy-start | bytes 196612
  241.2 39.5 %copy-start.4 = (f32[2,128,512]{2,1,0:T(8,128)S(1)}, f32[2,128,512]{2,1,0:T(8,128)}, u32[]{:S(2)}) copy-start(f32[2,128,512]{2,1,0:T(8,128)} %copy-done.3) | copy-start | bytes 1572868
  241.2 39.5 %copy-start.30 = (f32[2,128]{1,0:T(2,128)S(1)}, f32[2,128]{1,0:T(2,128)}, u32[]{:S(2)}) copy-start(f32[2,128]{1,0:T(2,128)} %copy-done.29) | copy-start | bytes 3076
  241.2 40.2 %copy-start.36 = (f32[2,128]{1,0:T(2,128)S(1)}, f32[2,128]{1,0:T(2,128)}, u32[]{:S(2)}) copy-start(f32[2,128]{1,0:T(2,128)} %copy-done.35) | copy-start | bytes 3076
  241.2 170.1 %reduce-scatter.15.cloned.1.call-start = ((), (), s32[]{:S(2)}) async-start(), calls=%async_computation.7 | async-start | bytes 1880064 | tf_op jit(solution)/shard_map/reduce_scatter | solution.py:386
  282.6 9.4 %collective-permute-start.10 = (bf16[256,768]{1,0:T(8,128)(2,1)S(1)}, bf16[256,768]{1,0:T(8,128)(2,1)S(1)}, u32[]{:S(2)}, u32[]{:S(2)}) collective-permute-start(bf16[256,768]{1,0:T(8,128)(2,1)S(1)} %pad_maximum_fusion.10), channel_id=1, source_target_pairs={{0,1},{1,0},{2,3},{3,2},{4,5},{5,4},{6,7},{7,6},{8,9},{9,8},{10,11... | collective-permute-start | bytes 1179656 | tf_op jit(solution)/shard_map/ppermute | solution.py:43
  295.6 208.4 %reduce-scatter.19.cloned.1.call-start = ((), (), s32[]{:S(2)}) async-start(), calls=%async_computation.10 | async-start | bytes 8460288
  305.4 301.2 %reduce-scatter.21.cloned.1.call-start = ((), (), s32[]{:S(2)}) async-start(), calls=%async_computation.11 | async-start | bytes 8460288
  313.9 395.6 %reduce-scatter.23.cloned.1.call-start = ((), (), s32[]{:S(2)}) async-start(), calls=%async_computation.12 | async-start | bytes 8460288
  323.6 17.9 %copy-start.13 = (bf16[1152,256]{1,0:T(8,128)(2,1)S(1)}, bf16[1152,256]{1,0:T(8,128)(2,1)}, u32[]{:S(2)}) copy-start(bf16[1152,256]{1,0:T(8,128)(2,1)} %copy-done.12) | copy-start | bytes 1769476
  323.6 17.8 %copy-start.15 = (bf16[1152,256]{1,0:T(8,128)(2,1)S(1)}, bf16[1152,256]{1,0:T(8,128)(2,1)}, u32[]{:S(2)}) copy-start(bf16[1152,256]{1,0:T(8,128)(2,1)} %copy-done.14) | copy-start | bytes 1769476
  347.3 3.8 collective-permute-start.8
  (49 other events, 306.0 us)
Sparse Core Ops, SparseCore 0:
  33.4 50.6 all-gather.2
  207.2 71.4 reduce-scatter.12
  282.3 57.5 reduce-scatter.16
  343.5 58.4 reduce-scatter.14
  405.9 97.9 reduce-scatter.18
  507.9 98.7 reduce-scatter.20
  610.7 98.7 reduce-scatter.22

commit v2 on v1

--- a/solution.py
+++ b/solution.py
@@ -13,6 +13,7 @@
 SCORE_SCALE = 0.0625
 F32 = jnp.float32
 BF16 = jnp.bfloat16
+MESH = pl.DeviceIdType.MESH
 
 
 def norm_gain(vector, gain):
@@ -207,6 +208,199 @@
     )(query_low, pairs, grad_mixed, mixed, totals, query_pos, key_pos)
 
 
+class Ring:
+    def __init__(self, devices):
+        self.chips = devices // 2
+        me = lax.axis_index("ctx")
+        self.core = me % 2
+        chip = me // 2
+        across = chip % 2
+        deep = chip // 2
+        self.place = deep + across * (self.chips - 1 - 2 * deep)
+        self.partner = me + 1 - 2 * self.core
+        self.right = self.device((self.place + 1) % self.chips, self.core)
+        self.left = self.device((self.place + self.chips - 1) % self.chips, self.core)
+
+    def device(self, place, core):
+        side = place // (self.chips // 2)
+        return 2 * (2 * (place + side * (self.chips - 1 - 2 * place)) + side) + core
+
+    def enter(self):
+        barrier = pltpu.get_barrier_semaphore()
+        for other in (self.left, self.right, self.partner):
+            pl.semaphore_signal(barrier, inc=1, device_id={"ctx": other}, device_id_type=MESH)
+        pl.semaphore_wait(barrier, 3)
+
+
+def ring_sum_kernel(devices, pieces, arrays, ahead, *refs):
+    parts, outs = refs[:arrays], refs[arrays : 2 * arrays]
+    own, other, flow = (refs[(2 + i) * arrays : (3 + i) * arrays] for i in range(3))
+    own_sem, put_sem, got_sem, send_sem, recv_sem = refs[5 * arrays :]
+    ring = Ring(devices)
+    chips = ring.chips
+
+    def region(p):
+        array, _, first, rows, start, cols = pieces[p]
+        return array, pl.ds(first, rows), pl.ds(start, cols)
+
+    def chunk(p, step):
+        way = pieces[p][1]
+        return (ring.place + 2 * chips + way * (-1 - step)) % chips
+
+    def load(p, step):
+        array, rows, cols = region(p)
+        source = ring.device(chunk(p, step), ring.core)
+        return pltpu.make_async_copy(
+            parts[array].at[source, rows, cols],
+            own[array].at[step, rows, cols],
+            own_sem.at[p, step],
+        )
+
+    def give(p, step):
+        array, rows, cols = region(p)
+        source = ring.device(chunk(p, step), 1 - ring.core)
+        return pltpu.make_async_remote_copy(
+            src_ref=parts[array].at[source, rows, cols],
+            dst_ref=other[array].at[step, rows, cols],
+            send_sem=put_sem.at[p, step],
+            recv_sem=got_sem.at[p, step],
+            device_id={"ctx": ring.partner},
+            device_id_type=MESH,
+        )
+
+    def pass_on(p, step):
+        array, rows, cols = region(p)
+        way = pieces[p][1]
+        return pltpu.make_async_remote_copy(
+            src_ref=flow[array].at[step, rows, cols],
+            dst_ref=flow[array].at[step + 1, rows, cols],
+            send_sem=send_sem.at[p, step],
+            recv_sem=recv_sem.at[p, step],
+            device_id={"ctx": ring.right if way > 0 else ring.left},
+            device_id_type=MESH,
+        )
+
+    def fetch(step):
+        for p in range(len(pieces)):
+            load(p, step).start()
+            give(p, step).start()
+
+    def add(p, step, first, last):
+        array, _, row, rows, start, cols = pieces[p]
+        width = 128 if cols % 128 == 0 else cols
+        while width < 512 and cols % (2 * width) == 0:
+            width *= 2
+        rows = pl.ds(row, rows)
+
+        def group(i, carry):
+            at = start + i * width
+            if cols > width:
+                at = pl.multiple_of(at, 128)
+            where = pl.ds(at, width)
+            total = own[array][step, rows, where].astype(F32) + other[array][
+                step, rows, where
+            ].astype(F32)
+            if not first:
+                total += flow[array][step, rows, where].astype(F32)
+            if last:
+                outs[array][rows, where] = total.astype(outs[array].dtype)
+            else:
+                flow[array][step, rows, where] = total.astype(flow[array].dtype)
+            return carry
+
+        if cols == width:
+            group(0, 0)
+        else:
+            lax.fori_loop(0, cols // width, group, 0)
+
+    def work(step, first=False, last=False):
+        for p in range(len(pieces)):
+            load(p, step).wait()
+            give(p, step).wait_recv()
+            if not first:
+                pass_on(p, step - 1).wait_recv()
+            add(p, step, first, last)
+            if not last:
+                pass_on(p, step).start()
+
+    for p in range(len(pieces)):
+        load(p, 0).start()
+    ring.enter()
+    for p in range(len(pieces)):
+        give(p, 0).start()
+    for step in range(1, min(ahead, chips)):
+        fetch(step)
+    work(0, first=True)
+
+    def middle(step, carry):
+        @pl.when(step + ahead - 1 < chips)
+        def _():
+            fetch(step + ahead - 1)
+
+        work(step)
+        return carry
+
+    lax.fori_loop(1, chips - 1, middle, 0)
+    work(chips - 1, last=True)
+
+    def drain(step, carry):
+        for p in range(len(pieces)):
+            give(p, step).wait_send()
+
+            @pl.when(step < chips - 1)
+            def _():
+                pass_on(p, step).wait_send()
+
+        return carry
+
+    lax.fori_loop(0, chips, drain, 0)
+
+
+def ring_sum(parts, pieces, devices, collective_id, ahead=3, name="ring_sum"):
+    chips, count, arrays = devices // 2, len(pieces), len(parts)
+    slots = [pltpu.VMEM((chips,) + p.shape[1:], p.dtype) for p in parts]
+    return pl.pallas_call(
+        functools.partial(ring_sum_kernel, devices, pieces, arrays, ahead),
+        out_shape=[jax.ShapeDtypeStruct(p.shape[1:], F32) for p in parts],
+        in_specs=[pl.BlockSpec(memory_space=pl.ANY)] * arrays,
+        out_specs=[pl.BlockSpec(memory_space=pltpu.VMEM)] * arrays,
+        scratch_shapes=slots * 3
+        + [pltpu.SemaphoreType.DMA((count, chips))] * 3
+        + [pltpu.SemaphoreType.DMA((count, chips - 1))] * 2,
+        compiler_params=pltpu.CompilerParams(
+            collective_id=collective_id, has_side_effects=True, vmem_limit_bytes=64000 * 1024
+        ),
+        name=name,
+    )(*parts)
+
+
+def split_ways(parts):
+    pieces, lead = [], 1
+    for i, p in enumerate(parts):
+        _, rows, cols = p.shape
+        tiles = cols // 128
+        if cols % 128 == 0 and tiles > 1:
+            left = (tiles + (1 if lead > 0 else 0)) // 2 * 128
+            if tiles % 2:
+                lead = -lead
+            pieces.append((i, 1, 0, rows, 0, left))
+            pieces.append((i, -1, 0, rows, left, cols - left))
+        elif rows % 32 == 0:
+            pieces.append((i, 1, 0, rows // 2, 0, cols))
+            pieces.append((i, -1, rows // 2, rows // 2, 0, cols))
+        else:
+            pieces.append((i, 1, 0, rows, 0, cols))
+    return tuple(pieces)
+
+
+def sum_over_ctx(parts, pieces, devices, collective_id):
+    if all(p.shape[1] % 8 == 0 for p in parts):
+        return ring_sum(parts, pieces, devices, collective_id)
+    return [
+        lax.psum_scatter(p, "ctx", scatter_dimension=0, tiled=False).astype(F32) for p in parts
+    ]
+
+
 def body(
     tokens,
     block_order,
@@ -356,7 +550,12 @@
     grad_query, grad_pairs = attend_backward(
         query_low, pairs, grad_mixed, mixed, totals, query_pos, key_pos, heads
     )
-    own_grads = lax.psum_scatter(grad_pairs, "ctx", scatter_dimension=0, tiled=False).astype(F32)
+    pair_rows = sequences * rows
+    slots = grad_pairs.reshape(devices, pair_rows, 2 * head_size)
+    share = pair_rows // 8
+    pieces = tuple((0, 1 - 2 * (i % 2), i * share, share, 0, 2 * head_size) for i in range(8))
+    own_grads = sum_over_ctx([slots], pieces, devices, 0)[0]
+    own_grads = own_grads.reshape(sequences, rows, 2 * head_size)
     grad_key_raw, grad_key_gain = key_back(own_grads[..., :head_size])
     value_grad_low = own_grads[..., head_size:].astype(BF16)
     grad_query_raw, grad_query_gain = query_back(
@@ -381,19 +580,6 @@
     part_qkv = weight_grad(
         both(normed_rows, swap(normed_rows)), both(columns(mine), swap(columns(1 - mine)))
     )
-
-    def reduce_rows(part):
-        return lax.psum_scatter(part, "ctx", scatter_dimension=0, tiled=True).astype(F32)
-
-    grad_down_w = reduce_rows(part_down)
-    grad_gate_w = reduce_rows(part_gate)
-    grad_up_w = reduce_rows(part_up)
-    grad_out_w = reduce_rows(part_out)
-    grad_qkv = reduce_rows(part_qkv)
-    query_cols = query_grad_low.shape[1] // 2
-    grad_query_w = grad_qkv[:, :query_cols]
-    grad_key_w = grad_qkv[:, query_cols : query_cols + local_size]
-    grad_value_w = grad_qkv[:, query_cols + local_size :]
 
     gain_grads = [
         grad_attn_pre,
@@ -406,7 +592,21 @@
     packed = jnp.concatenate([g.reshape(devices, 2, -1) for g in gain_grads], -1)
     keep = jnp.where(mine == 0, packed[:, 0], packed[:, 1])
     send = jnp.where(mine == 0, packed[:, 1], packed[:, 0])
-    packed = lax.psum_scatter(keep + swap(send), "ctx", scatter_dimension=0, tiled=False)
+    packed = keep + swap(send)
+    gain_size = packed.shape[-1]
+    packed = jnp.pad(packed, ((0, 0), (0, 1024 - gain_size))).reshape(devices, 8, 128)
+    parts = [
+        p.reshape(devices, p.shape[0] // devices, p.shape[1])
+        for p in (part_down, part_gate, part_up, part_qkv, part_out)
+    ] + [packed]
+    grad_down_w, grad_gate_w, grad_up_w, grad_qkv, grad_out_w, packed = sum_over_ctx(
+        parts, split_ways(parts), devices, 1
+    )
+    packed = packed.reshape(-1)
+    query_cols = query_grad_low.shape[1] // 2
+    grad_query_w = grad_qkv[:, :query_cols]
+    grad_key_w = grad_qkv[:, query_cols : query_cols + local_size]
+    grad_value_w = grad_qkv[:, query_cols + local_size :]
     outs, first = [], 0
     for g in gain_grads:
         size = g.shape[0] // (2 * devices)

time: 725 us -> 458 us (0.63)
  waiting for transfers between devices: 437 us -> 74 us
  Pallas kernels: 15 us -> 183 us
  blocking collectives: 57.7 us -> 0 us
  matrix products: 114 us -> 102 us
  local copies, waits for them, and re-layouts: 26.3 us -> 35.9 us
  other arithmetic: 33.5 us -> 25.8 us
    unnamed x10 -> x1, waiting for transfers between devices: 291 us -> 0.02 us
    pallas_call x0 -> x2, Pallas kernels: none -> 168 us  [ring_sum(): pl.pallas_call(functools.partial(ring_sum_kernel, devices, pieces, arrays...]
    unnamed x1 -> x0, blocking collectives: 57.7 us -> none
    reduce_scatter x3 -> x0, waiting for transfers between devices: 51.9 us -> none  [the longest x1 37.3 us: body(): lax.psum_scatter(grad_pairs, 'ctx', scatter_dimension=0, tiled=False)]
    ppermute x13, waiting for transfers between devices: 79 us -> 59.1 us  [swap(): return lax.ppermute(value, 'wsh', [(0, 1), (1, 0)])]
    dot_general x19, matrix products: 102 us -> 88.8 us  [dot(): lax.dot_general(left, right, (dims, ((), ())), preferred_element_type=F32)]
    convert_element_type x5 -> x0, other arithmetic: 8.75 us -> none  [the longest x4 7.7 us: reduce_rows(): lax.psum_scatter(part, 'ctx', scatter_dimension=0, tiled=True).astype(F32)]
  transfers between devices with their start and end apart: 20 -> 14, of which waited for: 16 -> 7; matrix products, arithmetic and copies ran while one was open for 15% -> 31% of each run, Pallas kernels for 1% -> 10%
where the time goes in v2:
time: 458 us; the launch traced here: 452 us
  Pallas kernels  183 us (40%)
  matrix products  102 us (22%)
  waiting for transfers between devices  74 us (16%)
  local copies, waits for them, and re-layouts  35.9 us (8%)
  other arithmetic  25.8 us (6%)
  between operations  16.6 us (4%)
  starting transfers between devices  13.9 us (3%)
    pallas_call x2, Pallas kernels, ring_sum(): pl.pallas_call(functools.partial(ring_sum_kernel, devices, pieces, arrays...  168 us
    dot_general x19, matrix products, dot(): lax.dot_general(left, right, (dims, ((), ())), preferred_element_type=F32)  88.8 us
    ppermute x13, waiting for transfers between devices, swap(): return lax.ppermute(value, 'wsh', [(0, 1), (1, 0)])  59.1 us
    all_gather x1, waiting for transfers between devices, body(): pairs = lax.all_gather(local_pair, 'ctx', axis=0, tiled=False)  14.9 us
    ppermute x13, starting transfers between devices, swap(): return lax.ppermute(value, 'wsh', [(0, 1), (1, 0)])  13.8 us
    unnamed x126, local copies, waits for them, and re-layouts  9.23 us
  transfers between devices with their start and end apart: 14, of which 7 were waited for; matrix products, arithmetic and copies ran while one was open for 31% of the time, Pallas kernels for 10%

profile of v2, /device:TPU:0, one launch (start us, length us, event | category | flops | bytes accessed | tf_op | source)
XLA Modules:
  0.0 451.7 jit_solution(12197564285592382440)
XLA Ops:
  7.3 4.2 concatenate.176
  11.5 3.0 collective-permute-start
  20.6 9.8 %collective-permute-done.2 = bf16[1152,256]{1,0:T(8,128)(2,1)S(1)} collective-permute-done((bf16[1152,256]{1,0:T(8,128)(2,1)S(1)}, bf16[1152,256]{1,0:T(8,128)(2,1)S(1)}, u32[]{:S(2)}, u32[]{:S(2)}) %collective-permute-start.2) | collective-permute-done | bytes 589856 | tf_op jit(solution)/shard_map/ppermute | solution.py:44
  39.2 24.7 %collective-permute-done.1 = bf16[1152,512]{1,0:T(8,128)(2,1)} collective-permute-done((bf16[1152,512]{1,0:T(8,128)(2,1)}, bf16[1152,512]{1,0:T(8,128)(2,1)}, u32[]{:S(2)}, u32[]{:S(2)}) %collective-permute-start.1) | collective-permute-done | bytes 1179680 | tf_op jit(solution)/shard_map/ppermute | solution.py:44
  63.9 3.5 fusion.25
  70.6 14.9 %all-gather.3.cloned.1.call-done = bf16[32,128,512]{2,1,0:T(8,128)(2,1)} async-done(((bf16[2,128,512]{2,1,0:T(8,128)(2,1)}), bf16[32,128,512]{2,1,0:T(8,128)(2,1)}) %all-gather.3.cloned.1.call-update) | async-done | bytes 4194320 | tf_op jit(solution)/shard_map/all_gather | solution.py:481
  85.5 5.8 %attend_forward.1 = (bf16[2,128,1024]{2,1,0:T(8,128)(2,1)}, f32[2,512,256]{2,1,0:T(8,128)}, f32[2,512,128]{2,1,0:T(8,128)}) custom-call(bf16[2,128,1024]{2,1,0:T(8,128)(2,1)} %convert_element_type.142.q_ref, bf16[16,2,128,512]{3,2,1,0:T(8,128)(2,1)} %bitcast.93, s32[512,1]{1,0:T(8,128)} %copy.65.qpos_ref, s32[2,1024]{1,0:T(2,128)} %pad_add_fusion.2.kpos_ref), custom_call_target="tpu_custom_call" | custom-call | tf_op jit(solution)/shard_map/attend_forward/pallas_call | solution.py:164
  91.3 3.8 multiply_reduce_fusion.6
  98.1 6.0 %fusion.107 = f32[256,3456]{1,0:T(8,128)S(1)} fusion(bf16[256,1152]{1,0:T(8,128)(2,1)S(1)} %bitcast.111, bf16[1152,3456]{1,0:T(8,128)(2,1)} %param.28), kind=kOutput, calls=%fused_computation.221 | convolution fusion | flops 2038431744 | bytes 12091392 | tf_op jit(solution)/shard_map/dot_general | solution.py:61
  104.2 8.4 %collective-permute-done.4 = bf16[256,1152]{1,0:T(8,128)(2,1)S(1)} collective-permute-done((bf16[256,1152]{1,0:T(8,128)(2,1)S(1)}, bf16[256,1152]{1,0:T(8,128)(2,1)S(1)}, u32[]{:S(2)}, u32[]{:S(2)}) %collective-permute-start.4) | collective-permute-done | bytes 589856 | tf_op jit(solution)/shard_map/ppermute | solution.py:44
  112.6 2.5 fusion.108
  115.2 4.4 multiply_convert_fusion.2
  119.6 2.6 convolution_convert_fusion.4
  123.4 4.3 multiply_convert_fusion.3
  127.7 8.9 %collective-permute-done.5 = bf16[256,1152]{1,0:T(8,128)(2,1)S(1)} collective-permute-done((bf16[256,1152]{1,0:T(8,128)(2,1)S(1)}, bf16[256,1152]{1,0:T(8,128)(2,1)S(1)}, u32[]{:S(2)}, u32[]{:S(2)}) %collective-permute-start.5) | collective-permute-done | bytes 589856 | tf_op jit(solution)/shard_map/ppermute | solution.py:44
  136.6 4.2 multiply_reduce_fusion.4
  143.6 7.0 %multiply_convert_fusion.1 = (bf16[256,3456]{1,0:T(8,128)(2,1)}, bf16[256,3456]{1,0:T(8,128)(2,1)}) fusion(f32[256,3456]{1,0:T(8,128)S(1)} %fusion.107, f32[256,3456]{1,0:T(8,128)S(1)} %get-tuple-element.101, bf16[256,1152]{1,0:T(8,128)(2,1)} %bitcast.10, bf16[1152,3456]{1,0:T(8,128)(2,1)S(1)} %bitcast.125), kind=kOutput, calls=%fused_computation.31 | convolution fusion | flops 2059665408 | bytes 19169280 | tf_op jit(solution)/shard_map/dot_general | solution.py:61
  151.3 7.5 %fusion.109 = f32[256,1152]{1,0:T(8,128)} fusion(bf16[256,3456]{1,0:T(8,128)(2,1)} %get-tuple-element.56, bf16[1152,3456]{1,0:T(8,128)(2,1)} %param.28), kind=kOutput, calls=%fused_computation.223 | convolution fusion | flops 2038431744 | bytes 10911744 | tf_op jit(solution)/shard_map/dot_general | solution.py:61
  158.9 8.7 %multiply_convert_fusion = (bf16[256,3456]{1,0:T(8,128)(2,1)S(1)}, bf16[256,3456]{1,0:T(8,128)(2,1)S(1)}) fusion(f32[256,3456]{1,0:T(8,128)S(1)} %copy-done.40, f32[256,3456]{1,0:T(8,128)} %get-tuple-element.103, bf16[256,1152]{1,0:T(8,128)(2,1)} %collective-permute-done.6, bf16[1152,3456]{1,0:T(8,128)(2,1)} %param.30), kind=kOutput, calls=%fused_computation.30 | convolution fusion | flops 2059665408 | bytes 19169280 | tf_op jit(solution)/shard_map/dot_general | solution.py:61
  167.6 2.6 fusion.110
  170.3 2.6 fusion.23
  174.2 8.0 %convolution_convert_fusion.1 = bf16[1152,3456]{1,0:T(8,128)(2,1)} fusion(bf16[256,3456]{1,0:T(8,128)(2,1)} %copy-done.47, bf16[256,3456]{1,0:T(8,128)(2,1)S(1)} %copy-done.46, bf16[256,1152]{1,0:T(8,128)(2,1)S(1)} %copy-done.37, bf16[256,1152]{1,0:T(8,128)(2,1)S(1)} %bitcast.113), kind=kOutput, calls=%fused_computation.1 | convolution fusion | flops 4090281984 | bytes 12681216 | tf_op jit(solution)/shard_map/dot_general | solution.py:61
  182.2 8.2 %convolution_convert_fusion.2 = bf16[1152,3456]{1,0:T(8,128)(2,1)} fusion(bf16[256,3456]{1,0:T(8,128)(2,1)S(1)} %copy-done.43, bf16[256,3456]{1,0:T(8,128)(2,1)S(1)} %copy-done.44, bf16[256,1152]{1,0:T(8,128)(2,1)} %collective-permute-done.6, bf16[256,1152]{1,0:T(8,128)(2,1)} %bitcast.10), kind=kOutput, calls=%fused_computation.2 | convolution fusion | flops 4090281984 | bytes 12681216 | tf_op jit(solution)/shard_map/dot_general | solution.py:61
  190.4 6.7 %convolution_convert_fusion = bf16[1152,3456]{1,0:T(8,128)(2,1)} fusion(bf16[256,3456]{1,0:T(8,128)(2,1)S(1)} %get-tuple-element.53, bf16[256,3456]{1,0:T(8,128)(2,1)S(1)} %copy-done.45, bf16[256,1152]{1,0:T(8,128)(2,1)S(1)} %copy-done.37, bf16[256,1152]{1,0:T(8,128)(2,1)S(1)} %bitcast.114), kind=kOutput, calls=%fused_computation | convolution fusion | flops 4090281984 | bytes 12681216 | tf_op jit(solution)/shard_map/dot_general | solution.py:61
  197.2 2.6 convert_add_fusion.2
  202.6 4.4 fusion.35.g_ref
  207.0 8.8 %attend_backward.1 = (f32[2,128,1024]{2,1,0:T(8,128)}, bf16[16,2,128,512]{3,2,1,0:T(8,128)(2,1)}) custom-call(bf16[2,128,1024]{2,1,0:T(8,128)(2,1)} %convert_element_type.142.q_ref, bf16[16,2,128,512]{3,2,1,0:T(8,128)(2,1)} %bitcast.94, bf16[2,128,1024]{2,1,0:T(8,128)(2,1)} %fusion.35.g_ref, f32[2,512,256]{2,1,0:T(8,128)} %get-tuple-element.27.mix_ref, ...), custom_call_target="tpu_custom_call" | custom-call | tf_op jit(solution)/shard_map/attend_backward/pallas_call | solution.py:190
  215.8 30.6 %ring_sum.2 = f32[256,512]{1,0:T(8,128)} custom-call(bf16[16,256,512]{2,1,0:T(8,128)(2,1)} %bitcast.102), custom_call_target="tpu_custom_call" | custom-call | tf_op jit(solution)/shard_map/ring_sum/pallas_call | solution.py:362
  260.9 3.4 convolution_add_fusion
  280.5 5.4 %collective-permute-done.11 = bf16[256,576]{1,0:T(8,128)(2,1)S(1)} collective-permute-done((bf16[256,576]{1,0:T(8,128)(2,1)S(1)}, bf16[256,576]{1,0:T(8,128)(2,1)S(1)}, u32[]{:S(2)}, u32[]{:S(2)}) %collective-permute-start.11) | collective-permute-done | bytes 294944 | tf_op jit(solution)/shard_map/ppermute | solution.py:44
  291.3 3.8 convolution_convert_fusion.3
  295.1 137.9 %ring_sum.3 = (f32[72,3456]{1,0:T(8,128)}, f32[72,3456]{1,0:T(8,128)}, f32[72,3456]{1,0:T(8,128)}, f32[72,768]{1,0:T(8,128)}, f32[64,576]{1,0:T(8,128)}, /*index=5*/f32[8,128]{1,0:T(8,128)}) custom-call(bf16[16,72,3456]{2,1,0:T(8,128)(2,1)} %bitcast.99, bf16[16,72,3456]{2,1,0:T(8,128)(2,1)} %bitcast.98, bf16[16,72,3456]{2,1,0:T(8,128)(2,1)} %bitcast.100, ...), custom_call_target="tpu_custom_call" | custom-call | tf_op jit(solution)/shard_map/ring_sum/pallas_call | solution.py:362
  (249 shorter events, 76.1 us)
Async XLA Ops:
  7.2 12.2 %copy-start.29 = (bf16[576]{0:T(1024)(128)(2,1)S(1)}, bf16[576]{0:T(1024)(128)(2,1)}, u32[]{:S(2)}) copy-start(bf16[576]{0:T(1024)(128)(2,1)} %param.18) | copy-start | bytes 3460
  7.2 12.4 %copy-start.34 = (bf16[128]{0:T(256)(128)(2,1)S(1)}, bf16[128]{0:T(256)(128)(2,1)}, u32[]{:S(2)}) copy-start(bf16[128]{0:T(256)(128)(2,1)} %param.20) | copy-start | bytes 772
  7.2 12.4 %copy-start.2 = (bf16[2,128,1152]{2,1,0:T(8,128)(2,1)S(1)}, bf16[2,128,1152]{2,1,0:T(8,128)(2,1)}, u32[]{:S(2)}) copy-start(bf16[2,128,1152]{2,1,0:T(8,128)(2,1)} %param.16) | copy-start | bytes 1769476
  7.2 9.8 %copy-start.38 = (s32[16]{0:T(128)S(1)}, s32[16]{0:T(128)}, u32[]{:S(2)}) copy-start(s32[16]{0:T(128)} %param.17) | copy-start | bytes 196
  7.2 78.3 %all-gather.3.cloned.1.call-start = ((), (), s32[]{:S(2)}) async-start(), calls=%async_computation | async-start | bytes 4456448 | tf_op jit(solution)/shard_map/all_gather | solution.py:481
  11.5 7.9 %collective-permute-start = (bf16[2560]{0:T(1024)(128)(2,1)S(1)}, bf16[2560]{0:T(1024)(128)(2,1)S(1)}, u32[]{:S(2)}, u32[]{:S(2)}) collective-permute-start(bf16[2560]{0:T(1024)(128)(2,1)S(1)} %concatenate.176), channel_id=1, source_target_pairs={{0,1},{1,0},{2,3},{3,2},{4,5},{5,4},{6,7},{7,6},{8,9},{9,8},{10,11... | collective-permute-start | bytes 15368 | tf_op jit(solution)/shard_map/ppermute | solution.py:44
  15.6 14.9 %copy-start.10 = (bf16[1152,128]{1,0:T(8,128)(2,1)S(1)}, bf16[1152,128]{1,0:T(8,128)(2,1)}, u32[]{:S(2)}) copy-start(bf16[1152,128]{1,0:T(8,128)(2,1)} %param.25) | copy-start | bytes 884740
  15.6 14.9 %copy-start.11 = (bf16[1152,128]{1,0:T(8,128)(2,1)S(1)}, bf16[1152,128]{1,0:T(8,128)(2,1)}, u32[]{:S(2)}) copy-start(bf16[1152,128]{1,0:T(8,128)(2,1)} %param.26) | copy-start | bytes 884740
  15.6 14.9 %collective-permute-start.2 = (bf16[1152,256]{1,0:T(8,128)(2,1)S(1)}, bf16[1152,256]{1,0:T(8,128)(2,1)S(1)}, u32[]{:S(2)}, u32[]{:S(2)}) collective-permute-start(bf16[1152,256]{1,0:T(8,128)(2,1)S(1)} %pad_maximum_fusion.7), channel_id=1, source_target_pairs={{0,1},{1,0},{2,3},{3,2},{4,5},{5,4},{6,7},{7,6},{8,9},{9,8},{10,11... | collective-permute-start | bytes 1769480 | tf_op jit(solution)/shard_map/ppermute | solution.py:44
  17.0 13.9 %copy-start.27 = (f32[2,128]{1,0:T(2,128)}, f32[2,128]{1,0:T(2,128)S(1)}, u32[]{:S(2)}) copy-start(f32[2,128]{1,0:T(2,128)S(1)} %fusion.45) | copy-start | bytes 3076
  19.3 11.6 %copy-start.24 = (f32[2,128]{1,0:T(2,128)}, f32[2,128]{1,0:T(2,128)S(1)}, u32[]{:S(2)}) copy-start(f32[2,128]{1,0:T(2,128)S(1)} %fusion.83) | copy-start | bytes 3076
  34.7 29.2 %collective-permute-start.1 = (bf16[1152,512]{1,0:T(8,128)(2,1)}, bf16[1152,512]{1,0:T(8,128)(2,1)}, u32[]{:S(2)}, u32[]{:S(2)}) collective-permute-start(bf16[1152,512]{1,0:T(8,128)(2,1)} %param.24), channel_id=1, source_target_pairs={{0,1},{1,0},{2,3},{3,2},{4,5},{5,4},{6,7},{7,6},{8,9},{9,8},{10,11... | collective-permute-start | bytes 3538952 | tf_op jit(solution)/shard_map/ppermute | solution.py:44
  35.0 56.2 %collective-permute-start.3 = (bf16[1024,576]{0,1:T(8,128)(2,1)}, bf16[1024,576]{0,1:T(8,128)(2,1)}, u32[]{:S(2)}, u32[]{:S(2)}) collective-permute-start(bf16[1024,576]{0,1:T(8,128)(2,1)} %param.27), channel_id=1, source_target_pairs={{0,1},{1,0},{2,3},{3,2},{4,5},{5,4},{6,7},{7,6},{8,9},{9,8},{10,11... | collective-permute-start | bytes 3538952 | tf_op jit(solution)/shard_map/ppermute | solution.py:44
  38.7 250.7 %collective-permute-start.8 = (bf16[256,1152]{1,0:T(8,128)(2,1)}, bf16[256,1152]{1,0:T(8,128)(2,1)}, u32[]{:S(2)}, u32[]{:S(2)}) collective-permute-start(bf16[256,1152]{1,0:T(8,128)(2,1)} %bitcast.21), channel_id=1, source_target_pairs={{0,1},{1,0},{2,3},{3,2},{4,5},{5,4},{6,7},{7,6},{8,9},{9,8},{10,11... | collective-permute-start | bytes 1769480 | tf_op jit(solution)/shard_map/ppermute | solution.py:44
  95.5 17.1 %slice-start.2 = ((s8[7962624]{0:T(1024)(128)(4,1)}), s8[3768320]{0:T(1024)(128)(4,1)S(1)}, s32[]{:S(2)}) async-start(s8[7962624]{0:T(1024)(128)(4,1)} %bitcast.126), calls=%async_computation.3 | async-start | bytes 7536640
  96.1 27.3 %copy-start.19 = (bf16[2,128,1152]{2,1,0:T(8,128)(2,1)}, bf16[2,128,1152]{2,1,0:T(8,128)(2,1)S(1)}, u32[]{:S(2)}) copy-start(bf16[2,128,1152]{2,1,0:T(8,128)(2,1)S(1)} %multiply_convert_fusion.4) | copy-start | bytes 1769476
  96.1 16.5 %collective-permute-start.4 = (bf16[256,1152]{1,0:T(8,128)(2,1)S(1)}, bf16[256,1152]{1,0:T(8,128)(2,1)S(1)}, u32[]{:S(2)}, u32[]{:S(2)}) collective-permute-start(bf16[256,1152]{1,0:T(8,128)(2,1)S(1)} %bitcast.110), channel_id=1, source_target_pairs={{0,1},{1,0},{2,3},{3,2},{4,5},{5,4},{6,7},{7,6},{8,9},{9,8},{10,11... | collective-permute-start | bytes 1769480 | tf_op jit(solution)/shard_map/ppermute | solution.py:44
  97.6 15.0 %slice-start.3 = ((s8[7962624]{0:T(1024)(128)(4,1)}), s8[4194304]{0:T(1024)(128)(4,1)S(1)}, s32[]{:S(2)}) async-start(s8[7962624]{0:T(1024)(128)(4,1)} %bitcast.126), calls=%async_computation.4 | async-start | bytes 8388608
  97.6 182.9 %collective-permute-start.10 = (bf16[256,1024]{1,0:T(8,128)(2,1)}, bf16[256,1024]{1,0:T(8,128)(2,1)}, u32[]{:S(2)}, u32[]{:S(2)}) collective-permute-start(bf16[256,1024]{1,0:T(8,128)(2,1)} %bitcast.23), channel_id=1, source_target_pairs={{0,1},{1,0},{2,3},{3,2},{4,5},{5,4},{6,7},{7,6},{8,9},{9,8},{10,11... | collective-permute-start | bytes 1572872 | tf_op jit(solution)/shard_map/ppermute | solution.py:44
  98.1 17.0 %slice-start.6 = ((s8[7962624]{0:T(1024)(128)(4,1)}), s8[4194304]{0:T(1024)(128)(4,1)S(1)}, s32[]{:S(2)}) async-start(s8[7962624]{0:T(1024)(128)(4,1)} %bitcast.130), calls=%async_computation.7 | async-start | bytes 8388608
  104.2 11.0 %slice-start.7 = ((s8[7962624]{0:T(1024)(128)(4,1)}), s8[3768320]{0:T(1024)(128)(4,1)S(1)}, s32[]{:S(2)}) async-start(s8[7962624]{0:T(1024)(128)(4,1)} %bitcast.130), calls=%async_computation.8 | async-start | bytes 7536640
  122.2 14.4 %collective-permute-start.5 = (bf16[256,1152]{1,0:T(8,128)(2,1)S(1)}, bf16[256,1152]{1,0:T(8,128)(2,1)S(1)}, u32[]{:S(2)}, u32[]{:S(2)}) collective-permute-start(bf16[256,1152]{1,0:T(8,128)(2,1)S(1)} %convolution_convert_fusion.4), channel_id=1, source_target_pairs={{0,1},{1,0},{2,3},{3,2},{4,5},{5,4},{6,7},{7,6},{8,9},{9,8},{10,11... | collective-permute-start | bytes 1769480 | tf_op jit(solution)/shard_map/ppermute | solution.py:44
  142.8 16.0 %collective-permute-start.6 = (bf16[256,1152]{1,0:T(8,128)(2,1)}, bf16[256,1152]{1,0:T(8,128)(2,1)}, u32[]{:S(2)}, u32[]{:S(2)}) collective-permute-start(bf16[256,1152]{1,0:T(8,128)(2,1)} %bitcast.10), channel_id=1, source_target_pairs={{0,1},{1,0},{2,3},{3,2},{4,5},{5,4},{6,7},{7,6},{8,9},{9,8},{10,11... | collective-permute-start | bytes 1769480 | tf_op jit(solution)/shard_map/ppermute | solution.py:44
  151.3 16.2 %slice-start.4 = ((s8[7962624]{0:T(1024)(128)(4,1)}), s8[4194304]{0:T(1024)(128)(4,1)S(1)}, s32[]{:S(2)}) async-start(s8[7962624]{0:T(1024)(128)(4,1)} %bitcast.128), calls=%async_computation.5 | async-start | bytes 8388608
  151.3 18.9 %slice-start.8 = ((s8[7962624]{0:T(1024)(128)(4,1)}), s8[4194304]{0:T(1024)(128)(4,1)S(1)}, s32[]{:S(2)}) async-start(s8[7962624]{0:T(1024)(128)(4,1)} %bitcast.132), calls=%async_computation.9 | async-start | bytes 8388608
  158.9 11.3 %slice-start.9 = ((s8[7962624]{0:T(1024)(128)(4,1)}), s8[3768320]{0:T(1024)(128)(4,1)S(1)}, s32[]{:S(2)}) async-start(s8[7962624]{0:T(1024)(128)(4,1)} %bitcast.132), calls=%async_computation.10 | async-start | bytes 7536640
  172.8 24.3 %collective-permute-start.7 = (bf16[256,1152]{1,0:T(8,128)(2,1)S(1)}, bf16[256,1152]{1,0:T(8,128)(2,1)S(1)}, u32[]{:S(2)}, u32[]{:S(2)}) collective-permute-start(bf16[256,1152]{1,0:T(8,128)(2,1)S(1)} %fusion.23), channel_id=1, source_target_pairs={{0,1},{1,0},{2,3},{3,2},{4,5},{5,4},{6,7},{7,6},{8,9},{9,8},{10,11... | collective-permute-start | bytes 1769480 | tf_op jit(solution)/shard_map/ppermute | solution.py:44
  264.3 10.7 %copy-start.9 = (bf16[2,128,1152]{2,1,0:T(8,128)(2,1)S(1)}, bf16[2,128,1152]{2,1,0:T(8,128)(2,1)}, u32[]{:S(2)}) copy-start(bf16[2,128,1152]{2,1,0:T(8,128)(2,1)} %copy-done.8) | copy-start | bytes 1769476
  265.3 13.1 %copy-start.1 = (f32[2,128,1152]{2,1,0:T(8,128)S(1)}, f32[2,128,1152]{2,1,0:T(8,128)}, u32[]{:S(2)}) copy-start(f32[2,128,1152]{2,1,0:T(8,128)} %copy-done) | copy-start | bytes 3538948
  274.1 5.7 %collective-permute-start.12 = (f32[16,160]{1,0:T(8,128)S(1)}, f32[16,160]{1,0:T(8,128)S(1)}, u32[]{:S(2)}, u32[]{:S(2)}) collective-permute-start(f32[16,160]{1,0:T(8,128)S(1)} %bitcast.120), channel_id=1, source_target_pairs={{0,1},{1,0},{2,3},{3,2},{4,5},{5,4},{6,7},{7,6},{8,9},{9,8},{10,11... | collective-permute-start | bytes 30728 | tf_op jit(solution)/shard_map/ppermute | solution.py:44
  275.2 10.6 %collective-permute-start.11 = (bf16[256,576]{1,0:T(8,128)(2,1)S(1)}, bf16[256,576]{1,0:T(8,128)(2,1)S(1)}, u32[]{:S(2)}, u32[]{:S(2)}) collective-permute-start(bf16[256,576]{1,0:T(8,128)(2,1)S(1)} %get-tuple-element.66), channel_id=1, source_target_pairs={{0,1},{1,0},{2,3},{3,2},{4,5},{5,4},{6,7},{7,6},{8,9},{9,8},{10,11... | collective-permute-start | bytes 884744 | tf_op jit(solution)/shard_map/ppermute | solution.py:44
  277.5 13.8 %collective-permute-start.9 = (bf16[256,768]{1,0:T(8,128)(2,1)S(1)}, bf16[256,768]{1,0:T(8,128)(2,1)}, u32[]{:S(2)}, u32[]{:S(2)}) collective-permute-start(bf16[256,768]{1,0:T(8,128)(2,1)S(1)} %pad_maximum_fusion.10), channel_id=1, source_target_pairs={{0,1},{1,0},{2,3},{3,2},{4,5},{5,4},{6,7},{7,6},{8,9},{9,8},{10,11... | collective-permute-start | bytes 1179656 | tf_op jit(solution)/shard_map/ppermute | solution.py:44
  (41 other events, 189.9 us)
Sparse Core Ops, SparseCore 0:
  34.8 50.6 all-gather.2

commit v3 on v2

--- a/solution.py
+++ b/solution.py
@@ -225,11 +225,14 @@
         side = place // (self.chips // 2)
         return 2 * (2 * (place + side * (self.chips - 1 - 2 * place)) + side) + core
 
-    def enter(self):
+    def enter(self, across=False):
         barrier = pltpu.get_barrier_semaphore()
-        for other in (self.left, self.right, self.partner):
-            pl.semaphore_signal(barrier, inc=1, device_id={"ctx": other}, device_id_type=MESH)
-        pl.semaphore_wait(barrier, 3)
+        targets = [{"ctx": other} for other in (self.left, self.right, self.partner)]
+        if across:
+            targets.append({"wsh": 1 - lax.axis_index("wsh")})
+        for target in targets:
+            pl.semaphore_signal(barrier, inc=1, device_id=target, device_id_type=MESH)
+        pl.semaphore_wait(barrier, len(targets))
 
 
 def ring_sum_kernel(devices, pieces, arrays, ahead, *refs):
@@ -399,6 +402,204 @@
     return [
         lax.psum_scatter(p, "ctx", scatter_dimension=0, tiled=False).astype(F32) for p in parts
     ]
+
+
+def front_kernel(
+    devices,
+    tokens_ref,
+    gains_ref,
+    cos_ref,
+    sin_ref,
+    key_weight,
+    value_weight,
+    query_weight,
+    out_weight,
+    pairs_ref,
+    normed_ref,
+    key_ref,
+    all_gains_ref,
+    key_other,
+    value_other,
+    query_other,
+    out_other,
+    gains_other,
+    cross_send,
+    cross_recv,
+    side_send,
+    side_recv,
+    flow_send,
+    flow_recv,
+    twin_send,
+    twin_recv,
+):
+    ring = Ring(devices)
+    chips, far = ring.chips, ring.chips // 2
+    me = lax.axis_index("ctx")
+    mine = lax.axis_index("wsh")
+    sequences, rows, width = tokens_ref.shape
+    count = sequences * rows
+    weights = (
+        (key_weight, key_other),
+        (value_weight, value_other),
+        (query_weight, query_other),
+        (out_weight, out_other),
+    )
+
+    def cross(i):
+        if i == len(weights):
+            source, target = gains_ref, gains_other
+        else:
+            local, other = weights[i]
+            half = local.shape[0] // 2
+            part = pl.ds(pl.multiple_of(ring.core * half, 16), half)
+            source, target = local.at[part], other.at[part]
+        return pltpu.make_async_remote_copy(
+            src_ref=source,
+            dst_ref=target,
+            send_sem=cross_send.at[i],
+            recv_sem=cross_recv.at[i],
+            device_id={"wsh": 1 - mine},
+            device_id_type=MESH,
+        )
+
+    def side(i):
+        other = weights[i][1]
+        half = other.shape[0] // 2
+        part = pl.ds(pl.multiple_of(ring.core * half, 16), half)
+        return pltpu.make_async_remote_copy(
+            src_ref=other.at[part],
+            dst_ref=other.at[part],
+            send_sem=side_send.at[i],
+            recv_sem=side_recv.at[i],
+            device_id={"ctx": ring.partner},
+            device_id_type=MESH,
+        )
+
+    def flow(way, seq, hop):
+        stream = (1 if way < 0 else 0) * sequences + seq
+        place = (ring.place + chips - way * hop) % chips
+        block = pairs_ref.at[ring.device(place, ring.core), seq]
+        return pltpu.make_async_remote_copy(
+            src_ref=block,
+            dst_ref=block,
+            send_sem=flow_send.at[stream, hop],
+            recv_sem=flow_recv.at[stream, hop],
+            device_id={"ctx": ring.right if way > 0 else ring.left},
+            device_id_type=MESH,
+        )
+
+    def twin(way, seq, hop):
+        stream = (1 if way < 0 else 0) * sequences + seq
+        place = (ring.place + chips - way * hop) % chips
+        block = pairs_ref.at[ring.device(place, ring.core), seq]
+        return pltpu.make_async_remote_copy(
+            src_ref=block,
+            dst_ref=block,
+            send_sem=twin_send.at[stream, hop],
+            recv_sem=twin_recv.at[stream, hop],
+            device_id={"ctx": ring.partner},
+            device_id_type=MESH,
+        )
+
+    def hops(way, seq):
+        return far if (seq % 2 == 0) == (way > 0) else far - 1
+
+    ring.enter(across=True)
+    order = (len(weights), 0, 1, 2, 3)
+    for i in order:
+        cross(i).start()
+    inputs = tokens_ref[...].reshape(count, width).astype(F32)
+    scale = lax.rsqrt(jnp.mean(inputs * inputs, -1, keepdims=True) + EPS)
+    cross(len(weights)).wait_recv()
+    all_gains_ref[...] = gains_ref[...] + gains_other[...]
+    normed_ref[...] = (inputs * scale * all_gains_ref[0:1, :]).astype(BF16)
+    for i in (0, 1):
+        cross(i).wait_recv()
+        side(i).start()
+    key_here = dot(normed_ref[...], key_weight[...], ((1,), (0,)))
+    value_here = dot(normed_ref[...], value_weight[...], ((1,), (0,)))
+    for i in (0, 1):
+        side(i).wait_recv()
+    key_there = dot(normed_ref[...], key_other[...], ((1,), (0,)))
+    value_there = dot(normed_ref[...], value_other[...], ((1,), (0,)))
+    lower = mine == 0
+    first = jnp.where(lower, key_here, key_there)
+    second = jnp.where(lower, key_there, key_here)
+    middle = first.shape[1]
+    key_ref[:, :middle] = first
+    key_ref[:, middle:] = second
+    power = jnp.sum(first * first, -1, keepdims=True) + jnp.sum(second * second, -1, keepdims=True)
+    scale = lax.rsqrt(power / (2 * middle) + EPS)
+    gain = all_gains_ref[4:5, 2 * middle : 4 * middle]
+    first = first * scale * gain[:, :middle]
+    second = second * scale * gain[:, middle:]
+    cosine, sine = cos_ref[...], sin_ref[...]
+    value_first = jnp.where(lower, value_here, value_there).astype(BF16)
+    value_second = jnp.where(lower, value_there, value_here).astype(BF16)
+    for seq in range(sequences):
+        span = slice(seq * rows, (seq + 1) * rows)
+        head, tail = first[span], second[span]
+        pairs_ref[me, seq, :, 0 * middle : 1 * middle] = (head * cosine - tail * sine).astype(BF16)
+        pairs_ref[me, seq, :, 1 * middle : 2 * middle] = (tail * cosine + head * sine).astype(BF16)
+        pairs_ref[me, seq, :, 2 * middle : 3 * middle] = value_first[span]
+        pairs_ref[me, seq, :, 3 * middle : 4 * middle] = value_second[span]
+    streams = [(way, seq) for seq in range(sequences) for way in (1, -1)]
+    for hop in range(far + 1):
+        for way, seq in streams:
+            if hop > hops(way, seq):
+                continue
+            if hop > 0:
+                flow(way, seq, hop - 1).wait_recv()
+            if hop < hops(way, seq):
+                flow(way, seq, hop).start()
+            if hop > 0 or way > 0:
+                twin(way, seq, hop).start()
+    for i in (2, 3):
+        cross(i).wait_recv()
+        side(i).start()
+    for hop in range(far + 1):
+        for way, seq in streams:
+            if hop > hops(way, seq):
+                continue
+            if hop > 0 or way > 0:
+                twin(way, seq, hop).wait()
+            if hop < hops(way, seq):
+                flow(way, seq, hop).wait_send()
+    for i in order:
+        cross(i).wait_send()
+    for i in (2, 3):
+        side(i).wait()
+    for i in (0, 1):
+        side(i).wait_send()
+
+
+def front(tokens, gains, cosine, sine, weights, devices, collective_id):
+    sequences, rows, width = tokens.shape
+    size = 2 * cosine.shape[1]
+    far = devices // 4
+    here, there = pl.BlockSpec(memory_space=pltpu.VMEM), pl.BlockSpec(memory_space=pl.ANY)
+    streams = pltpu.SemaphoreType.DMA((2 * sequences, far + 1))
+    like = lambda a: jax.ShapeDtypeStruct(a.shape, a.dtype)
+    return pl.pallas_call(
+        functools.partial(front_kernel, devices),
+        in_specs=[here] * 6 + [there] * 2,
+        out_specs=[here] * 6 + [there] * 2,
+        out_shape=[
+            jax.ShapeDtypeStruct((devices, sequences, rows, 2 * size), BF16),
+            jax.ShapeDtypeStruct((sequences * rows, width), BF16),
+            jax.ShapeDtypeStruct((sequences * rows, size), F32),
+            like(gains),
+        ]
+        + [like(w) for w in weights],
+        scratch_shapes=[pltpu.VMEM(gains.shape, gains.dtype)]
+        + [pltpu.SemaphoreType.DMA((5,))] * 2
+        + [pltpu.SemaphoreType.DMA((4,))] * 2
+        + [streams] * 4,
+        compiler_params=pltpu.CompilerParams(
+            collective_id=collective_id, has_side_effects=True, vmem_limit_bytes=60000 * 1024
+        ),
+        name="front",
+    )(tokens, gains, cosine, sine, *weights)
 
 
 def body(
@@ -426,28 +627,8 @@
     me = lax.axis_index("ctx")
     mine = lax.axis_index("wsh")
 
-    key_value_other = swap(jnp.concatenate([weight_key, weight_value], 1))
-    local_size = weight_key.shape[1]
-    gains = [gain_attn_pre, gain_query, gain_key, gain_attn_post, gain_ff_pre, gain_ff_post]
-    gain_sizes = [g.shape[0] for g in gains]
-    gains_other = swap(jnp.concatenate(gains))
-    starts = [sum(gain_sizes[:i]) for i in range(len(gains))]
-    attn_pre, query_gain, key_gain, attn_post, ff_pre, ff_post = [
-        join_halves(mine, g, gains_other[s : s + n]).astype(F32)
-        for g, s, n in zip(gains, starts, gain_sizes)
-    ]
-    pair_weight = jnp.concatenate(
-        [
-            join_halves(mine, weight_key, key_value_other[:, :local_size]),
-            join_halves(mine, weight_value, key_value_other[:, local_size:]),
-        ],
-        1,
-    )
-    weight_query = join_halves(mine, weight_query, swap(weight_query))
-    weight_out = join_halves(mine, weight_out, swap(weight_out))
-
-    head_size = query_gain.shape[0]
-    heads = weight_query.shape[1] // head_size
+    head_size = 2 * gain_key.shape[0]
+    heads = 2 * weight_query.shape[1] // head_size
 
     lane = jnp.arange(block, dtype=jnp.int32)
     late_order = 2 * devices - 1 - block_order
@@ -460,13 +641,39 @@
     own_pos = jnp.concatenate([own_early, own_late])
     query_pos = jnp.concatenate([jnp.tile(own_early, heads), jnp.tile(own_late, heads)])[:, None]
 
+    cosine, sine = angle_tables(own_pos, head_size)
+
+    def placed(gain):
+        zeros = jnp.zeros_like(gain)
+        return jnp.where(
+            mine == 0, jnp.concatenate([gain, zeros]), jnp.concatenate([zeros, gain])
+        ).astype(F32)
+
+    own_gains = [placed(g) for g in (gain_attn_pre, gain_attn_post, gain_ff_pre, gain_ff_post)]
+    small = [placed(gain_query), placed(gain_key)]
+    own_gains.append(jnp.concatenate(small + [jnp.zeros((width - 2 * head_size,), F32)]))
+    own_gains = jnp.stack(own_gains + [jnp.zeros((width,), F32)] * 3)
+    pairs, normed_low, key_raw, all_gains, key_other, value_other, query_other, out_other = front(
+        tokens,
+        own_gains,
+        cosine,
+        sine,
+        (weight_key, weight_value, weight_query, weight_out),
+        devices,
+        2,
+    )
+    attn_pre, attn_post, ff_pre, ff_post = (all_gains[i] for i in range(4))
+    query_gain = all_gains[4, :head_size]
+    key_gain = all_gains[4, head_size : 2 * head_size]
+    normed_low = normed_low.reshape(sequences, rows, width)
+    key_raw = key_raw.reshape(sequences, rows, head_size)
+    pair_weight = jnp.concatenate(
+        [join_halves(mine, weight_key, key_other), join_halves(mine, weight_value, value_other)], 1
+    )
+    weight_query = join_halves(mine, weight_query, query_other)
+    weight_out = join_halves(mine, weight_out, out_other)
+    local_size = weight_key.shape[1]
     inputs = tokens.astype(F32)
-    normed, pre_back = jax.vjp(norm_gain, inputs, attn_pre)
-    normed_low = normed.astype(BF16)
-    key_value = jnp.einsum("srd,de->sre", normed_low, pair_weight, preferred_element_type=F32)
-    key_raw = key_value[..., :head_size]
-    value_low = key_value[..., head_size:].astype(BF16)
-    cosine, sine = angle_tables(own_pos, head_size)
 
     def key_path(key_in, key_scale):
         return rotate(norm_gain(key_in, key_scale), cosine[None], sine[None])
@@ -476,9 +683,6 @@
             norm_gain(query_in, query_scale), cosine[None, :, None, :], sine[None, :, None, :]
         )
 
-    key_rot, key_back = jax.vjp(key_path, key_raw, key_gain)
-    local_pair = jnp.concatenate([key_rot.astype(BF16), value_low], -1)
-    pairs = lax.all_gather(local_pair, "ctx", axis=0, tiled=False)
     query_raw = jnp.einsum(
         "srd,de->sre", normed_low, weight_query, preferred_element_type=F32
     ).reshape(sequences, rows, heads, head_size)
@@ -556,7 +760,7 @@
     pieces = tuple((0, 1 - 2 * (i % 2), i * share, share, 0, 2 * head_size) for i in range(8))
     own_grads = sum_over_ctx([slots], pieces, devices, 0)[0]
     own_grads = own_grads.reshape(sequences, rows, 2 * head_size)
-    grad_key_raw, grad_key_gain = key_back(own_grads[..., :head_size])
+    grad_key_raw, grad_key_gain = jax.vjp(key_path, key_raw, key_gain)[1](own_grads[..., :head_size])
     value_grad_low = own_grads[..., head_size:].astype(BF16)
     grad_query_raw, grad_query_gain = query_back(
         grad_query.reshape(sequences, rows, heads, head_size)
@@ -568,7 +772,7 @@
         dot(query_grad_low, weight_query, ((1,), (1,)))
         + dot(jnp.concatenate([key_grad_low, value_grad_low], -1), pair_weight, ((1,), (1,)))
     ).reshape(sequences, rows, width)
-    grad_inputs, grad_attn_pre = pre_back(grad_normed)
+    grad_inputs, grad_attn_pre = jax.vjp(norm_gain, inputs, attn_pre)[1](grad_normed)
     grad_tokens = grad_inputs + grad_hidden
 
     def columns(which):

time: 458 us -> 425 us (0.928)
  waiting for transfers between devices: 74 us -> 17.5 us
  Pallas kernels: 183 us -> 230 us
  between operations: 16.6 us -> 3.31 us
  matrix products: 102 us -> 96.1 us
    pallas_call x0 -> x1, Pallas kernels: none -> 47.1 us  [front(): pl.pallas_call(functools.partial(front_kernel, devices), in_specs=[here]...]
    ppermute x13 -> x9, waiting for transfers between devices: 59.1 us -> 17.5 us  [swap(): return lax.ppermute(value, 'wsh', [(0, 1), (1, 0)])]
    all_gather x1 -> x0, waiting for transfers between devices: 14.9 us -> none  [body(): pairs = lax.all_gather(local_pair, 'ctx', axis=0, tiled=False)]
    reshape x6, local copies, waits for them, and re-layouts: 7.06 us -> 1.25 us  [body(): g.reshape(devices, 2, -1)]
    unnamed x126 -> x177, local copies, waits for them, and re-layouts: 9.23 us -> 12.4 us
    ppermute x13 -> x9, starting transfers between devices: 13.8 us -> 10.8 us  [swap(): return lax.ppermute(value, 'wsh', [(0, 1), (1, 0)])]
  transfers between devices with their start and end apart: 14 -> 9, of which waited for: 7 -> 4; matrix products, arithmetic and copies ran while one was open for 31% -> 31% of each run, Pallas kernels for 10% -> 11%
where the time goes in v3:
time: 425 us; the launch traced here: 419 us
  Pallas kernels  230 us (54%)
  matrix products  96.1 us (23%)
  local copies, waits for them, and re-layouts  33.9 us (8%)
  other arithmetic  27.6 us (6%)
  waiting for transfers between devices  17.5 us (4%)
  starting transfers between devices  10.8 us (3%)
    pallas_call x2, Pallas kernels, ring_sum(): pl.pallas_call(functools.partial(ring_sum_kernel, devices, pieces, arrays...  168 us
    dot_general x19, matrix products, dot(): lax.dot_general(left, right, (dims, ((), ())), preferred_element_type=F32)  87.5 us
    pallas_call x1, Pallas kernels, front(): pl.pallas_call(functools.partial(front_kernel, devices), in_specs=[here]...  47.1 us
    ppermute x9, waiting for transfers between devices, swap(): return lax.ppermute(value, 'wsh', [(0, 1), (1, 0)])  17.5 us
    unnamed x177, local copies, waits for them, and re-layouts  12.4 us
    ppermute x9, starting transfers between devices, swap(): return lax.ppermute(value, 'wsh', [(0, 1), (1, 0)])  10.8 us
    pallas_call x1, Pallas kernels, attend_backward(): pl.pallas_call(functools.partial(attend_backward_kernel, heads, min(shard...  8.9 us
  transfers between devices with their start and end apart: 9, of which 4 were waited for; matrix products, arithmetic and copies ran while one was open for 31% of the time, Pallas kernels for 11%

profile of v3, /device:TPU:0, one launch (start us, length us, event | category | flops | bytes accessed | tf_op | source)
XLA Modules:
  0.0 419.0 jit_solution(7085860721491327310)
XLA Ops:
  8.1 2.5 copy.39.out_weight
  12.3 47.1 %front.1 = (bf16[16,2,128,512]{3,2,1,0:T(8,128)(2,1)}, bf16[256,1152]{1,0:T(8,128)(2,1)}, f32[256,256]{1,0:T(8,128)}, f32[8,1152]{1,0:T(8,128)}, bf16[1152,128]{...) custom-call(bf16[2,128,1152]{2,1,0:T(8,128)(2,1)} %tokens_ref.1, ...), custom_call_target="tpu_custom_call" | custom-call | tf_op jit(solution)/shard_map/front/pallas_call | solution.py:583
  63.2 2.4 fusion.67
  65.7 2.5 copy.55
  68.2 2.7 multiply_reduce_fusion.9
  74.8 5.8 %attend_forward.1 = (bf16[2,128,1024]{2,1,0:T(8,128)(2,1)}, f32[2,512,256]{2,1,0:T(8,128)}, f32[2,512,128]{2,1,0:T(8,128)}) custom-call(bf16[2,128,1024]{2,1,0:T(8,128)(2,1)} %bitcast.116, bf16[16,2,128,512]{3,2,1,0:T(8,128)(2,1)} %get-tuple-element.37.kv_ref, s32[512,1]{1,0:T(8,128)} %copy.42.qpos_ref, s32[2,1024]{1,0:T(2,128)} %pad_add_fusion.2.kpos_ref), custom_call_target="tpu_custom_call" | custom-call | tf_op jit(solution)/shard_map/attend_forward/pallas_call | solution.py:164
  80.6 3.6 multiply_reduce_fusion.6
  87.3 5.9 %fusion.95 = f32[256,3456]{1,0:T(8,128)S(1)} fusion(bf16[256,1152]{1,0:T(8,128)(2,1)S(1)} %bitcast.132, bf16[1152,3456]{1,0:T(8,128)(2,1)} %param.28), kind=kOutput, calls=%fused_computation.209 | convolution fusion | flops 2038431744 | bytes 12091392 | tf_op jit(solution)/shard_map/dot_general | solution.py:61
  93.4 5.0 %multiply_convert_fusion.3 = (bf16[256,3456]{1,0:T(8,128)(2,1)}, f32[256,3456]{1,0:T(8,128)}) fusion(f32[256,3456]{1,0:T(8,128)S(1)} %fusion.95, bf16[256,1152]{1,0:T(8,128)(2,1)S(1)} %bitcast.133, bf16[1152,3456]{1,0:T(8,128)(2,1)S(1)} %bitcast.159), kind=kOutput, calls=%fused_computation.33 | convolution fusion | flops 2047279104 | bytes 17399808 | tf_op jit(solution)/shard_map/dot_general | solution.py:61
  98.4 3.0 collective-permute-done
  101.5 2.6 fusion.96
  104.1 4.5 %multiply_convert_fusion.2 = (bf16[256,3456]{1,0:T(8,128)(2,1)S(1)}, f32[256,3456]{1,0:T(8,128)}) fusion(f32[256,3456]{1,0:T(8,128)S(1)} %fusion.96, bf16[256,1152]{1,0:T(8,128)(2,1)S(1)} %collective-permute-done, bf16[1152,3456]{1,0:T(8,128)(2,1)S(1)} %bitcast.159), kind=kOutput, calls=%fused_computation.32 | convolution fusion | flops 2047279104 | bytes 17399808 | tf_op jit(solution)/shard_map/dot_general | solution.py:61
  108.6 3.8 convolution_convert_fusion.4
  116.7 9.6 %collective-permute-done.1 = bf16[256,1152]{1,0:T(8,128)(2,1)} collective-permute-done((bf16[256,1152]{1,0:T(8,128)(2,1)}, bf16[256,1152]{1,0:T(8,128)(2,1)}, u32[]{:S(2)}, u32[]{:S(2)}) %collective-permute-start.1) | collective-permute-done | bytes 589856 | tf_op jit(solution)/shard_map/ppermute | solution.py:44
  126.4 6.2 %multiply_reduce_fusion.4 = (f32[256]{0:T(256)S(1)}, f32[256,1152]{1,0:T(8,128)S(1)}) fusion(bf16[256,1152]{1,0:T(8,128)(2,1)} %collective-permute-done.1, bf16[256,3456]{1,0:T(8,128)(2,1)S(1)} %copy-done.64, bf16[1152,3456]{1,0:T(8,128)(2,1)} %param.30), kind=kOutput, calls=%fused_computation.90 | convolution fusion | flops 2039611136 | bytes 11502592 | tf_op jit(solution)/shard_map/dot_general | solution.py:61
  136.1 5.9 %multiply_convert_fusion.1 = (bf16[256,3456]{1,0:T(8,128)(2,1)}, bf16[256,3456]{1,0:T(8,128)(2,1)}) fusion(f32[256,3456]{1,0:T(8,128)S(1)} %copy-done.62, f32[256,3456]{1,0:T(8,128)S(1)} %copy-done.63, bf16[256,1152]{1,0:T(8,128)(2,1)S(1)} %bitcast.129, bf16[1152,3456]{1,0:T(8,128)(2,1)S(1)} %bitcast.153), kind=kOutput, calls=%fused_computation.31 | convolution fusion | flops 2059665408 | bytes 19169280 | tf_op jit(solution)/shard_map/dot_general | solution.py:61
  142.7 7.5 %fusion.97 = f32[256,1152]{1,0:T(8,128)} fusion(bf16[256,3456]{1,0:T(8,128)(2,1)} %get-tuple-element.76, bf16[1152,3456]{1,0:T(8,128)(2,1)} %param.28), kind=kOutput, calls=%fused_computation.211 | convolution fusion | flops 2038431744 | bytes 10911744 | tf_op jit(solution)/shard_map/dot_general | solution.py:61
  150.3 8.7 %multiply_convert_fusion = (bf16[256,3456]{1,0:T(8,128)(2,1)S(1)}, bf16[256,3456]{1,0:T(8,128)(2,1)S(1)}) fusion(f32[256,3456]{1,0:T(8,128)S(1)} %copy-done.60, f32[256,3456]{1,0:T(8,128)} %get-tuple-element.120, bf16[256,1152]{1,0:T(8,128)(2,1)} %collective-permute-done.2, bf16[1152,3456]{1,0:T(8,128)(2,1)} %param.30), kind=kOutput, calls=%fused_computation.30 | convolution fusion | flops 2059665408 | bytes 19169280 | tf_op jit(solution)/shard_map/dot_general | solution.py:61
  159.0 2.6 fusion.98
  161.6 2.6 fusion.23
  165.8 8.0 %convolution_convert_fusion.1 = bf16[1152,3456]{1,0:T(8,128)(2,1)} fusion(bf16[256,3456]{1,0:T(8,128)(2,1)} %copy-done.70, bf16[256,3456]{1,0:T(8,128)(2,1)S(1)} %copy-done.69, bf16[256,1152]{1,0:T(8,128)(2,1)S(1)} %copy-done.57, bf16[256,1152]{1,0:T(8,128)(2,1)S(1)} %bitcast.134), kind=kOutput, calls=%fused_computation.1 | convolution fusion | flops 4090281984 | bytes 12681216 | tf_op jit(solution)/shard_map/dot_general | solution.py:61
  173.8 8.0 %convolution_convert_fusion.2 = bf16[1152,3456]{1,0:T(8,128)(2,1)} fusion(bf16[256,3456]{1,0:T(8,128)(2,1)S(1)} %copy-done.67, bf16[256,3456]{1,0:T(8,128)(2,1)S(1)} %copy-done.65, bf16[256,1152]{1,0:T(8,128)(2,1)} %collective-permute-done.2, bf16[256,1152]{1,0:T(8,128)(2,1)S(1)} %bitcast.130), kind=kOutput, calls=%fused_computation.2 | convolution fusion | flops 4090281984 | bytes 12681216 | tf_op jit(solution)/shard_map/dot_general | solution.py:61
  181.8 6.7 %convolution_convert_fusion = bf16[1152,3456]{1,0:T(8,128)(2,1)} fusion(bf16[256,3456]{1,0:T(8,128)(2,1)S(1)} %get-tuple-element.73, bf16[256,3456]{1,0:T(8,128)(2,1)S(1)} %copy-done.68, bf16[256,1152]{1,0:T(8,128)(2,1)S(1)} %copy-done.57, bf16[256,1152]{1,0:T(8,128)(2,1)S(1)} %bitcast.135), kind=kOutput, calls=%fused_computation | convolution fusion | flops 4090281984 | bytes 12681216 | tf_op jit(solution)/shard_map/dot_general | solution.py:61
  188.5 2.6 convert_add_fusion.2
  195.0 2.4 fusion.31.g_ref
  197.3 8.9 %attend_backward.1 = (f32[2,128,1024]{2,1,0:T(8,128)}, bf16[16,2,128,512]{3,2,1,0:T(8,128)(2,1)}) custom-call(bf16[2,128,1024]{2,1,0:T(8,128)(2,1)} %bitcast.117, bf16[16,2,128,512]{3,2,1,0:T(8,128)(2,1)} %get-tuple-element.37.kv_ref, bf16[2,128,1024]{2,1,0:T(8,128)(2,1)} %fusion.31.g_ref, f32[2,512,256]{2,1,0:T(8,128)} %get-tuple-element.40.mix_ref, ...), custom_call_target="tpu_custom_call" | custom-call | tf_op jit(solution)/shard_map/attend_backward/pallas_call | solution.py:190
  206.2 29.8 %ring_sum.2 = f32[256,512]{1,0:T(8,128)} custom-call(bf16[16,256,512]{2,1,0:T(8,128)(2,1)} %bitcast.119), custom_call_target="tpu_custom_call" | custom-call | tf_op jit(solution)/shard_map/ring_sum/pallas_call | solution.py:365
  257.0 3.6 collective-permute-done.7
  260.6 2.0 convolution_convert_fusion.5
  265.4 3.6 convolution_convert_fusion.3
  269.0 138.2 %ring_sum.3 = (f32[72,3456]{1,0:T(8,128)}, f32[72,3456]{1,0:T(8,128)}, f32[72,3456]{1,0:T(8,128)}, f32[72,768]{1,0:T(8,128)}, f32[64,576]{1,0:T(8,128)}, /*index=5*/f32[8,128]{1,0:T(8,128)}) custom-call(bf16[16,72,3456]{2,1,0:T(8,128)(2,1)} %bitcast.113, bf16[16,72,3456]{2,1,0:T(8,128)(2,1)} %bitcast.112, bf16[16,72,3456]{2,1,0:T(8,128)(2,1)} %bitcast.114, ...), custom_call_target="tpu_custom_call" | custom-call | tf_op jit(solution)/shard_map/ring_sum/pallas_call | solution.py:365
  414.6 2.2 copy.80
  (290 shorter events, 65.4 us)
Async XLA Ops:
  10.6 49.2 %copy-start.58 = (s32[16]{0:T(128)S(1)}, s32[16]{0:T(128)}, u32[]{:S(2)}) copy-start(s32[16]{0:T(128)} %param.17) | copy-start | bytes 196
  10.6 52.7 %copy-start.9 = (bf16[1152,512]{1,0:T(8,128)(2,1)S(1)}, bf16[1152,512]{1,0:T(8,128)(2,1)}, u32[]{:S(2)}) copy-start(bf16[1152,512]{1,0:T(8,128)(2,1)} %query_weight.1) | copy-start | bytes 3538948
  59.4 204.6 %collective-permute-start.4 = (bf16[256,1152]{1,0:T(8,128)(2,1)}, bf16[256,1152]{1,0:T(8,128)(2,1)}, u32[]{:S(2)}, u32[]{:S(2)}) collective-permute-start(bf16[256,1152]{1,0:T(8,128)(2,1)} %get-tuple-element.34), channel_id=1, source_target_pairs={{0,1},{1,0},{2,3},{3,2},{4,5},{5,4},{6,7},{7,6},{8,9},{9,8},{10,11... | collective-permute-start | bytes 1769480 | tf_op jit(solution)/shard_map/ppermute | solution.py:44
  61.6 9.3 %copy-start.38 = (f32[1,256]{1,0:T(1,128)}, f32[1,256]{1,0:T(1,128)S(1)}, u32[]{:S(2)}) copy-start(f32[1,256]{1,0:T(1,128)S(1)} %get-tuple-element.99) | copy-start | bytes 3076
  63.2 21.0 %copy-start.26 = (f32[1152]{0:T(1024)}, f32[1152]{0:T(1024)S(1)}, u32[]{:S(2)}) copy-start(f32[1152]{0:T(1024)S(1)} %get-tuple-element.68) | copy-start | bytes 13828
  84.7 30.0 %copy-start.45 = (f32[2,128]{1,0:T(2,128)}, f32[2,128]{1,0:T(2,128)S(1)}, u32[]{:S(2)}) copy-start(f32[2,128]{1,0:T(2,128)S(1)} %get-tuple-element.89) | copy-start | bytes 3076
  84.9 8.4 %slice-start.8 = ((s8[7962624]{0:T(1024)(128)(4,1)}), s8[4194304]{0:T(1024)(128)(4,1)S(1)}, s32[]{:S(2)}) async-start(s8[7962624]{0:T(1024)(128)(4,1)} %bitcast.158), calls=%async_computation.8 | async-start | bytes 8388608
  85.2 16.2 %collective-permute-start = (bf16[256,1152]{1,0:T(8,128)(2,1)S(1)}, bf16[256,1152]{1,0:T(8,128)(2,1)S(1)}, u32[]{:S(2)}, u32[]{:S(2)}) collective-permute-start(bf16[256,1152]{1,0:T(8,128)(2,1)S(1)} %bitcast.131), channel_id=1, source_target_pairs={{0,1},{1,0},{2,3},{3,2},{4,5},{5,4},{6,7},{7,6},{8,9},{9,8},{10,11... | collective-permute-start | bytes 1769480 | tf_op jit(solution)/shard_map/ppermute | solution.py:44
  87.0 170.0 %collective-permute-start.6 = (bf16[256,1024]{1,0:T(8,128)(2,1)}, bf16[256,1024]{1,0:T(8,128)(2,1)}, u32[]{:S(2)}, u32[]{:S(2)}) collective-permute-start(bf16[256,1024]{1,0:T(8,128)(2,1)} %bitcast.28), channel_id=1, source_target_pairs={{0,1},{1,0},{2,3},{3,2},{4,5},{5,4},{6,7},{7,6},{8,9},{9,8},{10,11... | collective-permute-start | bytes 1572872 | tf_op jit(solution)/shard_map/ppermute | solution.py:44
  87.3 14.2 %slice-start.4 = ((s8[7962624]{0:T(1024)(128)(4,1)}), s8[4194304]{0:T(1024)(128)(4,1)S(1)}, s32[]{:S(2)}) async-start(s8[7962624]{0:T(1024)(128)(4,1)} %bitcast.154), calls=%async_computation.4 | async-start | bytes 8388608
  93.4 20.8 %copy-start.46 = (f32[256]{0:T(256)}, f32[256]{0:T(256)S(1)}, u32[]{:S(2)}) copy-start(f32[256]{0:T(256)S(1)} %multiply_reduce_fusion.12) | copy-start | bytes 3076
  93.4 8.1 %slice-start.5 = ((s8[7962624]{0:T(1024)(128)(4,1)}), s8[3768320]{0:T(1024)(128)(4,1)S(1)}, s32[]{:S(2)}) async-start(s8[7962624]{0:T(1024)(128)(4,1)} %bitcast.154), calls=%async_computation.5 | async-start | bytes 7536640
  101.5 7.1 %slice-start = ((s8[7962624]{0:T(1024)(128)(4,1)}), s8[4194304]{0:T(1024)(128)(4,1)S(1)}, s32[]{:S(2)}) async-start(s8[7962624]{0:T(1024)(128)(4,1)} %bitcast.150), calls=%async_computation | async-start | bytes 8388608
  112.4 13.9 %collective-permute-start.1 = (bf16[256,1152]{1,0:T(8,128)(2,1)}, bf16[256,1152]{1,0:T(8,128)(2,1)}, u32[]{:S(2)}, u32[]{:S(2)}) collective-permute-start(bf16[256,1152]{1,0:T(8,128)(2,1)} %convolution_convert_fusion.4), channel_id=1, source_target_pairs={{0,1},{1,0},{2,3},{3,2},{4,5},{5,4},{6,7},{7,6},{8,9},{9,8},{10,11... | collective-permute-start | bytes 1769480 | tf_op jit(solution)/shard_map/ppermute | solution.py:44
  114.7 11.6 %copy-start.64 = (bf16[256,3456]{1,0:T(8,128)(2,1)S(1)}, bf16[256,3456]{1,0:T(8,128)(2,1)}, u32[]{:S(2)}) copy-start(bf16[256,3456]{1,0:T(8,128)(2,1)} %get-tuple-element.117) | copy-start | bytes 5308420
  115.3 20.8 %slice-start.2 = ((s8[7962624]{0:T(1024)(128)(4,1)}), s8[4194304]{0:T(1024)(128)(4,1)S(1)}, s32[]{:S(2)}) async-start(s8[7962624]{0:T(1024)(128)(4,1)} %bitcast.152), calls=%async_computation.2 | async-start | bytes 8388608
  126.4 9.7 %slice-start.3 = ((s8[7962624]{0:T(1024)(128)(4,1)}), s8[3768320]{0:T(1024)(128)(4,1)S(1)}, s32[]{:S(2)}) async-start(s8[7962624]{0:T(1024)(128)(4,1)} %bitcast.152), calls=%async_computation.3 | async-start | bytes 7536640
  134.4 15.9 %collective-permute-start.2 = (bf16[256,1152]{1,0:T(8,128)(2,1)S(1)}, bf16[256,1152]{1,0:T(8,128)(2,1)}, u32[]{:S(2)}, u32[]{:S(2)}) collective-permute-start(bf16[256,1152]{1,0:T(8,128)(2,1)S(1)} %bitcast.128), channel_id=1, source_target_pairs={{0,1},{1,0},{2,3},{3,2},{4,5},{5,4},{6,7},{7,6},{8,9},{9,8},{10,11... | collective-permute-start | bytes 1769480 | tf_op jit(solution)/shard_map/ppermute | solution.py:44
  142.7 7.5 %copy-start.60 = (f32[256,3456]{1,0:T(8,128)S(1)}, f32[256,3456]{1,0:T(8,128)}, u32[]{:S(2)}) copy-start(f32[256,3456]{1,0:T(8,128)} %copy-done.59) | copy-start | bytes 10616836
  142.7 16.2 %slice-start.6 = ((s8[7962624]{0:T(1024)(128)(4,1)}), s8[4194304]{0:T(1024)(128)(4,1)S(1)}, s32[]{:S(2)}) async-start(s8[7962624]{0:T(1024)(128)(4,1)} %bitcast.156), calls=%async_computation.6 | async-start | bytes 8388608
  142.7 18.8 %slice-start.10 = ((s8[7962624]{0:T(1024)(128)(4,1)}), s8[4194304]{0:T(1024)(128)(4,1)S(1)}, s32[]{:S(2)}) async-start(s8[7962624]{0:T(1024)(128)(4,1)} %bitcast.160), calls=%async_computation.10 | async-start | bytes 8388608
  150.3 8.7 %slice-start.7 = ((s8[7962624]{0:T(1024)(128)(4,1)}), s8[3768320]{0:T(1024)(128)(4,1)S(1)}, s32[]{:S(2)}) async-start(s8[7962624]{0:T(1024)(128)(4,1)} %bitcast.156), calls=%async_computation.7 | async-start | bytes 7536640
  150.3 11.3 %slice-start.11 = ((s8[7962624]{0:T(1024)(128)(4,1)}), s8[3768320]{0:T(1024)(128)(4,1)S(1)}, s32[]{:S(2)}) async-start(s8[7962624]{0:T(1024)(128)(4,1)} %bitcast.160), calls=%async_computation.11 | async-start | bytes 7536640
  164.2 9.6 %copy-start.65 = (bf16[256,3456]{1,0:T(8,128)(2,1)S(1)}, bf16[256,3456]{1,0:T(8,128)(2,1)}, u32[]{:S(2)}) copy-start(bf16[256,3456]{1,0:T(8,128)(2,1)} %get-tuple-element.117) | copy-start | bytes 5308420
  164.2 9.6 %copy-start.67 = (bf16[256,3456]{1,0:T(8,128)(2,1)S(1)}, bf16[256,3456]{1,0:T(8,128)(2,1)}, u32[]{:S(2)}) copy-start(bf16[256,3456]{1,0:T(8,128)(2,1)} %copy-done.66) | copy-start | bytes 5308420
  164.2 24.3 %collective-permute-start.3 = (bf16[256,1152]{1,0:T(8,128)(2,1)S(1)}, bf16[256,1152]{1,0:T(8,128)(2,1)S(1)}, u32[]{:S(2)}, u32[]{:S(2)}) collective-permute-start(bf16[256,1152]{1,0:T(8,128)(2,1)S(1)} %fusion.23), channel_id=1, source_target_pairs={{0,1},{1,0},{2,3},{3,2},{4,5},{5,4},{6,7},{7,6},{8,9},{9,8},{10,11... | collective-permute-start | bytes 1769480 | tf_op jit(solution)/shard_map/ppermute | solution.py:44
  173.8 8.0 %copy-start.68 = (bf16[256,3456]{1,0:T(8,128)(2,1)S(1)}, bf16[256,3456]{1,0:T(8,128)(2,1)}, u32[]{:S(2)}) copy-start(bf16[256,3456]{1,0:T(8,128)(2,1)} %get-tuple-element.75) | copy-start | bytes 5308420
  247.4 8.9 %collective-permute-start.8 = (f32[16,160]{1,0:T(8,128)S(1)}, f32[16,160]{1,0:T(8,128)S(1)}, u32[]{:S(2)}, u32[]{:S(2)}) collective-permute-start(f32[16,160]{1,0:T(8,128)S(1)} %bitcast.144), channel_id=1, source_target_pairs={{0,1},{1,0},{2,3},{3,2},{4,5},{5,4},{6,7},{7,6},{8,9},{9,8},{10,11... | collective-permute-start | bytes 30728 | tf_op jit(solution)/shard_map/ppermute | solution.py:44
  249.9 10.6 %collective-permute-start.7 = (bf16[256,576]{1,0:T(8,128)(2,1)S(1)}, bf16[256,576]{1,0:T(8,128)(2,1)S(1)}, u32[]{:S(2)}, u32[]{:S(2)}) collective-permute-start(bf16[256,576]{1,0:T(8,128)(2,1)S(1)} %get-tuple-element.88), channel_id=1, source_target_pairs={{0,1},{1,0},{2,3},{3,2},{4,5},{5,4},{6,7},{7,6},{8,9},{9,8},{10,11... | collective-permute-start | bytes 884744 | tf_op jit(solution)/shard_map/ppermute | solution.py:44
  252.5 12.9 %collective-permute-start.5 = (bf16[256,768]{1,0:T(8,128)(2,1)}, bf16[256,768]{1,0:T(8,128)(2,1)}, u32[]{:S(2)}, u32[]{:S(2)}) collective-permute-start(bf16[256,768]{1,0:T(8,128)(2,1)} %pad_maximum_fusion.3), channel_id=1, source_target_pairs={{0,1},{1,0},{2,3},{3,2},{4,5},{5,4},{6,7},{7,6},{8,9},{9,8},{10,11... | collective-permute-start | bytes 1179656 | tf_op jit(solution)/shard_map/ppermute | solution.py:44
  407.1 9.7 %copy-start.20 = (f32[72,3456]{1,0:T(8,128)S(1)}, f32[72,3456]{1,0:T(8,128)}, u32[]{:S(2)}) copy-start(f32[72,3456]{1,0:T(8,128)} %get-tuple-element.153) | copy-start | bytes 2985988
  407.1 10.7 %copy-start.19 = (f32[72,3456]{1,0:T(8,128)S(1)}, f32[72,3456]{1,0:T(8,128)}, u32[]{:S(2)}) copy-start(f32[72,3456]{1,0:T(8,128)} %get-tuple-element.154) | copy-start | bytes 2985988
  (61 other events, 181.6 us)

commit v4 on v3

--- a/solution.py
+++ b/solution.py
@@ -602,6 +602,513 @@
     )(tokens, gains, cosine, sine, *weights)
 
 
+class RingSum:
+    def __init__(self, ring, pieces, parts, own, other, flow, outs, sems):
+        self.ring, self.pieces, self.parts, self.own = ring, pieces, parts, own
+        self.other, self.flow, self.outs = other, flow, outs
+        self.put_sem, self.got_sem, self.send_sem, self.recv_sem = sems[:4]
+        self.own_sem = sems[4] if own is not None else None
+        self.last = ring.chips - 1
+
+    def region(self, p):
+        array, _, first, rows, start, cols = self.pieces[p]
+        return array, pl.ds(first, rows), pl.ds(start, cols)
+
+    def owner(self, p, step, core):
+        way = self.pieces[p][1]
+        chips = self.ring.chips
+        return self.ring.device((self.ring.place + 2 * chips + way * (-1 - step)) % chips, core)
+
+    def load(self, p, step):
+        array, rows, cols = self.region(p)
+        slot = step % self.own[array].shape[0]
+        return pltpu.make_async_copy(
+            self.parts[array].at[self.owner(p, step, self.ring.core), rows, cols],
+            self.own[array].at[slot, rows, cols],
+            self.own_sem.at[p, step],
+        )
+
+    def give(self, p, step):
+        array, rows, cols = self.region(p)
+        return pltpu.make_async_remote_copy(
+            src_ref=self.parts[array].at[self.owner(p, step, 1 - self.ring.core), rows, cols],
+            dst_ref=self.other[array].at[step, rows, cols],
+            send_sem=self.put_sem.at[p, step],
+            recv_sem=self.got_sem.at[p, step],
+            device_id={"ctx": self.ring.partner},
+            device_id_type=MESH,
+        )
+
+    def hop(self, p, step):
+        array, rows, cols = self.region(p)
+        way = self.pieces[p][1]
+        return pltpu.make_async_remote_copy(
+            src_ref=self.flow[array].at[step, rows, cols],
+            dst_ref=self.flow[array].at[step + 1, rows, cols],
+            send_sem=self.send_sem.at[p, step],
+            recv_sem=self.recv_sem.at[p, step],
+            device_id={"ctx": self.ring.right if way > 0 else self.ring.left},
+            device_id_type=MESH,
+        )
+
+    def load_all(self, step):
+        for p in range(len(self.pieces)):
+            self.load(p, step).start()
+
+    def give_all(self, step):
+        for p in range(len(self.pieces)):
+            self.give(p, step).start()
+
+    def work(self, p, step):
+        array, _, row, rows, start, cols = self.pieces[p]
+        if self.own is not None:
+            self.load(p, step).wait()
+            mine, at_mine = self.own[array], step % self.own[array].shape[0]
+        else:
+            mine, at_mine = self.parts[array], self.owner(p, step, self.ring.core)
+        self.give(p, step).wait_recv()
+        if step > 0:
+            self.hop(p, step - 1).wait_recv()
+        width = 128 if cols % 128 == 0 else cols
+        while width < 512 and cols % (2 * width) == 0:
+            width *= 2
+        rows = pl.ds(row, rows)
+
+        def group(i, carry):
+            at = start + i * width
+            if cols > width:
+                at = pl.multiple_of(at, 128)
+            where = pl.ds(at, width)
+            total = mine[at_mine, rows, where].astype(F32)
+            total += self.other[array][step, rows, where].astype(F32)
+            if step > 0:
+                total += self.flow[array][step, rows, where].astype(F32)
+            if step == self.last:
+                self.outs[array][rows, where] = total.astype(self.outs[array].dtype)
+            else:
+                self.flow[array][step, rows, where] = total.astype(self.flow[array].dtype)
+            return carry
+
+        if cols == width:
+            group(0, 0)
+        else:
+            lax.fori_loop(0, cols // width, group, 0)
+        if step < self.last:
+            self.hop(p, step).start()
+
+    def drain(self):
+        for p in range(len(self.pieces)):
+            for step in range(self.last + 1):
+                self.give(p, step).wait_send()
+                if step < self.last:
+                    self.hop(p, step).wait_send()
+
+
+def norm_back(upstream, vector, gain):
+    scale = lax.rsqrt(jnp.mean(vector * vector, -1, keepdims=True) + EPS)
+    normal = vector * scale
+    weighted = upstream * gain
+    back = scale * (weighted - normal * jnp.mean(weighted * normal, -1, keepdims=True))
+    return back, jnp.sum(upstream * normal, 0, keepdims=True)
+
+
+def turn_back(upstream, cosine, sine):
+    middle = upstream.shape[-1] // 2
+    first, second = upstream[:, :middle], upstream[:, middle:]
+    return jnp.concatenate([first * cosine + second * sine, second * cosine - first * sine], -1)
+
+
+def back_kernel(devices, heads, ff_pieces, kv_pieces, attn_pieces, names, *refs):
+    r = dict(zip(names, refs))
+    ring = Ring(devices)
+    chips = ring.chips
+    mine = lax.axis_index("wsh")
+    sequences, rows, _ = r["query"].shape
+    size = r["key_raw"].shape[1]
+    count = sequences * rows
+    block = rows // 2
+    stacked = heads * block
+
+    ff = RingSum(
+        ring,
+        ff_pieces,
+        [r["part_down"], r["part_gate"], r["part_up"]],
+        [r[f"ff_own{i}"] for i in range(3)],
+        [r[f"ff_other{i}"] for i in range(3)],
+        [r[f"ff_flow{i}"] for i in range(3)],
+        [r["grad_down"], r["grad_gate"], r["grad_up"]],
+        [r["ff_put"], r["ff_got"], r["ff_send"], r["ff_recv"], r["ff_load"]],
+    )
+    kv = RingSum(
+        ring,
+        kv_pieces,
+        [r["pairs"]],
+        None,
+        [r["kv_other"]],
+        [r["kv_flow"]],
+        [r["kv_sum"]],
+        [r["kv_put"], r["kv_got"], r["kv_send"], r["kv_recv"]],
+    )
+    attn = RingSum(
+        ring,
+        attn_pieces,
+        [r["qkv_part"], r["out_part"]],
+        None,
+        [r["qkv_other"], r["out_other"]],
+        [r["qkv_flow"], r["out_flow"]],
+        [r["grad_qkv"], r["grad_out"]],
+        [r["at_put"], r["at_got"], r["at_send"], r["at_recv"]],
+    )
+
+    def brought(i):
+        name = BROUGHT[i]
+        return pltpu.make_async_copy(r["in_" + name], r[name], r["bring"].at[i])
+
+    def need(*wanted):
+        for name in wanted:
+            brought(BROUGHT.index(name)).wait()
+
+    def across(i, source, target):
+        return pltpu.make_async_remote_copy(
+            src_ref=source,
+            dst_ref=target,
+            send_sem=r["cross_send"].at[i],
+            recv_sem=r["cross_recv"].at[i],
+            device_id={"wsh": 1 - mine},
+            device_id_type=MESH,
+        )
+
+    out_swap = across(0, r["att_send"], r["att_across"])
+    col_swap = across(1, r["col_send"], r["col_rows"].at[pl.ds(count, count)])
+    gain_swap = across(2, r["gain_own"], r["gain_across"])
+    gain_twin = pltpu.make_async_remote_copy(
+        src_ref=r["gain_pair"],
+        dst_ref=r["gain_twin"],
+        send_sem=r["twin_send"].at[0],
+        recv_sem=r["twin_recv"].at[0],
+        device_id={"ctx": ring.partner},
+        device_id_type=MESH,
+    )
+
+    def gain_hop(way, step):
+        return pltpu.make_async_remote_copy(
+            src_ref=r["gain_flow"].at[way, step],
+            dst_ref=r["gain_flow"].at[way, step + 1],
+            send_sem=r["gain_send"].at[way, step],
+            recv_sem=r["gain_recv"].at[way, step],
+            device_id={"ctx": ring.right if way == 0 else ring.left},
+            device_id_type=MESH,
+        )
+
+    gain_hops = (chips // 2, chips - 1 - chips // 2)
+
+    def attention(seq):
+        queries, scaled, correction = [], [], []
+        for half in range(2):
+            span = slice(half * stacked, (half + 1) * stacked)
+            lines = slice(half * block, (half + 1) * block)
+            cut = lambda ref: jnp.concatenate(
+                [ref[seq, lines, h * size : (h + 1) * size] for h in range(heads)], 0
+            )
+            queries.append(cut(r["query"]))
+            grad = cut(r["grad_mixed"]).astype(F32)
+            total = r["totals"][seq, span, :1]
+            delta = jnp.sum(grad * r["mixed"][seq, span, :], -1, keepdims=True)
+            scaled.append((grad / total).astype(BF16))
+            correction.append(delta / total)
+        grad_query = [jnp.zeros((stacked, size), F32) for _ in range(2)]
+        for key_half in range(2):
+            lines = pl.ds(seq * rows + key_half * block, block)
+            part = r["pairs"][:, lines, :].reshape(devices * block, 2 * size)
+            keys, values = part[:, :size], part[:, size:]
+            grad_keys = jnp.zeros((devices * block, size), F32)
+            grad_values = jnp.zeros((devices * block, size), F32)
+            for half in range(key_half, 2):
+                weights = jnp.exp(dot(queries[half], keys, ((1,), (1,))) * SCORE_SCALE)
+                if half == key_half:
+                    allowed = (
+                        r["key_pos"][key_half : key_half + 1, :]
+                        <= r["query_pos"][half * stacked : (half + 1) * stacked, :]
+                    )
+                    weights = jnp.where(allowed, weights, 0.0)
+                low = weights.astype(BF16)
+                grad_weights = dot(scaled[half], values, ((1,), (1,)))
+                grad_scores = (weights * (grad_weights - correction[half])).astype(BF16)
+                grad_query[half] += dot(grad_scores, keys, ((1,), (0,)))
+                grad_keys += dot(grad_scores, queries[half], ((0,), (0,)))
+                grad_values += dot(low, scaled[half], ((0,), (0,)))
+            both = jnp.concatenate([grad_keys * SCORE_SCALE, grad_values], -1).astype(BF16)
+            r["pairs"][:, lines, :] = both.reshape(devices, block, 2 * size)
+        for half in range(2):
+            lines = pl.ds(seq * rows + half * block, block)
+            for h in range(heads):
+                r["grad_query"][lines, h * size : (h + 1) * size] = (
+                    grad_query[half][h * block : (h + 1) * block] * SCORE_SCALE
+                )
+
+    def pick(value, which):
+        middle = value.shape[1] // 2
+        return jnp.where(which == 0, value[:, :middle], value[:, middle:])
+
+    def projections():
+        need("query_raw", "key_raw", "cosine", "sine", "gains")
+        cosine, sine = r["cosine"][...], r["sine"][...]
+        gain = r["gains"][4:5, :size]
+        total = jnp.zeros((1, size), F32)
+        lows = []
+        for h in range(heads):
+            cols = slice(h * size, (h + 1) * size)
+            back, part = norm_back(
+                turn_back(r["grad_query"][:, cols], cosine, sine), r["query_raw"][:, cols], gain
+            )
+            total += part
+            r["query_low"][:, cols] = back.astype(BF16)
+        back, key_total = norm_back(
+            turn_back(r["kv_sum"][:, :size], cosine, sine),
+            r["key_raw"][...],
+            r["gains"][4:5, size : 2 * size],
+        )
+        r["pair_low"][:, :size] = back.astype(BF16)
+        r["pair_low"][:, size:] = r["kv_sum"][:, size:].astype(BF16)
+        first = 0
+        for value in (
+            r["query_low"][...],
+            r["pair_low"][:, :size],
+            r["pair_low"][:, size:],
+        ):
+            cols = slice(first, first + value.shape[1] // 2)
+            r["col_rows"][:count, cols] = pick(value, mine)
+            r["col_send"][:, cols] = pick(value, 1 - mine)
+            first += value.shape[1] // 2
+        col_swap.start()
+        need("weight_query", "weight_pair", "tokens", "grad_hidden", "gain_part")
+        grad_normed = dot(r["query_low"][...], r["weight_query"][...], ((1,), (1,)))
+        grad_normed += dot(r["pair_low"][...], r["weight_pair"][...], ((1,), (1,)))
+        back, part = norm_back(grad_normed, r["tokens"][...].astype(F32), r["gains"][0:1, :])
+        r["grad_tokens"][...] = back + r["grad_hidden"][...]
+        r["gain_own"][...] = r["gain_part"][...]
+        r["gain_own"][0:1, :] = part
+        r["gain_own"][4:5, :size] = total
+        r["gain_own"][4:5, size : 2 * size] = key_total
+        gain_swap.start()
+
+    def out_part():
+        need("mixed_turned", "att_own")
+        out_swap.wait_recv()
+        _, lines, cols = r["out_part"].shape
+        value = dot(r["mixed_turned"][:, :count], r["att_own"][...], ((1,), (0,)))
+        value += dot(r["mixed_turned"][:, count:], r["att_across"][...], ((1,), (0,)))
+        r["out_part"][...] = value.reshape(devices, lines, cols).astype(BF16)
+
+    def qkv_part():
+        need("normed_turned")
+        col_swap.wait_recv()
+        _, lines, cols = r["qkv_part"].shape
+        width = 256
+        for first in range(0, cols, width):
+            value = dot(
+                r["normed_turned"][...], r["col_rows"][:, first : first + width], ((1,), (0,))
+            )
+            r["qkv_part"][:, :, first : first + width] = value.reshape(
+                devices, lines, width
+            ).astype(BF16)
+
+    def gains_step(step):
+        if step == 0:
+            gain_swap.wait_recv()
+            r["gain_pair"][...] = r["gain_own"][...] + r["gain_across"][...]
+            gain_twin.start()
+        elif step == 1:
+            gain_twin.wait_recv()
+            both = r["gain_pair"][...] + r["gain_twin"][...]
+            r["gain_flow"][0, 0] = both
+            r["gain_flow"][1, 0] = both
+            r["gain_sum"][...] = both
+            for way in range(2):
+                gain_hop(way, 0).start()
+        else:
+            for way in range(2):
+                if step - 2 < gain_hops[way]:
+                    gain_hop(way, step - 2).wait_recv()
+                    if step - 1 < gain_hops[way]:
+                        gain_hop(way, step - 1).start()
+                    r["gain_sum"][...] += r["gain_flow"][way, step - 1]
+
+    def ff_step(step, extra=()):
+        extra = list(extra)
+        if step + 1 < chips:
+            ff.load_all(step + 1)
+        if step + 2 < chips:
+            ff.give_all(step + 2)
+        for p in range(len(ff_pieces)):
+            ff.work(p, step)
+            if p % 2 == 1 and extra:
+                extra.pop(0)()
+        for left in extra:
+            left()
+
+    def kv_step(step):
+        def run():
+            for p in range(len(kv_pieces)):
+                kv.work(p, step)
+
+        return run
+
+    def attn_step(step):
+        def run():
+            gains_step(step)
+            for p in range(len(attn_pieces)):
+                attn.work(p, step)
+
+        return run
+
+    ff.load_all(0)
+    for i in range(len(BROUGHT)):
+        brought(i).start()
+    ring.enter(across=True)
+    ff.give_all(0)
+    ff.give_all(1)
+    need("att_send")
+    out_swap.start()
+    ff_step(0)
+    need("pairs", "query", "grad_mixed", "mixed", "totals", "query_pos", "key_pos")
+    for seq in range(sequences):
+        attention(seq)
+    for step in range(chips):
+        kv.give_all(step)
+    ff_step(1, [kv_step(0), kv_step(1), kv_step(2)])
+    ff_step(2, [kv_step(3), kv_step(4), kv_step(5)])
+    ff_step(3, [kv_step(6), kv_step(7), out_part])
+    projections()
+    ff_step(4)
+    qkv_part()
+    for step in range(chips):
+        attn.give_all(step)
+    ff_step(5, [attn_step(0), attn_step(1), attn_step(2)])
+    ff_step(6, [attn_step(3), attn_step(4), attn_step(5)])
+    ff_step(7, [attn_step(6), attn_step(7)])
+    r["gains_total"][...] = r["gain_sum"][...]
+    for copy in (out_swap, col_swap, gain_swap, gain_twin):
+        copy.wait_send()
+    for way in range(2):
+        for step in range(gain_hops[way]):
+            gain_hop(way, step).wait_send()
+    ff.drain()
+    kv.drain()
+    attn.drain()
+
+
+BROUGHT = (
+    "att_send",
+    "pairs",
+    "query",
+    "grad_mixed",
+    "mixed",
+    "totals",
+    "query_pos",
+    "key_pos",
+    "att_own",
+    "mixed_turned",
+    "query_raw",
+    "key_raw",
+    "cosine",
+    "sine",
+    "gains",
+    "weight_query",
+    "weight_pair",
+    "tokens",
+    "grad_hidden",
+    "gain_part",
+    "normed_turned",
+)
+
+
+def back(given, ff_parts, heads, devices, collective_id):
+    chips = devices // 2
+    count, width = given["tokens"].shape
+    size = given["key_raw"].shape[1]
+    out_cols = given["att_send"].shape[1]
+    out_lines = given["mixed_turned"].shape[0] // devices
+    lines = width // devices
+    cols = (heads * size + 2 * size) // 2
+    slots = lambda n, p: pltpu.VMEM((n,) + tuple(p.shape[1:]), p.dtype)
+    ff_pieces = split_ways(ff_parts)
+    pair_rows = given["pairs"].shape[1]
+    kv_pieces = tuple(
+        (0, 1 - 2 * i, i * pair_rows // 2, pair_rows // 2, 0, 2 * size) for i in range(2)
+    )
+    attn_pieces = (
+        (0, 1, 0, lines, 0, cols // 2),
+        (0, -1, 0, lines, cols // 2, cols // 2),
+        (1, 1, 0, out_lines // 2, 0, out_cols),
+        (1, -1, out_lines // 2, out_lines // 2, 0, out_cols),
+    )
+    dma = lambda *shape: pltpu.SemaphoreType.DMA(shape)
+    names, specs, operands = [], [], []
+    for name, array in zip(("part_down", "part_gate", "part_up"), ff_parts):
+        names.append(name)
+        operands.append(array)
+    for name in BROUGHT:
+        names.append("in_" + name)
+        operands.append(given[name])
+    outs = {
+        "grad_tokens": ((count, width), F32),
+        "grad_down": (ff_parts[0].shape[1:], BF16),
+        "grad_gate": (ff_parts[1].shape[1:], BF16),
+        "grad_up": (ff_parts[2].shape[1:], BF16),
+        "grad_qkv": ((lines, cols), F32),
+        "grad_out": ((out_lines, out_cols), F32),
+        "gains_total": (given["gains"].shape, F32),
+    }
+    scratch = {}
+    for name in BROUGHT:
+        shape = given[name].shape
+        scratch[name] = pltpu.VMEM(shape, given[name].dtype)
+    for i, p in enumerate(ff_parts):
+        scratch[f"ff_own{i}"] = slots(2, p)
+        scratch[f"ff_other{i}"] = slots(chips, p)
+        scratch[f"ff_flow{i}"] = slots(chips, p)
+    for kind, pieces in (("ff", ff_pieces), ("kv", kv_pieces), ("at", attn_pieces)):
+        for name, steps in (("put", chips), ("got", chips), ("send", chips - 1), ("recv", chips - 1)):
+            scratch[f"{kind}_{name}"] = dma(len(pieces), steps)
+    scratch["ff_load"] = dma(len(ff_pieces), chips)
+    scratch["kv_other"] = slots(chips, given["pairs"])
+    scratch["kv_flow"] = slots(chips, given["pairs"])
+    scratch["kv_sum"] = pltpu.VMEM((pair_rows, 2 * size), F32)
+    scratch["att_across"] = pltpu.VMEM((count, out_cols), BF16)
+    scratch["grad_query"] = pltpu.VMEM((count, heads * size), F32)
+    scratch["query_low"] = pltpu.VMEM((count, heads * size), BF16)
+    scratch["pair_low"] = pltpu.VMEM((count, 2 * size), BF16)
+    scratch["col_rows"] = pltpu.VMEM((2 * count, cols), BF16)
+    scratch["col_send"] = pltpu.VMEM((count, cols), BF16)
+    for name, shape in (("qkv", (lines, cols)), ("out", (out_lines, out_cols))):
+        scratch[f"{name}_part"] = pltpu.VMEM((devices,) + shape, BF16)
+        scratch[f"{name}_other"] = pltpu.VMEM((chips,) + shape, BF16)
+        scratch[f"{name}_flow"] = pltpu.VMEM((chips,) + shape, BF16)
+    for name in ("gain_own", "gain_across", "gain_pair", "gain_twin", "gain_sum"):
+        scratch[name] = pltpu.VMEM(given["gains"].shape, F32)
+    scratch["gain_flow"] = pltpu.VMEM((2, chips // 2 + 1) + given["gains"].shape, F32)
+    scratch["bring"] = dma(len(BROUGHT))
+    for name, n in (("cross_send", 3), ("cross_recv", 3), ("twin_send", 1), ("twin_recv", 1)):
+        scratch[name] = dma(n)
+    scratch["gain_send"] = dma(2, chips // 2)
+    scratch["gain_recv"] = dma(2, chips // 2)
+    names += list(outs) + list(scratch)
+    return pl.pallas_call(
+        functools.partial(
+            back_kernel, devices, heads, ff_pieces, kv_pieces, attn_pieces, tuple(names)
+        ),
+        in_specs=[pl.BlockSpec(memory_space=pl.ANY)] * len(operands),
+        out_specs=[pl.BlockSpec(memory_space=pltpu.VMEM)] * len(outs),
+        out_shape=[jax.ShapeDtypeStruct(shape, kind) for shape, kind in outs.values()],
+        scratch_shapes=list(scratch.values()),
+        compiler_params=pltpu.CompilerParams(
+            collective_id=collective_id, has_side_effects=True, vmem_limit_bytes=67043328
+        ),
+        name="back",
+    )(*operands)
+
+
 def body(
     tokens,
     block_order,
@@ -747,75 +1254,128 @@
     ).astype(BF16)
     attended_low = attended_low.reshape(count, width)
     mixed_rows = mixed_low.reshape(count, heads * head_size)
-    part_out = weight_grad(
-        both(mixed_rows, swap(mixed_rows)),
-        both(half_of(attended_low, mine), swap(half_of(attended_low, 1 - mine))),
-    )
-    grad_query, grad_pairs = attend_backward(
-        query_low, pairs, grad_mixed, mixed, totals, query_pos, key_pos, heads
-    )
-    pair_rows = sequences * rows
-    slots = grad_pairs.reshape(devices, pair_rows, 2 * head_size)
-    share = pair_rows // 8
-    pieces = tuple((0, 1 - 2 * (i % 2), i * share, share, 0, 2 * head_size) for i in range(8))
-    own_grads = sum_over_ctx([slots], pieces, devices, 0)[0]
-    own_grads = own_grads.reshape(sequences, rows, 2 * head_size)
-    grad_key_raw, grad_key_gain = jax.vjp(key_path, key_raw, key_gain)[1](own_grads[..., :head_size])
-    value_grad_low = own_grads[..., head_size:].astype(BF16)
-    grad_query_raw, grad_query_gain = query_back(
-        grad_query.reshape(sequences, rows, heads, head_size)
-    )
-    query_grad_low = grad_query_raw.reshape(count, heads * head_size).astype(BF16)
-    key_grad_low = grad_key_raw.astype(BF16).reshape(count, head_size)
-    value_grad_low = value_grad_low.reshape(count, head_size)
-    grad_normed = (
-        dot(query_grad_low, weight_query, ((1,), (1,)))
-        + dot(jnp.concatenate([key_grad_low, value_grad_low], -1), pair_weight, ((1,), (1,)))
-    ).reshape(sequences, rows, width)
-    grad_inputs, grad_attn_pre = jax.vjp(norm_gain, inputs, attn_pre)[1](grad_normed)
-    grad_tokens = grad_inputs + grad_hidden
-
-    def columns(which):
-        return jnp.concatenate(
-            [half_of(v, which) for v in (query_grad_low, key_grad_low, value_grad_low)], -1
-        )
-
     normed_rows = normed_low.reshape(count, width)
-    part_qkv = weight_grad(
-        both(normed_rows, swap(normed_rows)), both(columns(mine), swap(columns(1 - mine)))
-    )
-
-    gain_grads = [
-        grad_attn_pre,
-        grad_query_gain,
-        grad_key_gain,
-        grad_attn_post,
-        grad_ff_pre,
-        grad_ff_post,
-    ]
-    packed = jnp.concatenate([g.reshape(devices, 2, -1) for g in gain_grads], -1)
-    keep = jnp.where(mine == 0, packed[:, 0], packed[:, 1])
-    send = jnp.where(mine == 0, packed[:, 1], packed[:, 0])
-    packed = keep + swap(send)
-    gain_size = packed.shape[-1]
-    packed = jnp.pad(packed, ((0, 0), (0, 1024 - gain_size))).reshape(devices, 8, 128)
-    parts = [
-        p.reshape(devices, p.shape[0] // devices, p.shape[1])
-        for p in (part_down, part_gate, part_up, part_qkv, part_out)
-    ] + [packed]
-    grad_down_w, grad_gate_w, grad_up_w, grad_qkv, grad_out_w, packed = sum_over_ctx(
-        parts, split_ways(parts), devices, 1
-    )
-    packed = packed.reshape(-1)
-    query_cols = query_grad_low.shape[1] // 2
+    given = {
+        "att_send": half_of(attended_low, 1 - mine),
+        "att_own": half_of(attended_low, mine),
+        "pairs": pairs.reshape(devices, count, 2 * head_size),
+        "query": query_low,
+        "grad_mixed": grad_mixed,
+        "mixed": mixed,
+        "totals": totals,
+        "query_pos": query_pos,
+        "key_pos": key_pos,
+        "mixed_turned": both(mixed_rows, swap(mixed_rows)).T,
+        "query_raw": query_raw.reshape(count, heads * head_size),
+        "key_raw": key_raw.reshape(count, head_size),
+        "cosine": jnp.tile(cosine, (sequences, 1)),
+        "sine": jnp.tile(sine, (sequences, 1)),
+        "gains": all_gains,
+        "weight_query": weight_query,
+        "weight_pair": pair_weight,
+        "tokens": tokens.reshape(count, width),
+        "grad_hidden": grad_hidden.reshape(count, width),
+        "gain_part": jnp.stack(
+            [jnp.zeros((width,), F32), grad_attn_post, grad_ff_pre, grad_ff_post]
+            + [jnp.zeros((width,), F32)] * 4
+        ),
+        "normed_turned": both(normed_rows, swap(normed_rows)).T,
+    }
+    if width % (8 * devices) == 0 and mixed_rows.shape[1] % (32 * devices) == 0:
+        ff_parts = [
+            p.reshape(devices, p.shape[0] // devices, p.shape[1])
+            for p in (part_down, part_gate, part_up)
+        ]
+        grad_tokens, grad_down_w, grad_gate_w, grad_up_w, grad_qkv, grad_out_w, gain_sums = back(
+            given, ff_parts, heads, devices, 0
+        )
+        grad_tokens = grad_tokens.reshape(sequences, rows, width)
+        place = me * 2 + mine
+
+        def share(row, first, size):
+            part = size // (2 * devices)
+            return lax.dynamic_slice(gain_sums, (row, first + place * part), (1, part))[0]
+
+        outs = [
+            share(0, 0, width),
+            share(4, 0, head_size),
+            share(4, head_size, head_size),
+            share(1, 0, width),
+            share(2, 0, width),
+            share(3, 0, width),
+        ]
+    else:
+        part_out = weight_grad(
+            both(mixed_rows, swap(mixed_rows)),
+            both(half_of(attended_low, mine), swap(half_of(attended_low, 1 - mine))),
+        )
+        grad_query, grad_pairs = attend_backward(
+            query_low, pairs, grad_mixed, mixed, totals, query_pos, key_pos, heads
+        )
+        pair_rows = sequences * rows
+        slots = grad_pairs.reshape(devices, pair_rows, 2 * head_size)
+        share = pair_rows // 8
+        pieces = tuple((0, 1 - 2 * (i % 2), i * share, share, 0, 2 * head_size) for i in range(8))
+        own_grads = sum_over_ctx([slots], pieces, devices, 0)[0]
+        own_grads = own_grads.reshape(sequences, rows, 2 * head_size)
+        grad_key_raw, grad_key_gain = jax.vjp(key_path, key_raw, key_gain)[1](own_grads[..., :head_size])
+        value_grad_low = own_grads[..., head_size:].astype(BF16)
+        grad_query_raw, grad_query_gain = query_back(
+            grad_query.reshape(sequences, rows, heads, head_size)
+        )
+        query_grad_low = grad_query_raw.reshape(count, heads * head_size).astype(BF16)
+        key_grad_low = grad_key_raw.astype(BF16).reshape(count, head_size)
+        value_grad_low = value_grad_low.reshape(count, head_size)
+        grad_normed = (
+            dot(query_grad_low, weight_query, ((1,), (1,)))
+            + dot(jnp.concatenate([key_grad_low, value_grad_low], -1), pair_weight, ((1,), (1,)))
+        ).reshape(sequences, rows, width)
+        grad_inputs, grad_attn_pre = jax.vjp(norm_gain, inputs, attn_pre)[1](grad_normed)
+        grad_tokens = grad_inputs + grad_hidden
+
+        def columns(which):
+            return jnp.concatenate(
+                [half_of(v, which) for v in (query_grad_low, key_grad_low, value_grad_low)], -1
+            )
+
+        part_qkv = weight_grad(
+            both(normed_rows, swap(normed_rows)), both(columns(mine), swap(columns(1 - mine)))
+        )
+
+        gain_grads = [
+            grad_attn_pre,
+            grad_query_gain,
+            grad_key_gain,
+            grad_attn_post,
+            grad_ff_pre,
+            grad_ff_post,
+        ]
+        packed = jnp.concatenate([g.reshape(devices, 2, -1) for g in gain_grads], -1)
+        keep = jnp.where(mine == 0, packed[:, 0], packed[:, 1])
+        send = jnp.where(mine == 0, packed[:, 1], packed[:, 0])
+        packed = keep + swap(send)
+        gain_size = packed.shape[-1]
+        packed = jnp.pad(packed, ((0, 0), (0, 1024 - gain_size))).reshape(devices, 8, 128)
+        parts = [
+            p.reshape(devices, p.shape[0] // devices, p.shape[1])
+            for p in (part_down, part_gate, part_up, part_qkv, part_out)
+        ] + [packed]
+        grad_down_w, grad_gate_w, grad_up_w, grad_qkv, grad_out_w, packed = sum_over_ctx(
+            parts, split_ways(parts), devices, 1
+        )
+        packed = packed.reshape(-1)
+        outs, first = [], 0
+        for g in gain_grads:
+            size = g.shape[0] // (2 * devices)
+            outs.append(packed[first : first + size])
+            first += size
+    query_cols = grad_qkv.shape[1] - 2 * local_size
     grad_query_w = grad_qkv[:, :query_cols]
     grad_key_w = grad_qkv[:, query_cols : query_cols + local_size]
     grad_value_w = grad_qkv[:, query_cols + local_size :]
-    outs, first = [], 0
-    for g in gain_grads:
-        size = g.shape[0] // (2 * devices)
-        outs.append(packed[first : first + size])
-        first += size
+    grad_down_w, grad_gate_w, grad_up_w = (
+        g.astype(F32) for g in (grad_down_w, grad_gate_w, grad_up_w)
+    )
     return (
         output,
         grad_tokens,

time: 425 us -> 390 us (0.918)
  Pallas kernels: 230 us -> 217 us
  waiting for transfers between devices: 17.5 us -> 7.5 us
  local copies, waits for them, and re-layouts: 33.9 us -> 26.4 us
    pallas_call x3 -> x1, Pallas kernels: 177 us -> 164 us  [back(): pl.pallas_call(functools.partial(back_kernel, devices, heads, ff_pieces,...]
    ppermute x9 -> x6, waiting for transfers between devices: 17.5 us -> 7.5 us  [swap(): return lax.ppermute(value, 'wsh', [(0, 1), (1, 0)])]
    convert_element_type x2 -> x3, other arithmetic: 0.49 us -> 5.14 us  [body(): g.astype(F32)]
    transpose x0 -> x2, other arithmetic: none -> 4.41 us  [the longest x1 2.25 us: body(): both(mixed_rows, swap(mixed_rows))]
    slice x4 -> x1, local copies, waits for them, and re-layouts: 5.06 us -> 0.7 us  [body(): query_gain = all_gains[4, :head_size]]
    ppermute x9 -> x6, starting transfers between devices: 10.8 us -> 6.95 us  [swap(): return lax.ppermute(value, 'wsh', [(0, 1), (1, 0)])]
    unnamed x177 -> x89, local copies, waits for them, and re-layouts: 12.4 us -> 9.05 us
    dot_general x19 -> x15, matrix products: 87.5 us -> 87.2 us  [dot(): lax.dot_general(left, right, (dims, ((), ())), preferred_element_type=F32)]
  transfers between devices with their start and end apart: 9 -> 6, of which waited for: 4 -> 1; matrix products, arithmetic and copies ran while one was open for 31% -> 20% of each run, Pallas kernels for 11% -> 0%
where the time goes in v4:
time: 390 us; the launch traced here: 384 us
  Pallas kernels  217 us (56%)
  matrix products  93.9 us (24%)
  other arithmetic  28.6 us (7%)
  local copies, waits for them, and re-layouts  26.4 us (7%)
  waiting for transfers between devices  7.5 us (2%)
  starting transfers between devices  6.95 us (2%)
    pallas_call x1, Pallas kernels, back(): pl.pallas_call(functools.partial(back_kernel, devices, heads, ff_pieces,...  164 us
    dot_general x15, matrix products, dot(): lax.dot_general(left, right, (dims, ((), ())), preferred_element_type=F32)  87.2 us
    pallas_call x1, Pallas kernels, front(): pl.pallas_call(functools.partial(front_kernel, devices), in_specs=[here]...  47.2 us
    unnamed x89, local copies, waits for them, and re-layouts  9.05 us
  transfers between devices with their start and end apart: 6, of which 1 were waited for; matrix products, arithmetic and copies ran while one was open for 20% of the time, Pallas kernels for 0%

profile of v4, /device:TPU:0, one launch (start us, length us, event | category | flops | bytes accessed | tf_op | source)
XLA Modules:
  0.0 383.9 jit_solution(5816323597827165729)
XLA Ops:
  8.8 2.4 copy.54.out_weight
  12.9 47.2 %front.1 = (bf16[16,2,128,512]{3,2,1,0:T(8,128)(2,1)}, bf16[256,1152]{1,0:T(8,128)(2,1)}, f32[256,256]{1,0:T(8,128)}, f32[8,1152]{1,0:T(8,128)}, bf16[1152,128]{...) custom-call(bf16[2,128,1152]{2,1,0:T(8,128)(2,1)} %tokens_ref.1, ...), custom_call_target="tpu_custom_call" | custom-call | tf_op jit(solution)/shard_map/front/pallas_call | solution.py:583
  61.7 2.4 maximum_select_fusion.refs_18_
  71.5 5.8 %attend_forward.1 = (bf16[2,128,1024]{2,1,0:T(8,128)(2,1)}, f32[2,512,256]{2,1,0:T(8,128)}, f32[2,512,128]{2,1,0:T(8,128)}) custom-call(bf16[2,128,1024]{2,1,0:T(8,128)(2,1)} %convert_element_type.95.q_ref.refs_5_, bf16[16,2,128,512]{3,2,1,0:T(8,128)(2,1)} %get-tuple-element.36.kv_ref, s32[512,1]{1,0:T(8,128)} %copy.57.qpos_ref.refs_9_, ...), custom_call_target="tpu_custom_call" | custom-call | tf_op jit(solution)/shard_map/attend_forward/pallas_call | solution.py:164
  77.3 3.6 multiply_reduce_fusion.6
  82.6 2.0 copy.64
  84.7 1.7 collective-permute-start.4
  87.8 6.0 %fusion.55 = f32[256,3456]{1,0:T(8,128)S(1)} fusion(bf16[256,1152]{1,0:T(8,128)(2,1)} %bitcast.7, bf16[1152,3456]{1,0:T(8,128)(2,1)} %param.28), kind=kOutput, calls=%fused_computation.137 | convolution fusion | flops 2038431744 | bytes 12091392 | tf_op jit(solution)/shard_map/dot_general | solution.py:61
  93.8 1.8 copy-done.20
  95.5 8.5 %multiply_convert_fusion.3 = (bf16[256,3456]{1,0:T(8,128)(2,1)}, f32[256,3456]{1,0:T(8,128)}) fusion(f32[256,3456]{1,0:T(8,128)S(1)} %fusion.55, bf16[256,1152]{1,0:T(8,128)(2,1)} %bitcast.7, bf16[1152,3456]{1,0:T(8,128)(2,1)} %param.29), kind=kOutput, calls=%fused_computation.33 | convolution fusion | flops 2047279104 | bytes 17399808 | tf_op jit(solution)/shard_map/dot_general | solution.py:61
  105.6 6.1 %fusion.56 = f32[256,3456]{1,0:T(8,128)S(1)} fusion(bf16[256,1152]{1,0:T(8,128)(2,1)} %collective-permute-done, bf16[1152,3456]{1,0:T(8,128)(2,1)} %param.28), kind=kOutput, calls=%fused_computation.138 | convolution fusion | flops 2038431744 | bytes 12091392 | tf_op jit(solution)/shard_map/dot_general | solution.py:61
  111.8 6.7 %multiply_convert_fusion.2 = (bf16[256,3456]{1,0:T(8,128)(2,1)S(1)}, f32[256,3456]{1,0:T(8,128)}) fusion(f32[256,3456]{1,0:T(8,128)S(1)} %fusion.56, bf16[256,1152]{1,0:T(8,128)(2,1)} %collective-permute-done, bf16[1152,3456]{1,0:T(8,128)(2,1)S(1)} %bitcast.112), kind=kOutput, calls=%fused_computation.32 | convolution fusion | flops 2047279104 | bytes 17399808 | tf_op jit(solution)/shard_map/dot_general | solution.py:61
  118.5 2.6 convolution_convert_fusion.3
  121.1 1.8 collective-permute-start.1
  124.1 2.2 maximum_bitcast_fusion.1.refs_12_
  126.3 2.2 maximum_bitcast_fusion.refs_23_
  128.5 7.5 %collective-permute-done.1 = bf16[256,1152]{1,0:T(8,128)(2,1)S(1)} collective-permute-done((bf16[256,1152]{1,0:T(8,128)(2,1)S(1)}, bf16[256,1152]{1,0:T(8,128)(2,1)S(1)}, u32[]{:S(2)}, u32[]{:S(2)}) %collective-permute-start.1) | collective-permute-done | bytes 589856 | tf_op jit(solution)/shard_map/ppermute | solution.py:44
  136.0 2.7 multiply_reduce_fusion.4
  140.5 1.7 collective-permute-start.2
  142.2 7.6 %multiply_convert_fusion.1 = (bf16[256,3456]{1,0:T(8,128)(2,1)}, bf16[256,3456]{1,0:T(8,128)(2,1)}) fusion(f32[256,3456]{1,0:T(8,128)S(1)} %copy-done.21, f32[256,3456]{1,0:T(8,128)} %get-tuple-element.89, bf16[256,1152]{1,0:T(8,128)(2,1)S(1)} %bitcast.100, bf16[1152,3456]{1,0:T(8,128)(2,1)S(1)} %bitcast.108), kind=kOutput, calls=%fused_computation.31 | convolution fusion | flops 2059665408 | bytes 19169280 | tf_op jit(solution)/shard_map/dot_general | solution.py:61
  149.9 5.2 %fusion.57 = f32[256,1152]{1,0:T(8,128)} fusion(bf16[256,3456]{1,0:T(8,128)(2,1)} %get-tuple-element.65, bf16[1152,3456]{1,0:T(8,128)(2,1)S(1)} %bitcast.110), kind=kOutput, calls=%fused_computation.139 | convolution fusion | flops 2038431744 | bytes 10911744 | tf_op jit(solution)/shard_map/dot_general | solution.py:61
  155.1 6.1 %multiply_convert_fusion = (bf16[256,3456]{1,0:T(8,128)(2,1)}, bf16[256,3456]{1,0:T(8,128)(2,1)}) fusion(f32[256,3456]{1,0:T(8,128)S(1)} %copy-done.23, f32[256,3456]{1,0:T(8,128)S(1)} %copy-done.24, bf16[256,1152]{1,0:T(8,128)(2,1)S(1)} %collective-permute-done.2, bf16[1152,3456]{1,0:T(8,128)(2,1)S(1)} %bitcast.108), kind=kOutput, calls=%fused_computation.30 | convolution fusion | flops 2059665408 | bytes 19169280 | tf_op jit(solution)/shard_map/dot_general | solution.py:61
  161.2 4.2 %fusion.58 = f32[256,1152]{1,0:T(8,128)S(1)} fusion(bf16[256,3456]{1,0:T(8,128)(2,1)} %get-tuple-element.67, bf16[1152,3456]{1,0:T(8,128)(2,1)S(1)} %bitcast.110), kind=kOutput, calls=%fused_computation.140 | convolution fusion | flops 2038431744 | bytes 10911744 | tf_op jit(solution)/shard_map/dot_general | solution.py:61
  165.4 6.0 %fusion.23 = bf16[256,1152]{1,0:T(8,128)(2,1)S(1)} fusion(f32[256,1152]{1,0:T(8,128)S(1)} %fusion.58, bf16[256,3456]{1,0:T(8,128)(2,1)S(1)} %copy-done.30, bf16[1152,3456]{1,0:T(8,128)(2,1)} %param.29), kind=kOutput, calls=%fused_computation.38 | convolution fusion | flops 2039021568 | bytes 11501568 | tf_op jit(solution)/shard_map/dot_general | solution.py:61
  172.6 7.9 %convolution_convert_fusion.1 = bf16[1152,3456]{1,0:T(8,128)(2,1)} fusion(bf16[256,3456]{1,0:T(8,128)(2,1)S(1)} %copy-done.33, bf16[256,3456]{1,0:T(8,128)(2,1)S(1)} %copy-done.32, bf16[256,1152]{1,0:T(8,128)(2,1)} %collective-permute-done, bf16[256,1152]{1,0:T(8,128)(2,1)} %bitcast.7), kind=kOutput, calls=%fused_computation.1 | convolution fusion | flops 4090281984 | bytes 12681216 | tf_op jit(solution)/shard_map/dot_general | solution.py:61
  180.6 6.7 %convolution_convert_fusion.2 = bf16[1152,3456]{1,0:T(8,128)(2,1)} fusion(bf16[256,3456]{1,0:T(8,128)(2,1)S(1)} %copy-done.28, bf16[256,3456]{1,0:T(8,128)(2,1)S(1)} %copy-done.26, bf16[256,1152]{1,0:T(8,128)(2,1)S(1)} %collective-permute-done.2, bf16[256,1152]{1,0:T(8,128)(2,1)S(1)} %bitcast.101), kind=kOutput, calls=%fused_computation.2 | convolution fusion | flops 4090281984 | bytes 12681216 | tf_op jit(solution)/shard_map/dot_general | solution.py:61
  187.3 8.3 %convolution_convert_fusion = bf16[1152,3456]{1,0:T(8,128)(2,1)} fusion(bf16[256,3456]{1,0:T(8,128)(2,1)S(1)} %copy-done.31, bf16[256,3456]{1,0:T(8,128)(2,1)S(1)} %copy-done.29, bf16[256,1152]{1,0:T(8,128)(2,1)} %collective-permute-done, bf16[256,1152]{1,0:T(8,128)(2,1)} %bitcast.7), kind=kOutput, calls=%fused_computation | convolution fusion | flops 4090281984 | bytes 12681216 | tf_op jit(solution)/shard_map/dot_general | solution.py:61
  195.6 2.6 convert_add_fusion.1
  201.0 2.3 fusion.33.refs_6_
  206.3 164.4 %back.1 = (f32[256,1152]{1,0:T(8,128)}, bf16[72,3456]{1,0:T(8,128)(2,1)}, bf16[72,3456]{1,0:T(8,128)(2,1)}, bf16[72,3456]{1,0:T(8,128)(2,1)}, f32[72,768]{1,0:T(...) custom-call(bf16[16,72,3456]{2,1,0:T(8,128)(2,1)} %bitcast.93, bf16[16,72,3456]{2,1,0:T(8,128)(2,1)} %bitcast.92, ...), custom_call_target="tpu_custom_call" | custom-call | tf_op jit(solution)/shard_map/back/pallas_call | solution.py:1097
  374.0 2.0 convert_element_type.115
  376.0 2.1 convert_element_type.116
  (172 shorter events, 40.5 us)
Async XLA Ops:
  11.2 50.5 %copy-start.7 = (bf16[1152,512]{1,0:T(8,128)(2,1)S(1)}, bf16[1152,512]{1,0:T(8,128)(2,1)}, u32[]{:S(2)}) copy-start(bf16[1152,512]{1,0:T(8,128)(2,1)} %query_weight.1) | copy-start | bytes 3538948
  71.5 5.9 %copy-start.5 = (bf16[1024,576]{1,0:T(8,128)(2,1)S(1)}, bf16[1024,576]{1,0:T(8,128)(2,1)}, u32[]{:S(2)}) copy-start(bf16[1024,576]{1,0:T(8,128)(2,1)} %copy.54.out_weight) | copy-start | bytes 3538948
  82.3 23.3 %collective-permute-start = (bf16[256,1152]{1,0:T(8,128)(2,1)}, bf16[256,1152]{1,0:T(8,128)(2,1)}, u32[]{:S(2)}, u32[]{:S(2)}) collective-permute-start(bf16[256,1152]{1,0:T(8,128)(2,1)} %bitcast.7), channel_id=1, source_target_pairs={{0,1},{1,0},{2,3},{3,2},{4,5},{5,4},{6,7},{7,6},{8,9},{9,8},{10,11... | collective-permute-start | bytes 1769480 | tf_op jit(solution)/shard_map/ppermute | solution.py:44
  84.7 39.4 %collective-permute-start.4 = (bf16[256,1024]{0,1:T(8,128)(2,1)}, bf16[256,1024]{0,1:T(8,128)(2,1)}, u32[]{:S(2)}, u32[]{:S(2)}) collective-permute-start(bf16[256,1024]{0,1:T(8,128)(2,1)} %copy.64), channel_id=1, source_target_pairs={{0,1},{1,0},{2,3},{3,2},{4,5},{5,4},{6,7},{7,6},{8,9},{9,8},{10,11... | collective-permute-start | bytes 1572872 | tf_op jit(solution)/shard_map/ppermute | solution.py:44
  87.5 38.9 %collective-permute-start.5 = (bf16[256,1152]{0,1:T(8,128)(2,1)}, bf16[256,1152]{0,1:T(8,128)(2,1)}, u32[]{:S(2)}, u32[]{:S(2)}) collective-permute-start(bf16[256,1152]{0,1:T(8,128)(2,1)} %copy.62), channel_id=1, source_target_pairs={{0,1},{1,0},{2,3},{3,2},{4,5},{5,4},{6,7},{7,6},{8,9},{9,8},{10,11... | collective-permute-start | bytes 1769480 | tf_op jit(solution)/shard_map/ppermute | solution.py:44
  95.5 8.5 %copy-start.11 = (bf16[1152,128]{1,0:T(8,128)(2,1)S(1)}, bf16[1152,128]{1,0:T(8,128)(2,1)}, u32[]{:S(2)}) copy-start(bf16[1152,128]{1,0:T(8,128)(2,1)} %key_weight.1) | copy-start | bytes 884740
  95.5 8.5 %copy-start.12 = (bf16[1152,128]{1,0:T(8,128)(2,1)S(1)}, bf16[1152,128]{1,0:T(8,128)(2,1)}, u32[]{:S(2)}) copy-start(bf16[1152,128]{1,0:T(8,128)(2,1)} %value_weight.1) | copy-start | bytes 884740
  95.5 8.5 %copy-start.17 = (bf16[1152,128]{1,0:T(8,128)(2,1)S(1)}, bf16[1152,128]{1,0:T(8,128)(2,1)}, u32[]{:S(2)}) copy-start(bf16[1152,128]{1,0:T(8,128)(2,1)} %get-tuple-element.42) | copy-start | bytes 884740
  104.0 7.7 %slice-start.4 = ((s8[7962624]{0:T(1024)(128)(4,1)}), s8[4194304]{0:T(1024)(128)(4,1)S(1)}, s32[]{:S(2)}) async-start(s8[7962624]{0:T(1024)(128)(4,1)} %bitcast.111), calls=%async_computation.4 | async-start | bytes 8388608
  105.6 6.2 %slice-start.5 = ((s8[7962624]{0:T(1024)(128)(4,1)}), s8[3768320]{0:T(1024)(128)(4,1)S(1)}, s32[]{:S(2)}) async-start(s8[7962624]{0:T(1024)(128)(4,1)} %bitcast.111), calls=%async_computation.5 | async-start | bytes 7536640
  105.6 12.9 %slice-start = ((s8[7962624]{0:T(1024)(128)(4,1)}), s8[4194304]{0:T(1024)(128)(4,1)S(1)}, s32[]{:S(2)}) async-start(s8[7962624]{0:T(1024)(128)(4,1)} %bitcast.107), calls=%async_computation | async-start | bytes 8388608
  111.8 6.7 %copy-start.22 = (f32[256,3456]{1,0:T(8,128)}, f32[256,3456]{1,0:T(8,128)S(1)}, u32[]{:S(2)}) copy-start(f32[256,3456]{1,0:T(8,128)S(1)} %fusion.56) | copy-start | bytes 10616836
  111.8 6.7 %slice-start.1 = ((s8[7962624]{0:T(1024)(128)(4,1)}), s8[3768320]{0:T(1024)(128)(4,1)S(1)}, s32[]{:S(2)}) async-start(s8[7962624]{0:T(1024)(128)(4,1)} %bitcast.107), calls=%async_computation.1 | async-start | bytes 7536640
  121.1 14.8 %collective-permute-start.1 = (bf16[256,1152]{1,0:T(8,128)(2,1)S(1)}, bf16[256,1152]{1,0:T(8,128)(2,1)S(1)}, u32[]{:S(2)}, u32[]{:S(2)}) collective-permute-start(bf16[256,1152]{1,0:T(8,128)(2,1)S(1)} %convolution_convert_fusion.3), channel_id=1, source_target_pairs={{0,1},{1,0},{2,3},{3,2},{4,5},{5,4},{6,7},{7,6},{8,9},{9,8},{10,11... | collective-permute-start | bytes 1769480 | tf_op jit(solution)/shard_map/ppermute | solution.py:44
  124.1 11.9 %copy-start.25 = (bf16[256,3456]{1,0:T(8,128)(2,1)S(1)}, bf16[256,3456]{1,0:T(8,128)(2,1)}, u32[]{:S(2)}) copy-start(bf16[256,3456]{1,0:T(8,128)(2,1)} %get-tuple-element.88) | copy-start | bytes 5308420
  139.2 10.7 %slice-start.2 = ((s8[7962624]{0:T(1024)(128)(4,1)}), s8[4194304]{0:T(1024)(128)(4,1)S(1)}, s32[]{:S(2)}) async-start(s8[7962624]{0:T(1024)(128)(4,1)} %bitcast.109), calls=%async_computation.2 | async-start | bytes 8388608
  140.5 14.6 %collective-permute-start.2 = (bf16[256,1152]{1,0:T(8,128)(2,1)S(1)}, bf16[256,1152]{1,0:T(8,128)(2,1)S(1)}, u32[]{:S(2)}, u32[]{:S(2)}) collective-permute-start(bf16[256,1152]{1,0:T(8,128)(2,1)S(1)} %bitcast.99), channel_id=1, source_target_pairs={{0,1},{1,0},{2,3},{3,2},{4,5},{5,4},{6,7},{7,6},{8,9},{9,8},{10,11... | collective-permute-start | bytes 1769480 | tf_op jit(solution)/shard_map/ppermute | solution.py:44
  142.2 7.6 %slice-start.3 = ((s8[7962624]{0:T(1024)(128)(4,1)}), s8[3768320]{0:T(1024)(128)(4,1)S(1)}, s32[]{:S(2)}) async-start(s8[7962624]{0:T(1024)(128)(4,1)} %bitcast.109), calls=%async_computation.3 | async-start | bytes 7536640
  149.9 5.2 %copy-start.23 = (f32[256,3456]{1,0:T(8,128)S(1)}, f32[256,3456]{1,0:T(8,128)}, u32[]{:S(2)}) copy-start(f32[256,3456]{1,0:T(8,128)} %copy-done.22) | copy-start | bytes 10616836
  165.4 7.2 %copy-start.32 = (bf16[256,3456]{1,0:T(8,128)(2,1)S(1)}, bf16[256,3456]{1,0:T(8,128)(2,1)}, u32[]{:S(2)}) copy-start(bf16[256,3456]{1,0:T(8,128)(2,1)} %get-tuple-element.65) | copy-start | bytes 5308420
  165.4 7.2 %copy-start.33 = (bf16[256,3456]{1,0:T(8,128)(2,1)S(1)}, bf16[256,3456]{1,0:T(8,128)(2,1)}, u32[]{:S(2)}) copy-start(bf16[256,3456]{1,0:T(8,128)(2,1)} %get-tuple-element.67) | copy-start | bytes 5308420
  171.5 9.1 %copy-start.26 = (bf16[256,3456]{1,0:T(8,128)(2,1)S(1)}, bf16[256,3456]{1,0:T(8,128)(2,1)}, u32[]{:S(2)}) copy-start(bf16[256,3456]{1,0:T(8,128)(2,1)} %get-tuple-element.88) | copy-start | bytes 5308420
  171.5 9.1 %copy-start.28 = (bf16[256,3456]{1,0:T(8,128)(2,1)S(1)}, bf16[256,3456]{1,0:T(8,128)(2,1)}, u32[]{:S(2)}) copy-start(bf16[256,3456]{1,0:T(8,128)(2,1)} %copy-done.27) | copy-start | bytes 5308420
  171.5 24.1 %collective-permute-start.3 = (bf16[256,1152]{1,0:T(8,128)(2,1)S(1)}, bf16[256,1152]{1,0:T(8,128)(2,1)S(1)}, u32[]{:S(2)}, u32[]{:S(2)}) collective-permute-start(bf16[256,1152]{1,0:T(8,128)(2,1)S(1)} %fusion.23), channel_id=1, source_target_pairs={{0,1},{1,0},{2,3},{3,2},{4,5},{5,4},{6,7},{7,6},{8,9},{9,8},{10,11... | collective-permute-start | bytes 1769480 | tf_op jit(solution)/shard_map/ppermute | solution.py:44
  180.5 6.7 %copy-start.29 = (bf16[256,3456]{1,0:T(8,128)(2,1)S(1)}, bf16[256,3456]{1,0:T(8,128)(2,1)}, u32[]{:S(2)}) copy-start(bf16[256,3456]{1,0:T(8,128)(2,1)} %get-tuple-element.64) | copy-start | bytes 5308420
  180.5 6.7 %copy-start.31 = (bf16[256,3456]{1,0:T(8,128)(2,1)S(1)}, bf16[256,3456]{1,0:T(8,128)(2,1)}, u32[]{:S(2)}) copy-start(bf16[256,3456]{1,0:T(8,128)(2,1)} %get-tuple-element.66) | copy-start | bytes 5308420
  180.6 15.0 %slice-start.6 = ((s8[7962624]{0:T(1024)(128)(4,1)}), s8[4194304]{0:T(1024)(128)(4,1)S(1)}, s32[]{:S(2)}) async-start(s8[7962624]{0:T(1024)(128)(4,1)} %bitcast.113), calls=%async_computation.6 | async-start | bytes 8388608
  187.3 8.3 %slice-start.7 = ((s8[7962624]{0:T(1024)(128)(4,1)}), s8[3768320]{0:T(1024)(128)(4,1)S(1)}, s32[]{:S(2)}) async-start(s8[7962624]{0:T(1024)(128)(4,1)} %bitcast.113), calls=%async_computation.7 | async-start | bytes 7536640
  187.3 8.3 %copy-start.34 = (f32[256,1152]{1,0:T(8,128)S(1)}, f32[256,1152]{1,0:T(8,128)}, u32[]{:S(2)}) copy-start(f32[256,1152]{1,0:T(8,128)} %fusion.57) | copy-start | bytes 3538948
  370.8 7.3 %copy-start.16 = (bf16[72,3456]{1,0:T(8,128)(2,1)S(1)}, bf16[72,3456]{1,0:T(8,128)(2,1)}, u32[]{:S(2)}) copy-start(bf16[72,3456]{1,0:T(8,128)(2,1)} %get-tuple-element.50) | copy-start | bytes 1492996
  372.4 9.4 %copy-start.13 = (f32[256,1152]{1,0:T(8,128)S(1)}, f32[256,1152]{1,0:T(8,128)}, u32[]{:S(2)}) copy-start(f32[256,1152]{1,0:T(8,128)} %get-tuple-element.44) | copy-start | bytes 3538948
  376.0 6.8 %copy-start.18 = (f32[64,576]{1,0:T(8,128)S(1)}, f32[64,576]{1,0:T(8,128)}, u32[]{:S(2)}) copy-start(f32[64,576]{1,0:T(8,128)} %get-tuple-element.122) | copy-start | bytes 442372
  (17 other events, 44.6 us)
